TPU v7x, 128 devices: a whole 4x4x4 slice. The times are simulated.
128 devices in a mesh: gx: 8 (over z, core), gy: 16 (over x, y).
Axes of the slice: x: 4, y: 4, z: 4, core: 2. Of those that a mesh axis runs over, the one named last changes fastest.
Arguments:
- atm_members: float32 [8, 16, 80, 12, 128], P('gx', 'gy'), may hold values from -6 to 6
- ocean_members: bfloat16 [8, 16, 80, 1024], P('gx', 'gy'), may hold values from -6 to 6
- remap_weights: bfloat16 [8, 16, 4, 1024, 128], P('gx', 'gy'), may hold values from -0.09375 to 0.09375
- pair_src: int32 [8, 16, 4], P('gx', 'gy'), may hold values from 0 to 127, as said below
- obs_cell: int32 [8, 16, 64], P('gx', 'gy'), may hold values from 0 to 127
- obs_value: float32 [8, 16, 64], P('gx', 'gy'), may hold values from -8 to 8
- obs_error: float32 [8, 16, 64], P('gx', 'gy'), may hold values from 2 to 16
- obs_live: int32 [8, 16, 64], P('gx', 'gy'), may hold values from 0 to 1, as said below
- obs_order: int32 [8, 16, 64], P('gx', 'gy'), may hold values from 0 to 63, each once within a row
Outputs:
- post_mean: float32 [8, 16, 13, 128], P('gx', 'gy')
- post_anom: float32 [8, 16, 80, 13, 128], P('gx', 'gy')
Inputs may be any that keep to these rules, and one draw needn't show every extreme that they name: `pair_src`: for atmosphere tile (i, j) the 4 numbers are distinct, each a * 16 + b with |a - i| <= 1 and |b - j| <= 1. `obs_live`: the live slots of a tile are its first ones, between 8 and 64 of them; some tile has all slots live. `obs_order`: each tile's last dimension is a permutation of its slots.
All inputs are finite; a program needn't handle non-finite values.
Results may differ from a plain program's by a relative error of at most 0.0003.
Values may be sent and summed in bfloat16 or wider, within the bound.
No kernel may reach another device: no remote copies, remote signals or barrier semaphores. Data moves between devices by JAX's collectives and lax.ppermute only.
A program may use at most 64 MiB of HBM per device.

v0:
```python
import jax
import jax.numpy as jnp
from jax import lax
from jax.sharding import PartitionSpec as P

MEM = 80
AX = 8
AY = 16
OCN_DEV = 1024
OB = 32
NB = 2
K = 4
FIELDS = 12
CELLS = 128
RAD = 2


exact_mode = lax.Precision.HIGHEST


def extended(block, sides, width):
    for axis, dim in sides:
        count = lax.axis_size(axis)
        forward = [(i, i + 1) for i in range(count - 1)]
        backward = [(target, source) for source, target in forward]
        low = lax.ppermute(
            lax.slice_in_dim(block, block.shape[dim] - width, None, axis=dim), axis, forward
        )
        high = lax.ppermute(lax.slice_in_dim(block, 0, width, axis=dim), axis, backward)
        block = jnp.concatenate([low, block, high], axis=dim)
    return block


def update_group(packets, anomaly, base_x, base_y):
    members = anomaly.shape[0]
    components = anomaly.shape[1]
    cell_count = anomaly.shape[2]
    observed = jnp.transpose(packets[:, :members, :], (1, 0, 2)).reshape(members, -1)
    innovation = packets[:, members, :].reshape(-1)
    errors = packets[:, members + 1, :].reshape(-1)
    obs_x = packets[:, members + 2, :].reshape(-1)
    obs_y = packets[:, members + 3, :].reshape(-1)
    live = packets[:, members + 4, :].reshape(-1)
    variance = jnp.sum(observed * observed, axis=0) / (members - 1)
    denominator = variance + errors + (1.0 - live)
    weighting = live / denominator
    damping = 1.0 / (1.0 + jnp.sqrt(errors / denominator))
    cell_index = jnp.arange(cell_count, dtype=jnp.int32)
    cell_x = (base_x + cell_index // AY).astype(jnp.float32)
    cell_y = (base_y + cell_index % AY).astype(jnp.float32)
    distance = (obs_x[:, None] - cell_x[None, :]) ** 2 + (obs_y[:, None] - cell_y[None, :]) ** 2
    taper = jnp.maximum(1.0 - distance / float(RAD * RAD), 0.0) ** 2
    flat_anomaly = anomaly.reshape(members, components * cell_count)
    covariance = jnp.dot(
        observed.T, flat_anomaly, precision=exact_mode, preferred_element_type=jnp.float32
    ) / (members - 1)
    gain = covariance.reshape(-1, components, cell_count) * (taper * weighting[:, None])[:, None, :]
    gain = gain.reshape(-1, components * cell_count)
    mean_step = jnp.dot(
        innovation[None, :], gain, precision=exact_mode, preferred_element_type=jnp.float32
    )
    anomaly_step = jnp.dot(
        observed * damping[None, :], gain, precision=exact_mode, preferred_element_type=jnp.float32
    )
    return (
        mean_step.reshape(components, cell_count),
        anomaly_step.reshape(members, components, cell_count),
    )


def local(
    atm_members,
    ocean_members,
    remap_weights,
    pair_src,
    obs_cell,
    obs_value,
    obs_error,
    obs_live,
    obs_order,
):
    sources = pair_src[0, 0]
    weights = remap_weights[0, 0].reshape(K * OCN_DEV, CELLS)
    row_count = lax.axis_size("gy")
    position = (sources // row_count - lax.axis_index("gx") + 1) * 3 + (
        sources % row_count - lax.axis_index("gy") + 1
    )
    column = extended(ocean_members, (("gx", 0),), 1)
    nearby_rows = extended(column, (("gy", 1),), 1)
    flattened = nearby_rows.reshape(9, MEM * OCN_DEV)
    selector = (position[:, None] == jnp.arange(9, dtype=jnp.int32)[None, :]).astype(jnp.bfloat16)
    chosen = jnp.dot(selector, flattened, preferred_element_type=jnp.float32)
    chosen = chosen.astype(jnp.bfloat16)
    stacked = jnp.transpose(chosen.reshape(K, MEM, OCN_DEV), (1, 0, 2)).reshape(MEM, K * OCN_DEV)
    surface = jnp.dot(stacked, weights, preferred_element_type=jnp.float32)
    state = jnp.concatenate([atm_members[0, 0], surface[:, None, :]], axis=1)
    ens_mean = jnp.sum(state, axis=0) / MEM
    anomaly = state - ens_mean[None]
    base_x = lax.axis_index("gx") * AX
    base_y = lax.axis_index("gy") * AY
    for batch_index in range(NB):
        obs_slots = obs_order[0, 0, batch_index * OB : (batch_index + 1) * OB]
        obs_cells = obs_cell[0, 0][obs_slots]
        observed = anomaly[:, FIELDS, :][:, obs_cells]
        predicted = ens_mean[FIELDS][obs_cells]
        innovation = obs_value[0, 0][obs_slots] - predicted
        errors = obs_error[0, 0][obs_slots]
        pos_x = (base_x + obs_cells // AY).astype(jnp.float32)
        pos_y = (base_y + obs_cells % AY).astype(jnp.float32)
        live = obs_live[0, 0][obs_slots].astype(jnp.float32)
        extras = jnp.stack([innovation, errors, pos_x, pos_y, live], axis=0)
        packet = jnp.concatenate([observed, extras], axis=0)[None, None]
        nearby = extended(packet, (("gx", 0), ("gy", 1)), 1)
        mean_total = jnp.zeros_like(ens_mean)
        anomaly_total = jnp.zeros_like(anomaly)
        for row_index in range(3):
            mean_step, anomaly_step = update_group(nearby[row_index], anomaly, base_x, base_y)
            mean_total = mean_total + mean_step
            anomaly_total = anomaly_total + anomaly_step
        ens_mean = ens_mean + mean_total
        anomaly = anomaly - anomaly_total
    return (ens_mean[None, None], anomaly[None, None])


def solution(mesh):
    in_specs = (
        P("gx", "gy", None, None, None),
        P("gx", "gy", None, None),
        P("gx", "gy", None, None, None),
        P("gx", "gy", None),
        P("gx", "gy", None),
        P("gx", "gy", None),
        P("gx", "gy", None),
        P("gx", "gy", None),
        P("gx", "gy", None),
    )
    out_specs = (P("gx", "gy", None, None), P("gx", "gy", None, None, None))
    return jax.shard_map(local, mesh=mesh, in_specs=in_specs, out_specs=out_specs, check_vma=False)
```

profile of v0, /device:TPU:7, one launch (start us, length us, event | category | flops | bytes accessed | tf_op | source)
XLA Modules:
  0.0 102.3 jit_solution(3507445476075853033)
XLA Ops:
  0.7 4.2 %collective-permute-start = (bf16[1,1,80,1024]{3,2,1,0:T(8,128)(2,1)}, bf16[1,1,80,1024]{3,2,1,0:T(8,128)(2,1)S(1)}, u32[]{:S(2)}, u32[]{:S(2)}) collective-permute-start(bf16[1,1,80,1024]{3,2,1,0:T(8,128)(2,1)} %param.10), channel_id=1, source_target_pairs={{0,16},{16,32},{32,48},{48,64},{64,80},{80,96},{96,112},{1,17},{17... | collective-permute-start | bytes 491528 | tf_op jit(solution)/shard_map/ppermute | solution.py:26
  4.9 1.9 %collective-permute-start.1 = (bf16[1,1,80,1024]{3,2,1,0:T(8,128)(2,1)}, bf16[1,1,80,1024]{3,2,1,0:T(8,128)(2,1)S(1)}, u32[]{:S(2)}, u32[]{:S(2)}) collective-permute-start(bf16[1,1,80,1024]{3,2,1,0:T(8,128)(2,1)} %param.10), channel_id=1, source_target_pairs={{16,0},{32,16},{48,32},{64,48},{80,64},{96,80},{112,96},{17,1},{33... | collective-permute-start | bytes 491528 | tf_op jit(solution)/shard_map/ppermute | solution.py:29
  6.9 0.8 fusion.91
  7.7 1.4 %gather_fusion = s32[32]{0:T(128)S(1)} fusion(s32[64]{0:T(128)} %bitcast.290, s32[1024]{0:T(1024)S(1)} %get-tuple-element.69), kind=kCustom, calls=%fused_computation | custom fusion | bytes 384 | tf_op jit(solution)/shard_map/gather | solution.py:103
  9.0 1.4 %gather_fusion.5 = s32[32]{0:T(128)S(1)} fusion(s32[64]{0:T(128)} %bitcast.292, s32[1024]{0:T(1024)S(1)} %get-tuple-element.69), kind=kCustom, calls=%fused_computation.5 | custom fusion | bytes 384 | tf_op jit(solution)/shard_map/gather | solution.py:110
  10.4 1.4 %gather_fusion.6 = s32[32]{0:T(128)S(1)} fusion(s32[64]{0:T(128)} %bitcast.291, s32[1024]{0:T(1024)S(1)} %get-tuple-element.68), kind=kCustom, calls=%fused_computation.6 | custom fusion | bytes 384 | tf_op jit(solution)/shard_map/gather | solution.py:103
  11.8 0.7 gather_fusion.11
  12.6 3.2 %collective-permute-start.2 = (bf16[3,1,80,1024]{3,2,1,0:T(8,128)(2,1)S(1)}, bf16[3,1,80,1024]{3,2,1,0:T(8,128)(2,1)S(1)}, u32[]{:S(2)}, u32[]{:S(2)}) collective-permute-start(bf16[3,1,80,1024]{3,2,1,0:T(8,128)(2,1)S(1)} %constant_dynamic-update-slice_fusion), channel_id=1, source_target_pairs={{0,1},{1,2},{2,3},{3,4},{4,5},{5,6},{6,7},{7,8},{8,9},{9,10},{10,1... | collective-permute-start | bytes 1474568 | tf_op jit(solution)/shard_map/ppermute | solution.py:26
  15.9 4.2 %collective-permute-start.3 = (bf16[3,1,80,1024]{3,2,1,0:T(8,128)(2,1)S(1)}, bf16[3,1,80,1024]{3,2,1,0:T(8,128)(2,1)S(1)}, u32[]{:S(2)}, u32[]{:S(2)}) collective-permute-start(bf16[3,1,80,1024]{3,2,1,0:T(8,128)(2,1)S(1)} %constant_dynamic-update-slice_fusion), channel_id=1, source_target_pairs={{1,0},{2,1},{3,2},{4,3},{5,4},{6,5},{7,6},{8,7},{9,8},{10,9},{11,1... | collective-permute-start | bytes 1474568 | tf_op jit(solution)/shard_map/ppermute | solution.py:29
  20.1 0.7 gather_fusion.2
  21.0 0.7 gather_fusion.4
  21.9 0.6 fusion.74
  22.5 5.2 %collective-permute-done.2 = bf16[3,1,80,1024]{3,2,1,0:T(8,128)(2,1)S(1)} collective-permute-done((bf16[3,1,80,1024]{3,2,1,0:T(8,128)(2,1)S(1)}, bf16[3,1,80,1024]{3,2,1,0:T(8,128)(2,1)S(1)}, u32[]{:S(2)}, u32[]{:S(2)}) %collective-permute-start.2) | collective-permute-done | bytes 491552 | tf_op jit(solution)/shard_map/ppermute | solution.py:26
  27.7 1.8 %collective-permute-done.3 = bf16[3,1,80,1024]{3,2,1,0:T(8,128)(2,1)S(1)} collective-permute-done((bf16[3,1,80,1024]{3,2,1,0:T(8,128)(2,1)S(1)}, bf16[3,1,80,1024]{3,2,1,0:T(8,128)(2,1)S(1)}, u32[]{:S(2)}, u32[]{:S(2)}) %collective-permute-start.3) | collective-permute-done | bytes 491552 | tf_op jit(solution)/shard_map/ppermute | solution.py:29
  30.0 1.4 %copy.96 = bf16[2,8,80,1024]{3,1,2,0:T(8,128)(2,1)S(1)} copy(bf16[2,8,80,1024]{3,2,1,0:T(8,128)(2,1)S(1)} %bitcast.304) | data formatting | bytes 5242880
  31.5 0.6 convolution_convert_fusion
  32.7 0.4 copy-done.4
  33.2 0.5 copy-done.13
  33.7 0.8 copy-done.6
  34.6 0.6 gather_fusion.1
  35.2 0.7 gather_fusion.3
  36.1 5.4 %collective-permute-start.4 = (f32[1,1,85,32]{2,3,1,0:T(8,128)S(1)}, f32[1,1,85,32]{2,3,1,0:T(8,128)S(1)}, u32[]{:S(2)}, u32[]{:S(2)}) collective-permute-start(f32[1,1,85,32]{2,3,1,0:T(8,128)S(1)} %bitcast.328), channel_id=1, source_target_pairs={{0,16},{16,32},{32,48},{48,64},{64,80},{80,96},{96,112},{1,17},{17... | collective-permute-start | bytes 32648 | tf_op jit(solution)/shard_map/ppermute | solution.py:26
  41.5 1.9 %collective-permute-start.5 = (f32[1,1,85,32]{2,3,1,0:T(8,128)S(1)}, f32[1,1,85,32]{2,3,1,0:T(8,128)S(1)}, u32[]{:S(2)}, u32[]{:S(2)}) collective-permute-start(f32[1,1,85,32]{2,3,1,0:T(8,128)S(1)} %bitcast.329), channel_id=1, source_target_pairs={{16,0},{32,16},{48,32},{64,48},{80,64},{96,80},{112,96},{17,1},{33... | collective-permute-start | bytes 32648 | tf_op jit(solution)/shard_map/ppermute | solution.py:29
  43.4 0.6 pad_clamp_fusion
  44.0 2.5 %collective-permute-done.5 = f32[1,1,85,32]{2,3,1,0:T(8,128)S(1)} collective-permute-done((f32[1,1,85,32]{2,3,1,0:T(8,128)S(1)}, f32[1,1,85,32]{2,3,1,0:T(8,128)S(1)}, u32[]{:S(2)}, u32[]{:S(2)}) %collective-permute-start.5) | collective-permute-done | bytes 10912 | tf_op jit(solution)/shard_map/ppermute | solution.py:29
  46.6 3.1 %collective-permute-start.6 = (f32[3,1,85,32]{2,3,1,0:T(8,128)S(1)}, f32[3,1,85,32]{2,3,1,0:T(8,128)S(1)}, u32[]{:S(2)}, u32[]{:S(2)}) collective-permute-start(f32[3,1,85,32]{2,3,1,0:T(8,128)S(1)} %pad_maximum_fusion.4), channel_id=1, source_target_pairs={{0,1},{1,2},{2,3},{3,4},{4,5},{5,6},{6,7},{7,8},{8,9},{9,10},{10,1... | collective-permute-start | bytes 97928 | tf_op jit(solution)/shard_map/ppermute | solution.py:26
  49.7 5.2 %collective-permute-start.7 = (f32[3,1,85,32]{2,3,1,0:T(8,128)S(1)}, f32[3,1,85,32]{2,3,1,0:T(8,128)S(1)}, u32[]{:S(2)}, u32[]{:S(2)}) collective-permute-start(f32[3,1,85,32]{2,3,1,0:T(8,128)S(1)} %pad_maximum_fusion.4), channel_id=1, source_target_pairs={{1,0},{2,1},{3,2},{4,3},{5,4},{6,5},{7,6},{8,7},{9,8},{10,9},{11,1... | collective-permute-start | bytes 97928 | tf_op jit(solution)/shard_map/ppermute | solution.py:29
  54.9 1.3 %gather_fusion.8 = f32[32]{0:T(128)} fusion(f32[64]{0:T(128)S(1)} %bitcast.295, s32[1024]{0:T(1024)S(1)} %get-tuple-element.68), kind=kCustom, calls=%fused_computation.8 | custom fusion | bytes 384 | tf_op jit(solution)/shard_map/gather | solution.py:106
  56.2 0.7 gather_fusion.10
  56.9 0.7 copy.62
  57.6 0.7 copy.61
  58.7 0.9 subtract_reduce_fusion.4
  59.7 0.9 subtract_reduce_fusion.5
  60.7 0.7 bitcast_multiply_fusion.7
  61.5 0.7 bitcast_multiply_fusion.9
  63.7 0.8 fusion.6
  64.6 0.6 fusion.33
  65.3 0.8 fusion.7
  66.2 1.7 %fusion.8 = f32[12,13,8,128]{3,2,1,0:T(8,128)S(1)} fusion(f32[80,96]{0,1:T(8,128)S(1)} %bitcast.309, f32[12,8,13,128]{3,2,1,0:T(8,128)S(1)} %bitcast.314, f32[13,128]{1,0:T(8,128)} %copy-done.9, f32[80,1,128]{2,0,1:T(8,128)} %copy-done.8, f32[80,12,128]{2,0,1:T(8,128)S(1)} %bitcast.303), kind=kOutput, calls=%fused_computation.28 | convolution fusion | flops 153939968 | bytes 1847808 | tf_op jit(solution)/shard_map/dot_general | solution.py:54
  67.9 0.6 convolution_add_fusion.3
  68.6 0.6 fusion.14
  69.3 0.7 copy.55
  70.0 0.8 reshape.1439
  70.8 1.0 fusion.31
  71.9 0.4 fusion.28
  72.4 0.4 fusion.25
  72.8 0.7 fusion.80
  73.6 0.7 gather_fusion.7
  74.3 0.8 gather_fusion.9
  75.1 0.7 subtract_bitcast_fusion
  76.0 2.2 %collective-permute-start.8 = (f32[1,1,85,32]{2,3,1,0:T(8,128)S(1)}, f32[1,1,85,32]{2,3,1,0:T(8,128)S(1)}, u32[]{:S(2)}, u32[]{:S(2)}) collective-permute-start(f32[1,1,85,32]{2,3,1,0:T(8,128)S(1)} %bitcast.332), channel_id=1, source_target_pairs={{0,16},{16,32},{32,48},{48,64},{64,80},{80,96},{96,112},{1,17},{17... | collective-permute-start | bytes 32648 | tf_op jit(solution)/shard_map/ppermute | solution.py:26
  78.2 2.1 %collective-permute-start.9 = (f32[1,1,85,32]{2,3,1,0:T(8,128)S(1)}, f32[1,1,85,32]{2,3,1,0:T(8,128)S(1)}, u32[]{:S(2)}, u32[]{:S(2)}) collective-permute-start(f32[1,1,85,32]{2,3,1,0:T(8,128)S(1)} %bitcast.333), channel_id=1, source_target_pairs={{16,0},{32,16},{48,32},{64,48},{80,64},{96,80},{112,96},{17,1},{33... | collective-permute-start | bytes 32648 | tf_op jit(solution)/shard_map/ppermute | solution.py:29
  80.3 2.9 %collective-permute-done.9 = f32[1,1,85,32]{2,3,1,0:T(8,128)S(1)} collective-permute-done((f32[1,1,85,32]{2,3,1,0:T(8,128)S(1)}, f32[1,1,85,32]{2,3,1,0:T(8,128)S(1)}, u32[]{:S(2)}, u32[]{:S(2)}) %collective-permute-start.9) | collective-permute-done | bytes 10912 | tf_op jit(solution)/shard_map/ppermute | solution.py:29
  83.2 1.9 %collective-permute-start.10 = (f32[3,1,85,32]{2,3,1,0:T(8,128)S(1)}, f32[3,1,85,32]{2,3,1,0:T(8,128)S(1)}, u32[]{:S(2)}, u32[]{:S(2)}) collective-permute-start(f32[3,1,85,32]{2,3,1,0:T(8,128)S(1)} %pad_maximum_fusion.5), channel_id=1, source_target_pairs={{0,1},{1,2},{2,3},{3,4},{4,5},{5,6},{6,7},{7,8},{8,9},{9,10},{10,1... | collective-permute-start | bytes 97928 | tf_op jit(solution)/shard_map/ppermute | solution.py:26
  85.2 5.7 %collective-permute-start.11 = (f32[3,1,85,32]{2,3,1,0:T(8,128)S(1)}, f32[3,1,85,32]{2,3,1,0:T(8,128)S(1)}, u32[]{:S(2)}, u32[]{:S(2)}) collective-permute-start(f32[3,1,85,32]{2,3,1,0:T(8,128)S(1)} %pad_maximum_fusion.5), channel_id=1, source_target_pairs={{1,0},{2,1},{3,2},{4,3},{5,4},{6,5},{7,6},{8,7},{9,8},{10,9},{11,1... | collective-permute-start | bytes 97928 | tf_op jit(solution)/shard_map/ppermute | solution.py:29
  90.9 0.9 collective-permute-done.11
  95.0 0.8 fusion.9
  95.8 0.6 fusion.23
  97.1 0.8 fusion.10
  98.0 0.8 fusion.11
  99.2 0.4 fusion.15
  99.6 0.6 broadcast_in_dim.13
  100.2 0.6 convolution_add_fusion.1
  100.9 1.4 %fusion.13 = f32[1,1,80,13,128]{4,2,3,1,0:T(8,128)} fusion(f32[80,13,128]{2,0,1:T(8,128)S(1)} %fusion.14, f32[80,13,128]{2,0,1:T(8,128)S(1)} %convolution_add_fusion.1, f32[80,96,1]{0,1,2:T(8,128)S(1)} %bitcast.326, f32[12,13,8,128]{3,2,1,0:T(8,128)S(1)} %fusion.11), kind=kOutput, calls=%fused_computation.34 | convolution fusion | flops 153620480 | bytes 2267136 | tf_op jit(solution)/shard_map/dot_general | solution.py:62
  (165 shorter events, 8.8 us)
Async XLA Ops:
  0.6 31.7 %copy-start = (bf16[1,1,4,1024,128]{4,3,2,1,0:T(8,128)(2,1)S(1)}, bf16[1,1,4,1024,128]{4,3,2,1,0:T(8,128)(2,1)}, u32[]{:S(2)}) copy-start(bf16[1,1,4,1024,128]{4,3,2,1,0:T(8,128)(2,1)} %param.11) | copy-start | bytes 3145732
  0.6 11.9 %copy-start.12 = (bf16[1,1,80,1024]{3,2,1,0:T(8,128)(2,1)S(1)}, bf16[1,1,80,1024]{3,2,1,0:T(8,128)(2,1)}, u32[]{:S(2)}) copy-start(bf16[1,1,80,1024]{3,2,1,0:T(8,128)(2,1)} %param.10) | copy-start | bytes 491524
  0.7 11.1 %copy-start.1 = (s32[1,1,64]{2,1,0:T(1,128)S(1)}, s32[1,1,64]{2,1,0:T(1,128)}, u32[]{:S(2)}) copy-start(s32[1,1,64]{2,1,0:T(1,128)} %param.16) | copy-start | bytes 772
  0.7 11.9 %copy-start.24 = (s32[1,1,4]{2,1,0:T(1,128)S(1)}, s32[1,1,4]{2,1,0:T(1,128)}, u32[]{:S(2)}) copy-start(s32[1,1,4]{2,1,0:T(1,128)} %param.12) | copy-start | bytes 52
  0.7 11.9 %collective-permute-start = (bf16[1,1,80,1024]{3,2,1,0:T(8,128)(2,1)}, bf16[1,1,80,1024]{3,2,1,0:T(8,128)(2,1)S(1)}, u32[]{:S(2)}, u32[]{:S(2)}) collective-permute-start(bf16[1,1,80,1024]{3,2,1,0:T(8,128)(2,1)} %param.10), channel_id=1, source_target_pairs={{0,16},{16,32},{32,48},{48,64},{64,80},{80,96},{96,112},{1,17},{17... | collective-permute-start | bytes 491528 | tf_op jit(solution)/shard_map/ppermute | solution.py:26
  4.9 7.7 %collective-permute-start.1 = (bf16[1,1,80,1024]{3,2,1,0:T(8,128)(2,1)}, bf16[1,1,80,1024]{3,2,1,0:T(8,128)(2,1)S(1)}, u32[]{:S(2)}, u32[]{:S(2)}) collective-permute-start(bf16[1,1,80,1024]{3,2,1,0:T(8,128)(2,1)} %param.10), channel_id=1, source_target_pairs={{16,0},{32,16},{48,32},{64,48},{80,64},{96,80},{112,96},{17,1},{33... | collective-permute-start | bytes 491528 | tf_op jit(solution)/shard_map/ppermute | solution.py:29
  7.7 12.4 %copy-start.2 = (f32[1,1,64]{2,1,0:T(1,128)S(1)}, f32[1,1,64]{2,1,0:T(1,128)}, u32[]{:S(2)}) copy-start(f32[1,1,64]{2,1,0:T(1,128)} %param.14) | copy-start | bytes 772
  9.0 11.9 %copy-start.3 = (f32[1,1,64]{2,1,0:T(1,128)S(1)}, f32[1,1,64]{2,1,0:T(1,128)}, u32[]{:S(2)}) copy-start(f32[1,1,64]{2,1,0:T(1,128)} %param.15) | copy-start | bytes 772
  12.6 15.1 %collective-permute-start.2 = (bf16[3,1,80,1024]{3,2,1,0:T(8,128)(2,1)S(1)}, bf16[3,1,80,1024]{3,2,1,0:T(8,128)(2,1)S(1)}, u32[]{:S(2)}, u32[]{:S(2)}) collective-permute-start(bf16[3,1,80,1024]{3,2,1,0:T(8,128)(2,1)S(1)} %constant_dynamic-update-slice_fusion), channel_id=1, source_target_pairs={{0,1},{1,2},{2,3},{3,4},{4,5},{5,6},{6,7},{7,8},{8,9},{9,10},{10,1... | collective-permute-start | bytes 1474568 | tf_op jit(solution)/shard_map/ppermute | solution.py:26
  15.9 13.6 %collective-permute-start.3 = (bf16[3,1,80,1024]{3,2,1,0:T(8,128)(2,1)S(1)}, bf16[3,1,80,1024]{3,2,1,0:T(8,128)(2,1)S(1)}, u32[]{:S(2)}, u32[]{:S(2)}) collective-permute-start(bf16[3,1,80,1024]{3,2,1,0:T(8,128)(2,1)S(1)} %constant_dynamic-update-slice_fusion), channel_id=1, source_target_pairs={{1,0},{2,1},{3,2},{4,3},{5,4},{6,5},{7,6},{8,7},{9,8},{10,9},{11,1... | collective-permute-start | bytes 1474568 | tf_op jit(solution)/shard_map/ppermute | solution.py:29
  32.1 1.0 %copy-start.4 = (f32[1,1,80,12,128]{4,2,3,1,0:T(8,128)S(1)}, f32[1,1,80,12,128]{4,2,3,1,0:T(8,128)}, u32[]{:S(2)}) copy-start(f32[1,1,80,12,128]{4,2,3,1,0:T(8,128)} %param.9) | copy-start | bytes 1474564
  32.7 32.6 %copy-start.8 = (f32[80,1,128]{2,0,1:T(8,128)}, f32[80,1,128]{2,0,1:T(8,128)S(1)}, u32[]{:S(2)}) copy-start(f32[80,1,128]{2,0,1:T(8,128)S(1)} %convolution_bitcast_fusion) | copy-start | bytes 122884
  33.1 0.6 copy-start.13
  33.2 32.1 %copy-start.9 = (f32[13,128]{1,0:T(8,128)}, f32[13,128]{1,0:T(8,128)S(1)}, u32[]{:S(2)}) copy-start(f32[13,128]{1,0:T(8,128)S(1)} %broadcast_multiply_fusion) | copy-start | bytes 19972
  33.7 0.8 copy-start.6
  36.1 7.9 %collective-permute-start.4 = (f32[1,1,85,32]{2,3,1,0:T(8,128)S(1)}, f32[1,1,85,32]{2,3,1,0:T(8,128)S(1)}, u32[]{:S(2)}, u32[]{:S(2)}) collective-permute-start(f32[1,1,85,32]{2,3,1,0:T(8,128)S(1)} %bitcast.328), channel_id=1, source_target_pairs={{0,16},{16,32},{32,48},{48,64},{64,80},{80,96},{96,112},{1,17},{17... | collective-permute-start | bytes 32648 | tf_op jit(solution)/shard_map/ppermute | solution.py:26
  41.5 5.1 %collective-permute-start.5 = (f32[1,1,85,32]{2,3,1,0:T(8,128)S(1)}, f32[1,1,85,32]{2,3,1,0:T(8,128)S(1)}, u32[]{:S(2)}, u32[]{:S(2)}) collective-permute-start(f32[1,1,85,32]{2,3,1,0:T(8,128)S(1)} %bitcast.329), channel_id=1, source_target_pairs={{16,0},{32,16},{48,32},{64,48},{80,64},{96,80},{112,96},{17,1},{33... | collective-permute-start | bytes 32648 | tf_op jit(solution)/shard_map/ppermute | solution.py:29
  46.6 11.7 %collective-permute-start.6 = (f32[3,1,85,32]{2,3,1,0:T(8,128)S(1)}, f32[3,1,85,32]{2,3,1,0:T(8,128)S(1)}, u32[]{:S(2)}, u32[]{:S(2)}) collective-permute-start(f32[3,1,85,32]{2,3,1,0:T(8,128)S(1)} %pad_maximum_fusion.4), channel_id=1, source_target_pairs={{0,1},{1,2},{2,3},{3,4},{4,5},{5,6},{6,7},{7,8},{8,9},{9,10},{10,1... | collective-permute-start | bytes 97928 | tf_op jit(solution)/shard_map/ppermute | solution.py:26
  49.7 8.6 %collective-permute-start.7 = (f32[3,1,85,32]{2,3,1,0:T(8,128)S(1)}, f32[3,1,85,32]{2,3,1,0:T(8,128)S(1)}, u32[]{:S(2)}, u32[]{:S(2)}) collective-permute-start(f32[3,1,85,32]{2,3,1,0:T(8,128)S(1)} %pad_maximum_fusion.4), channel_id=1, source_target_pairs={{1,0},{2,1},{3,2},{4,3},{5,4},{6,5},{7,6},{8,7},{9,8},{10,9},{11,1... | collective-permute-start | bytes 97928 | tf_op jit(solution)/shard_map/ppermute | solution.py:29
  54.9 8.5 %copy-start.20 = (f32[128]{0:T(128)}, f32[128]{0:T(128)S(1)}, u32[]{:S(2)}) copy-start(f32[128]{0:T(128)S(1)} %get-tuple-element.70) | copy-start | bytes 1540
  54.9 8.5 %copy-start.22 = (f32[128]{0:T(128)}, f32[128]{0:T(128)S(1)}, u32[]{:S(2)}) copy-start(f32[128]{0:T(128)S(1)} %get-tuple-element.71) | copy-start | bytes 1540
  66.1 1.8 %copy-start.10 = (f32[80,3,32]{0,2,1:T(8,128)S(1)}, f32[80,3,32]{0,2,1:T(8,128)}, u32[]{:S(2)}) copy-start(f32[80,3,32]{0,2,1:T(8,128)} %bitcast_multiply_fusion.9) | copy-start | bytes 92164
  66.2 2.4 %copy-start.7 = (f32[80,13,128]{2,0,1:T(8,128)S(1)}, f32[80,13,128]{2,0,1:T(8,128)}, u32[]{:S(2)}) copy-start(f32[80,13,128]{2,0,1:T(8,128)} %copy-done.6) | copy-start | bytes 1597444
  66.2 2.4 %copy-start.11 = (f32[80,3,32]{0,2,1:T(8,128)S(1)}, f32[80,3,32]{0,2,1:T(8,128)}, u32[]{:S(2)}) copy-start(f32[80,3,32]{0,2,1:T(8,128)} %bitcast_multiply_fusion.7) | copy-start | bytes 92164
  68.6 3.2 %copy-start.19 = (f32[3,32]{1,0:T(4,128)S(1)}, f32[3,32]{1,0:T(4,128)}, u32[]{:S(2)}) copy-start(f32[3,32]{1,0:T(4,128)} %get-tuple-element.31) | copy-start | bytes 1156
  69.2 3.6 %copy-start.14 = (f32[13,128]{1,0:T(8,128)S(1)}, f32[13,128]{1,0:T(8,128)}, u32[]{:S(2)}) copy-start(f32[13,128]{1,0:T(8,128)} %copy-done.13) | copy-start | bytes 19972
  70.0 5.9 %copy-start.15 = (f32[1,32]{0,1:T(8,128)S(1)}, f32[1,32]{0,1:T(8,128)}, u32[]{:S(2)}) copy-start(f32[1,32]{0,1:T(8,128)} %get-tuple-element.44) | copy-start | bytes 388
  70.0 5.9 %copy-start.16 = (f32[1,32]{0,1:T(8,128)S(1)}, f32[1,32]{0,1:T(8,128)}, u32[]{:S(2)}) copy-start(f32[1,32]{0,1:T(8,128)} %get-tuple-element.45) | copy-start | bytes 388
  71.8 1.7 %copy-start.5 = (f32[80,128]{0,1:T(8,128)S(1)}, f32[80,128]{0,1:T(8,128)}, u32[]{:S(2)}) copy-start(f32[80,128]{0,1:T(8,128)} %copy.55) | copy-start | bytes 122884
  71.8 4.1 %copy-start.17 = (f32[1,32]{0,1:T(8,128)S(1)}, f32[1,32]{0,1:T(8,128)}, u32[]{:S(2)}) copy-start(f32[1,32]{0,1:T(8,128)} %copy.62) | copy-start | bytes 388
  71.8 4.1 %copy-start.18 = (f32[1,32]{0,1:T(8,128)S(1)}, f32[1,32]{0,1:T(8,128)}, u32[]{:S(2)}) copy-start(f32[1,32]{0,1:T(8,128)} %copy.61) | copy-start | bytes 388
  73.5 21.1 %copy-start.21 = (f32[128]{0:T(128)S(1)}, f32[128]{0:T(128)}, u32[]{:S(2)}) copy-start(f32[128]{0:T(128)} %copy-done.20) | copy-start | bytes 1540
  73.6 21.1 %copy-start.23 = (f32[128]{0:T(128)S(1)}, f32[128]{0:T(128)}, u32[]{:S(2)}) copy-start(f32[128]{0:T(128)} %copy-done.22) | copy-start | bytes 1540
  76.0 4.3 %collective-permute-start.8 = (f32[1,1,85,32]{2,3,1,0:T(8,128)S(1)}, f32[1,1,85,32]{2,3,1,0:T(8,128)S(1)}, u32[]{:S(2)}, u32[]{:S(2)}) collective-permute-start(f32[1,1,85,32]{2,3,1,0:T(8,128)S(1)} %bitcast.332), channel_id=1, source_target_pairs={{0,16},{16,32},{32,48},{48,64},{64,80},{80,96},{96,112},{1,17},{17... | collective-permute-start | bytes 32648 | tf_op jit(solution)/shard_map/ppermute | solution.py:26
  78.2 5.1 %collective-permute-start.9 = (f32[1,1,85,32]{2,3,1,0:T(8,128)S(1)}, f32[1,1,85,32]{2,3,1,0:T(8,128)S(1)}, u32[]{:S(2)}, u32[]{:S(2)}) collective-permute-start(f32[1,1,85,32]{2,3,1,0:T(8,128)S(1)} %bitcast.333), channel_id=1, source_target_pairs={{16,0},{32,16},{48,32},{64,48},{80,64},{96,80},{112,96},{17,1},{33... | collective-permute-start | bytes 32648 | tf_op jit(solution)/shard_map/ppermute | solution.py:29
  83.2 7.6 %collective-permute-start.10 = (f32[3,1,85,32]{2,3,1,0:T(8,128)S(1)}, f32[3,1,85,32]{2,3,1,0:T(8,128)S(1)}, u32[]{:S(2)}, u32[]{:S(2)}) collective-permute-start(f32[3,1,85,32]{2,3,1,0:T(8,128)S(1)} %pad_maximum_fusion.5), channel_id=1, source_target_pairs={{0,1},{1,2},{2,3},{3,4},{4,5},{5,6},{6,7},{7,8},{8,9},{9,10},{10,1... | collective-permute-start | bytes 97928 | tf_op jit(solution)/shard_map/ppermute | solution.py:26
  85.2 6.6 %collective-permute-start.11 = (f32[3,1,85,32]{2,3,1,0:T(8,128)S(1)}, f32[3,1,85,32]{2,3,1,0:T(8,128)S(1)}, u32[]{:S(2)}, u32[]{:S(2)}) collective-permute-start(f32[3,1,85,32]{2,3,1,0:T(8,128)S(1)} %pad_maximum_fusion.5), channel_id=1, source_target_pairs={{1,0},{2,1},{3,2},{4,3},{5,4},{6,5},{7,6},{8,7},{9,8},{10,9},{11,1... | collective-permute-start | bytes 97928 | tf_op jit(solution)/shard_map/ppermute | solution.py:29
where the time goes:
time: 104 us; the launch traced here: 102 us
  starting transfers between devices  41.1 us (40%)
  local copies, waits for them, and re-layouts  22.4 us (22%)
  matrix products  14.5 us (14%)
  waiting for transfers between devices  13.4 us (13%)
  other arithmetic  9.46 us (9%)
  between operations  1.53 us (1%)
    ppermute x6, starting transfers between devices, extended(): lax.ppermute(lax.slice_in_dim(block, 0, width, axis=dim), axis, backward)  21 us
    ppermute x6, starting transfers between devices, extended(): lax.ppermute(lax.slice_in_dim(block, block.shape[dim] - width, None, axis...  20.1 us
    ppermute x6, waiting for transfers between devices, extended(): lax.ppermute(lax.slice_in_dim(block, 0, width, axis=dim), axis, backward)  8.14 us
    dot_general x6, matrix products, update_group(): jnp.dot(observed.T, flat_anomaly, precision=exact_mode, preferred_element...  5.78 us
    ppermute x6, waiting for transfers between devices, extended(): lax.ppermute(lax.slice_in_dim(block, block.shape[dim] - width, None, axis...  5.26 us
    dot_general x6, matrix products, update_group(): jnp.dot(observed * damping[None, :], gain, precision=exact_mode, preferre...  4.66 us
    unnamed x55, local copies, waits for them, and re-layouts  3.86 us
    dot_general x6, matrix products, update_group(): jnp.dot(innovation[None, :], gain, precision=exact_mode, preferred_elemen...  3.1 us
  transfers between devices with their start and end apart: 12, of which 5 were waited for; matrix products, arithmetic and copies ran while one was open for 12% of the time, Pallas kernels for 0%

commit v1 on v0

v1 whole, which is shorter than its diff:
```python
import functools

import jax
import jax.numpy as jnp
from jax import lax
from jax.experimental import pallas as pl
from jax.experimental.pallas import tpu as pltpu
from jax.sharding import PartitionSpec as P

MEM = 80
AX = 8
AY = 16
OCN_DEV = 1024
OB = 32
NB = 2
K = 4
FIELDS = 12
COMP = 13
CELLS = 128
OBS_DEV = 64

f32 = jnp.float32
META = 4
TAPER = {0: 1.0, 1: 0.5625, 2: 0.25}
OFFSETS = [(dx, dy) for dx in (-1, 0, 1) for dy in (-1, 0, 1)]


def ring(block, axis, step):
    count = lax.axis_size(axis)
    return lax.ppermute(block, axis, [(i, (i + step) % count) for i in range(count)])


def swap(block, axis, first):
    count = lax.axis_size(axis)
    pairs = []
    for at in range(first, count + first, 2):
        low, high = at % count, (at + 1) % count
        pairs += [(low, high), (high, low)]
    return lax.ppermute(block, axis, sorted(pairs))


def lanes(rows=1):
    return lax.broadcasted_iota(jnp.int32, (rows, CELLS), 1)


def remap_kernel(sel_ref, meta_ref, w_ref, *refs):
    tiles, (state_ref, message_ref) = refs[:9], refs[9:]
    state_ref[...] = jnp.zeros_like(state_ref)

    def one(k, carry):
        for index, tile in enumerate(tiles):

            @pl.when(sel_ref[k] == index)
            def _():
                state_ref[...] += jnp.dot(tile[...], w_ref[k], preferred_element_type=f32)

        return carry

    lax.fori_loop(0, K, one, 0)
    lane = lanes()
    message_ref[...] = jnp.where(
        (lane >= META) & (lane < META + 3), meta_ref[...], state_ref[...]
    )


def anomaly_kernel(atm_ref, state_ref, mean_ref, anom_ref):
    total = jnp.sum(atm_ref[...], axis=0) / MEM
    surface = state_ref[...]
    sst_mean = jnp.sum(surface, axis=0, keepdims=True) / MEM
    mean_ref[...] = jnp.zeros_like(mean_ref)
    mean_ref[0:FIELDS, :] = total
    mean_ref[FIELDS : FIELDS + 1, :] = sst_mean

    def one(m, carry):
        anom_ref[m, 0:FIELDS, :] = atm_ref[m] - total
        anom_ref[m, FIELDS:16, :] = jnp.broadcast_to(
            state_ref[pl.ds(m, 1), :] - sst_mean, (16 - FIELDS, CELLS)
        )
        return carry

    lax.fori_loop(0, MEM, one, 0, unroll=4)


def side_kernel(meta_ref, state_ref, before_ref, after_ref, right_ref, left_ref):
    lane = lanes()
    state = state_ref[...]
    before = before_ref[...]
    after = after_ref[...]
    columns = jnp.where(lane % AY >= 8, before, after)
    turned = pltpu.roll(columns, 64, 1)
    right = jnp.where(lane >= 64, state, turned)
    left = jnp.where(lane < 64, state, turned)
    meta = meta_ref[...]

    def put(block, start, record, shift):
        moved = pltpu.roll(record, shift, 1) if shift else record
        return jnp.where((lane >= start) & (lane < start + 3), moved, block)

    for n, record in enumerate((meta, before, after)):
        right = put(right, META + 3 * n, record, 3 * n)
        left = put(left, 32 + META + 3 * n, record, 32 + 3 * n)
    right_ref[...] = right
    left_ref[...] = left


def views(blocks):
    lane = lanes()
    y = lane % AY
    x = lane // AY
    m0, m1, h0, h1 = blocks

    def up(a, b):
        return jnp.where(y == 15, pltpu.roll(b, 15, 1), pltpu.roll(a, 127, 1))

    def down(a, b):
        return jnp.where(y == 0, pltpu.roll(b, 113, 1), pltpu.roll(a, 1, 1))

    rows = {
        0: blocks,
        1: (up(m0, h0), up(m1, h1), up(h0, m0), up(h1, m1)),
        -1: (down(m0, h0), down(m1, h1), down(h0, m0), down(h1, m1)),
    }
    out = {}
    for dy, (a0, a1, b0, b1) in rows.items():
        out[0, dy] = (a0, a1, b0, b1)
        for dx, edge, shift in ((1, 0, 112), (-1, 7, 16)):

            def pair(u, v):
                return (
                    pltpu.roll(jnp.where(x == edge, v, u), shift, 1),
                    pltpu.roll(jnp.where(x == edge, u, v), shift, 1),
                )

            out[dx, dy] = pair(a0, a1) + pair(b0, b1)
    return out


def own_views(blocks):
    return {key: value[0] for key, value in views(blocks).items()}


def analysis_kernel(
    flag_ref, meta_ref, state_ref, before_ref, after_ref, west_ref, east_ref, mean_ref, anom_ref,
    post_mean_ref, post_anom_ref, first_ref, second_ref, work_ref,
):
    lane = lanes()
    y = lane % AY
    low_x = lane < 64
    high_y = y >= 8
    has_west = flag_ref[0]
    has_east = flag_ref[1]
    has_before = flag_ref[2]
    has_after = flag_ref[3]
    west = west_ref[...]
    east = east_ref[...]
    fields = [
        state_ref[...],
        jnp.where(low_x, east, west),
        jnp.where(high_y, before_ref[...], after_ref[...]),
        pltpu.roll(jnp.where(low_x, west, east), 64, 1),
    ]
    means = [jnp.sum(field, axis=0, keepdims=True) / MEM for field in fields]
    anoms = [field - mean for field, mean in zip(fields, means)]
    side_x = jnp.where(low_x, has_east, has_west)
    side_y = jnp.where(high_y, has_before, has_after)
    open_lane = [jnp.ones_like(side_x), side_x, side_y, side_x * side_y]

    def weights(batch, anoms, means):
        rows = pl.ds(batch * OB, OB)

        def column(ref, at):
            return jnp.broadcast_to(ref[rows, at : at + 1], (OB, CELLS))

        def record(block, n):
            if block == 0:
                return column(meta_ref, META + n)
            if block == 1:
                return jnp.where(
                    low_x, column(east_ref, 32 + META + n), column(west_ref, META + n)
                )
            if block == 2:
                return jnp.where(
                    high_y, column(before_ref, META + n), column(after_ref, META + n)
                )
            return jnp.where(
                low_x,
                jnp.where(
                    high_y,
                    column(east_ref, 32 + META + 3 + n),
                    column(east_ref, 32 + META + 6 + n),
                ),
                jnp.where(
                    high_y, column(west_ref, META + 3 + n), column(west_ref, META + 6 + n)
                ),
            )

        pulls, damped = [], []
        for block in range(4):
            anom, mean = anoms[block], means[block]
            variance = jnp.sum(anom * anom, axis=0, keepdims=True) / (MEM - 1)
            here = (record(block, 0) == lane.astype(f32)) & (open_lane[block] > 0)
            error = record(block, 2)
            denominator = variance + error
            pull = (record(block, 1) - mean) / denominator
            damp = 1.0 / (denominator + jnp.sqrt(error * denominator))
            pulls.append(jnp.sum(jnp.where(here, pull, 0.0), axis=0, keepdims=True))
            damped.append(jnp.sum(jnp.where(here, damp, 0.0), axis=0, keepdims=True))
        return pulls, damped

    def spread(rows):
        return [jnp.broadcast_to(row, (8, CELLS)) for row in rows]

    pulls, damped = weights(0, anoms, means)
    shifted = views(anoms)
    for n, key in enumerate(OFFSETS):
        first_ref[n] = shifted[key][0]
    pull_views = views(spread(pulls))
    damp_views = views(spread(damped))

    def scale(key):
        return TAPER[key[0] ** 2 + key[1] ** 2] / (MEM - 1)

    next_means, next_anoms = [], []
    for block in range(4):
        step = jnp.zeros_like(means[block])
        moved = anoms[block]
        for key in OFFSETS:
            view = shifted[key][block]
            covariance = jnp.sum(view * anoms[block], axis=0, keepdims=True) * scale(key)
            step = step + covariance * pull_views[key][block][0:1]
            moved = moved - (covariance * damp_views[key][block][0:1]) * view
        next_means.append(means[block] + step)
        next_anoms.append(moved)
    next_pulls, next_damped = weights(1, next_anoms, next_means)
    next_shifted = own_views(next_anoms)
    for n, key in enumerate(OFFSETS):
        second_ref[n] = next_shifted[key]
    next_pull_views = own_views(spread(next_pulls))
    next_damp_views = own_views(spread(next_damped))

    zero = jnp.zeros((16, CELLS), f32)

    def cov_first(m, sums):
        block = anom_ref[m]
        return tuple(s + block * first_ref[n, pl.ds(m, 1), :] for n, s in enumerate(sums))

    sums = lax.fori_loop(0, MEM, cov_first, (zero,) * 9, unroll=2)
    mean = mean_ref[...]
    gains = []
    for n, key in enumerate(OFFSETS):
        covariance = sums[n] * scale(key)
        mean = mean + covariance * pull_views[key][0][0:1]
        gains.append(covariance * damp_views[key][0][0:1])

    def step_first(m, sums):
        block = anom_ref[m]
        for n in range(9):
            block = block - gains[n] * first_ref[n, pl.ds(m, 1), :]
        work_ref[m] = block
        return tuple(s + block * second_ref[n, pl.ds(m, 1), :] for n, s in enumerate(sums))

    sums = lax.fori_loop(0, MEM, step_first, (zero,) * 9)
    last = []
    for n, key in enumerate(OFFSETS):
        covariance = sums[n] * scale(key)
        mean = mean + covariance * next_pull_views[key][0:1]
        last.append(covariance * next_damp_views[key][0:1])
    post_mean_ref[...] = mean[0:COMP]

    def step_second(m, carry):
        block = work_ref[m]
        for n in range(9):
            block = block - last[n] * second_ref[n, pl.ds(m, 1), :]
        post_anom_ref[m] = block[0:COMP]
        return carry

    lax.fori_loop(0, MEM, step_second, 0, unroll=2)


VMEM = pl.BlockSpec(memory_space=pltpu.VMEM)
SMEM = pl.BlockSpec(memory_space=pltpu.SMEM)


def flat(*shape):
    return jax.ShapeDtypeStruct(shape, f32)


def local(
    atm_members,
    ocean_members,
    remap_weights,
    pair_src,
    obs_cell,
    obs_value,
    obs_error,
    obs_live,
    obs_order,
):
    at_x = lax.axis_index("gx")
    at_y = lax.axis_index("gy")
    rows = lax.axis_size("gy")
    own = ocean_members[0, 0]
    before = ring(own, "gy", 1)
    after = ring(own, "gy", -1)
    tiles = [own, before, after]
    for first in (0, 1):
        tiles += [swap(tile, "gx", first) for tile in (own, before, after)]
    source = pair_src[0, 0]
    step_x = source // rows - at_x
    step_y = source % rows - at_y
    side = jnp.where(step_x == 0, 0, jnp.where((step_x == 1) == (at_x % 2 == 0), 1, 2))
    select = side * 3 + jnp.where(step_y == 0, 0, jnp.where(step_y < 0, 1, 2))

    order = obs_order[0, 0][:, None] == jnp.arange(OBS_DEV, dtype=jnp.int32)[None, :]

    def ordered(values):
        return jnp.sum(jnp.where(order, values[None, :], 0.0), axis=1, keepdims=True)

    cell = jnp.where(obs_live[0, 0] > 0, obs_cell[0, 0], -1).astype(f32)
    lane = jnp.arange(CELLS, dtype=jnp.int32)[None, :]
    meta = jnp.where(
        lane == META,
        ordered(cell),
        jnp.where(
            lane == META + 1,
            ordered(obs_value[0, 0]),
            jnp.where(lane == META + 2, ordered(obs_error[0, 0]), 0.0),
        ),
    )
    meta = jnp.pad(meta, ((0, MEM - OBS_DEV), (0, 0)))
    flags = jnp.stack(
        [at_x > 0, at_x < lax.axis_size("gx") - 1, at_y > 0, at_y < rows - 1]
    ).astype(jnp.int32)

    state, message = pl.pallas_call(
        remap_kernel,
        in_specs=[SMEM, VMEM, VMEM] + [VMEM] * 9,
        out_specs=[VMEM, VMEM],
        out_shape=[flat(MEM, CELLS), flat(MEM, CELLS)],
        name="remap",
    )(select, meta, remap_weights[0, 0], *tiles)
    from_before = ring(message, "gy", 1)
    from_after = ring(message, "gy", -1)
    mean, anomaly = pl.pallas_call(
        anomaly_kernel,
        in_specs=[VMEM, VMEM],
        out_specs=[VMEM, VMEM],
        out_shape=[flat(16, CELLS), flat(MEM, 16, CELLS)],
        name="anomaly",
    )(atm_members[0, 0], state)
    to_right, to_left = pl.pallas_call(
        side_kernel,
        in_specs=[VMEM] * 4,
        out_specs=[VMEM, VMEM],
        out_shape=[flat(MEM, CELLS), flat(MEM, CELLS)],
        name="side",
    )(meta, state, from_before, from_after)
    from_west = ring(to_right, "gx", 1)
    from_east = ring(to_left, "gx", -1)
    post_mean, post_anom = pl.pallas_call(
        analysis_kernel,
        in_specs=[SMEM] + [VMEM] * 8,
        out_specs=[VMEM, VMEM],
        out_shape=[flat(COMP, CELLS), flat(MEM, COMP, CELLS)],
        scratch_shapes=[
            pltpu.VMEM((9, MEM, CELLS), f32),
            pltpu.VMEM((9, MEM, CELLS), f32),
            pltpu.VMEM((MEM, 16, CELLS), f32),
        ],
        name="analysis",
    )(flags, meta, state, from_before, from_after, from_west, from_east, mean, anomaly)
    return post_mean[None, None], post_anom[None, None]


def solution(mesh):
    in_specs = (
        P("gx", "gy", None, None, None),
        P("gx", "gy", None, None),
        P("gx", "gy", None, None, None),
        P("gx", "gy", None),
        P("gx", "gy", None),
        P("gx", "gy", None),
        P("gx", "gy", None),
        P("gx", "gy", None),
        P("gx", "gy", None),
    )
    out_specs = (P("gx", "gy", None, None), P("gx", "gy", None, None, None))
    return jax.shard_map(local, mesh=mesh, in_specs=in_specs, out_specs=out_specs, check_vma=False)
```

time: 104 us -> 58.8 us (0.57)
  the two profiles are of different devices: /device:TPU:7 before, /device:TPU:0 now
where the time goes in v1:
time: 58.8 us; the launch traced here: 58.4 us
  waiting for transfers between devices  20.2 us (34%)
  starting transfers between devices  14 us (24%)
  Pallas kernels  13.5 us (23%)
  local copies, waits for them, and re-layouts  8.27 us (14%)
  other arithmetic  1.51 us (3%)
  between operations  0.82 us (1%)
    ppermute x6, waiting for transfers between devices, ring(): lax.ppermute(block, axis, [(i, (i + step) % count) for i in range(count)])  15 us
    ppermute x6, starting transfers between devices, ring(): lax.ppermute(block, axis, [(i, (i + step) % count) for i in range(count)])  10.2 us
    unnamed x41, local copies, waits for them, and re-layouts  7.65 us
    pallas_call x1, Pallas kernels, local(): pl.pallas_call(analysis_kernel, in_specs=[SMEM] + [VMEM] * 8, out_specs=[...  6.33 us
    ppermute x6, waiting for transfers between devices, swap(): return lax.ppermute(block, axis, sorted(pairs))  5.28 us
    ppermute x6, starting transfers between devices, swap(): return lax.ppermute(block, axis, sorted(pairs))  3.84 us
    pallas_call x1, Pallas kernels, local(): pl.pallas_call(remap_kernel, in_specs=[SMEM, VMEM, VMEM] + [VMEM] * 9, ou...  3.4 us
    pallas_call x1, Pallas kernels, local(): pl.pallas_call(anomaly_kernel, in_specs=[VMEM, VMEM], out_specs=[VMEM, VM...  2.18 us
  transfers between devices with their start and end apart: 12, of which 5 were waited for; matrix products, arithmetic and copies ran while one was open for 5% of the time, Pallas kernels for 4%

profile of v1, /device:TPU:0, one launch (start us, length us, event | category | flops | bytes accessed | tf_op | source)
XLA Modules:
  0.0 58.4 jit_solution(12134867851233876677)
XLA Ops:
  0.6 3.7 %collective-permute-start.5 = (bf16[80,1024]{1,0:T(8,128)(2,1)}, bf16[80,1024]{1,0:T(8,128)(2,1)S(1)}, u32[]{:S(2)}, u32[]{:S(2)}) collective-permute-start(bf16[80,1024]{1,0:T(8,128)(2,1)} %bitcast.32), channel_id=1, source_target_pairs={{0,112},{16,32},{32,16},{48,64},{64,48},{80,96},{96,80},{112,0},{1... | collective-permute-start | bytes 491528 | tf_op jit(solution)/shard_map/ppermute | solution.py:39
  4.3 0.0 collective-permute-start.2
  4.3 5.2 %collective-permute-start.1 = (bf16[80,1024]{1,0:T(8,128)(2,1)}, bf16[80,1024]{1,0:T(8,128)(2,1)S(1)}, u32[]{:S(2)}, u32[]{:S(2)}) collective-permute-start(bf16[80,1024]{1,0:T(8,128)(2,1)} %bitcast.34), channel_id=1, source_target_pairs={{0,15},{1,0},{2,1},{3,2},{4,3},{5,4},{6,5},{7,6},{8,7},{9,8},{10,9... | collective-permute-start | bytes 491528 | tf_op jit(solution)/shard_map/ppermute | solution.py:30
  9.5 0.0 collective-permute-start
  9.5 0.0 copy-start.17
  9.6 0.0 copy-start.18
  9.6 0.6 %copy-done.17 = s32[1,1,64]{2,1,0:T(1,128)S(1)} copy-done((s32[1,1,64]{2,1,0:T(1,128)S(1)}, s32[1,1,64]{2,1,0:T(1,128)}, u32[]{:S(2)}) %copy-start.17) | copy-done | bytes 280
  10.2 0.0 copy-done.18
  10.2 0.0 copy-start.13
  10.2 0.0 copy-start.15
  10.2 0.6 %copy-done.13 = s32[1,1,64]{2,1,0:T(1,128)S(1)} copy-done((s32[1,1,64]{2,1,0:T(1,128)S(1)}, s32[1,1,64]{2,1,0:T(1,128)}, u32[]{:S(2)}) %copy-start.13) | copy-done | bytes 280
  10.9 0.0 copy-done.14
  10.9 0.0 copy-done.15
  10.9 0.2 select_reduce_fusion.2
  11.1 0.1 select_select_fusion
  11.2 0.0 copy-start.16
  11.2 0.6 %pad.4.meta_ref = f32[80,128]{1,0:T(8,128)} pad(f32[64,128]{1,0:T(8,128)S(1)} %select_select_fusion, f32[]{:T(128)} %constant.60.clone.1), padding=0_16x0_0 | pad | bytes 73732 | tf_op jit(solution)/shard_map/jit(_pad)/pad | solution.py:330
  11.9 2.1 %collective-permute-done.1.refs_2_ = bf16[80,1024]{1,0:T(8,128)(2,1)S(1)} collective-permute-done((bf16[80,1024]{1,0:T(8,128)(2,1)}, bf16[80,1024]{1,0:T(8,128)(2,1)S(1)}, u32[]{:S(2)}, u32[]{:S(2)}) %collective-permute-start.1) | collective-permute-done | bytes 163872 | tf_op jit(solution)/shard_map/ppermute | solution.py:30
  14.0 0.0 collective-permute-start.7
  14.0 0.1 collective-permute-start.4
  14.0 5.3 %collective-permute-done.refs_1_ = bf16[80,1024]{1,0:T(8,128)(2,1)S(1)} collective-permute-done((bf16[80,1024]{1,0:T(8,128)(2,1)}, bf16[80,1024]{1,0:T(8,128)(2,1)S(1)}, u32[]{:S(2)}, u32[]{:S(2)}) %collective-permute-start) | collective-permute-done | bytes 163872 | tf_op jit(solution)/shard_map/ppermute | solution.py:30
  19.4 0.0 collective-permute-start.6
  19.4 0.0 collective-permute-done.5.refs_6_
  19.4 0.0 copy-start.1
  19.4 0.1 collective-permute-start.3
  19.5 0.0 copy-done.16
  19.5 0.5 fusion.3.sel_ref
  20.0 0.0 collective-permute-done.2.refs_3_
  20.0 0.0 collective-permute-done.7.refs_8_
  20.0 0.0 copy-start.5
  20.0 0.0 collective-permute-done.4.refs_5_
  20.1 0.0 copy-start.6
  20.1 5.3 %collective-permute-done.6.refs_7_ = bf16[80,1024]{1,0:T(8,128)(2,1)S(1)} collective-permute-done((bf16[80,1024]{1,0:T(8,128)(2,1)S(1)}, bf16[80,1024]{1,0:T(8,128)(2,1)S(1)}, u32[]{:S(2)}, u32[]{:S(2)}) %collective-permute-start.6) | collective-permute-done | bytes 163872 | tf_op jit(solution)/shard_map/ppermute | solution.py:39
  25.3 0.0 collective-permute-done.3.refs_4_
  25.3 0.0 copy-done.3
  25.3 0.0 copy-done.4
  25.4 0.0 copy-done.1
  25.4 0.0 copy-done.2
  25.4 0.0 copy-done.5
  25.4 0.0 copy-done.6
  25.4 0.6 %copy-done.7 = bf16[80,1024]{1,0:T(8,128)(2,1)} copy-done((bf16[80,1024]{1,0:T(8,128)(2,1)}, bf16[80,1024]{1,0:T(8,128)(2,1)S(1)}, u32[]{:S(2)}) %copy-start.7) | copy-done | bytes 163864
  26.0 0.1 copy-done.8
  26.1 3.4 %remap.1 = (f32[80,128]{1,0:T(8,128)}, f32[80,128]{1,0:T(8,128)}) custom-call(s32[4]{0:T(128)} %fusion.3.sel_ref, f32[80,128]{1,0:T(8,128)} %pad.4.meta_ref, bf16[4,1024,128]{2,1,0:T(8,128)(2,1)} %bitcast.30, bf16[80,1024]{1,0:T(8,128)(2,1)} %bitcast.36, bf16[80,1024]{1,0:T(8,128)(2,1)} %copy-done.4, bf16[80,1024]{1,0:T(8,128)(2,1)} %copy-done.3, ...), custom_call_target="tpu_custom_call" | custom-call | tf_op jit(solution)/shard_map/remap/pallas_call | solution.py:335
  29.5 2.0 %collective-permute-start.9 = (f32[80,128]{1,0:T(8,128)}, f32[80,128]{1,0:T(8,128)S(1)}, u32[]{:S(2)}, u32[]{:S(2)}) collective-permute-start(f32[80,128]{1,0:T(8,128)} %get-tuple-element.11), channel_id=1, source_target_pairs={{0,15},{1,0},{2,1},{3,2},{4,3},{5,4},{6,5},{7,6},{8,7},{9,8},{10,9... | collective-permute-start | bytes 122888 | tf_op jit(solution)/shard_map/ppermute | solution.py:30
  31.5 0.0 collective-permute-start.8
  31.5 2.2 %collective-permute-done.9.after_ref = f32[80,128]{1,0:T(8,128)S(1)} collective-permute-done((f32[80,128]{1,0:T(8,128)}, f32[80,128]{1,0:T(8,128)S(1)}, u32[]{:S(2)}, u32[]{:S(2)}) %collective-permute-start.9) | collective-permute-done | bytes 40992 | tf_op jit(solution)/shard_map/ppermute | solution.py:30
  33.7 5.4 %collective-permute-done.8.before_ref = f32[80,128]{1,0:T(8,128)S(1)} collective-permute-done((f32[80,128]{1,0:T(8,128)}, f32[80,128]{1,0:T(8,128)S(1)}, u32[]{:S(2)}, u32[]{:S(2)}) %collective-permute-start.8) | collective-permute-done | bytes 40992 | tf_op jit(solution)/shard_map/ppermute | solution.py:30
  39.0 0.0 copy-done.9
  39.0 0.6 %copy-done.10 = f32[80,128]{1,0:T(8,128)} copy-done((f32[80,128]{1,0:T(8,128)}, f32[80,128]{1,0:T(8,128)S(1)}, u32[]{:S(2)}) %copy-start.10) | copy-done | bytes 40984
  39.6 1.6 %side.1 = (f32[80,128]{1,0:T(8,128)}, f32[80,128]{1,0:T(8,128)}) custom-call(f32[80,128]{1,0:T(8,128)} %pad.4.meta_ref, f32[80,128]{1,0:T(8,128)} %get-tuple-element.10.state_ref, f32[80,128]{1,0:T(8,128)} %copy-done.10, f32[80,128]{1,0:T(8,128)} %copy-done.9), custom_call_target="tpu_custom_call" | custom-call | tf_op jit(solution)/shard_map/side/pallas_call | solution.py:351
  41.2 0.0 collective-permute-start.10
  41.2 3.0 %collective-permute-start.11 = (f32[80,128]{1,0:T(8,128)}, f32[80,128]{1,0:T(8,128)S(1)}, u32[]{:S(2)}, u32[]{:S(2)}) collective-permute-start(f32[80,128]{1,0:T(8,128)} %get-tuple-element.13), channel_id=1, source_target_pairs={{0,112},{16,0},{32,16},{48,32},{64,48},{80,64},{96,80},{112,96},{1... | collective-permute-start | bytes 122888 | tf_op jit(solution)/shard_map/ppermute | solution.py:30
  44.2 0.7 %add_convert_fusion.flag_ref = s32[4]{0:T(128)} fusion(pred[1]{0:T(512)(128)(4,1)} %bitcast.3, pred[1]{0:T(512)(128)(4,1)} %bitcast.2, pred[1]{0:T(512)(128)(4,1)} %bitcast.1, pred[1]{0:T(512)(128)(4,1)} %bitcast), kind=kLoop, calls=%fused_computation.6 | loop fusion | flops 16 | bytes 20 | tf_op jit(solution)/shard_map/convert_element_type | solution.py:333
  44.9 0.0 copy-done
  44.9 1.0 %copy.18 = f32[1,1,80,12,128]{4,3,2,1,0:T(8,128)} copy(f32[1,1,80,12,128]{4,2,3,1,0:T(8,128)S(1)} %copy-done) | data formatting | bytes 983040 | tf_op args[0]
  45.9 2.2 %anomaly.1 = (f32[16,128]{1,0:T(8,128)}, f32[80,16,128]{2,1,0:T(8,128)}) custom-call(f32[80,12,128]{2,1,0:T(8,128)} %bitcast.29, f32[80,128]{1,0:T(8,128)} %get-tuple-element.10.state_ref), custom_call_target="tpu_custom_call" | custom-call | tf_op jit(solution)/shard_map/anomaly/pallas_call | solution.py:344
  48.1 0.0 collective-permute-done.10.west_ref
  48.1 0.0 collective-permute-done.11.east_ref
  48.1 0.0 copy-start.12
  48.1 0.6 %copy-done.11 = f32[80,128]{1,0:T(8,128)} copy-done((f32[80,128]{1,0:T(8,128)}, f32[80,128]{1,0:T(8,128)S(1)}, u32[]{:S(2)}) %copy-start.11) | copy-done | bytes 40984
  48.7 0.0 copy-done.12
  48.7 6.3 %analysis.1 = (f32[13,128]{1,0:T(8,128)}, f32[80,13,128]{2,1,0:T(8,128)}) custom-call(s32[4]{0:T(128)} %add_convert_fusion.flag_ref, f32[80,128]{1,0:T(8,128)} %pad.4.meta_ref, f32[80,128]{1,0:T(8,128)} %get-tuple-element.10.state_ref, f32[80,128]{1,0:T(8,128)} %copy-done.10, f32[80,128]{1,0:T(8,128)} %copy-done.9, f32[80,128]{1,0:T(8,128)} %copy-done.11, ...), custom_call_target="tpu_custom_call" | custom-call | tf_op jit(solution)/shard_map/analysis/pallas_call | solution.py:360
  55.0 1.3 %copy.15 = f32[1,1,13,128]{3,1,2,0:T(1,128)} copy(f32[1,1,13,128]{3,2,1,0:T(8,128)} %bitcast.37) | data formatting | bytes 13312
  56.3 2.1 %copy.16 = f32[1,1,80,13,128]{4,2,3,1,0:T(8,128)} copy(f32[1,1,80,13,128]{4,3,2,1,0:T(8,128)} %bitcast.31) | data formatting | bytes 1064960
  (13 shorter events, 0.0 us)
Async XLA Ops:
  0.6 18.8 %collective-permute-start.5 = (bf16[80,1024]{1,0:T(8,128)(2,1)}, bf16[80,1024]{1,0:T(8,128)(2,1)S(1)}, u32[]{:S(2)}, u32[]{:S(2)}) collective-permute-start(bf16[80,1024]{1,0:T(8,128)(2,1)} %bitcast.32), channel_id=1, source_target_pairs={{0,112},{16,32},{32,16},{48,64},{64,48},{80,96},{96,80},{112,0},{1... | collective-permute-start | bytes 491528 | tf_op jit(solution)/shard_map/ppermute | solution.py:39
  4.3 15.7 %collective-permute-start.2 = (bf16[80,1024]{1,0:T(8,128)(2,1)}, bf16[80,1024]{1,0:T(8,128)(2,1)S(1)}, u32[]{:S(2)}, u32[]{:S(2)}) collective-permute-start(bf16[80,1024]{1,0:T(8,128)(2,1)} %bitcast.33), channel_id=1, source_target_pairs={{0,16},{16,0},{32,48},{48,32},{64,80},{80,64},{96,112},{112,96},{1... | collective-permute-start | bytes 491528 | tf_op jit(solution)/shard_map/ppermute | solution.py:39
  4.3 9.7 %collective-permute-start.1 = (bf16[80,1024]{1,0:T(8,128)(2,1)}, bf16[80,1024]{1,0:T(8,128)(2,1)S(1)}, u32[]{:S(2)}, u32[]{:S(2)}) collective-permute-start(bf16[80,1024]{1,0:T(8,128)(2,1)} %bitcast.34), channel_id=1, source_target_pairs={{0,15},{1,0},{2,1},{3,2},{4,3},{5,4},{6,5},{7,6},{8,7},{9,8},{10,9... | collective-permute-start | bytes 491528 | tf_op jit(solution)/shard_map/ppermute | solution.py:30
  9.5 9.9 %collective-permute-start = (bf16[80,1024]{1,0:T(8,128)(2,1)}, bf16[80,1024]{1,0:T(8,128)(2,1)S(1)}, u32[]{:S(2)}, u32[]{:S(2)}) collective-permute-start(bf16[80,1024]{1,0:T(8,128)(2,1)} %bitcast.35), channel_id=1, source_target_pairs={{0,1},{1,2},{2,3},{3,4},{4,5},{5,6},{6,7},{7,8},{8,9},{9,10},{10,1... | collective-permute-start | bytes 491528 | tf_op jit(solution)/shard_map/ppermute | solution.py:30
  9.5 0.7 %copy-start.17 = (s32[1,1,64]{2,1,0:T(1,128)S(1)}, s32[1,1,64]{2,1,0:T(1,128)}, u32[]{:S(2)}) copy-start(s32[1,1,64]{2,1,0:T(1,128)} %param.13) | copy-start | bytes 772
  9.6 0.7 %copy-start.18 = (s32[1,1,64]{2,1,0:T(1,128)S(1)}, s32[1,1,64]{2,1,0:T(1,128)}, u32[]{:S(2)}) copy-start(s32[1,1,64]{2,1,0:T(1,128)} %param.16) | copy-start | bytes 772
  10.2 0.7 %copy-start.13 = (s32[1,1,64]{2,1,0:T(1,128)S(1)}, s32[1,1,64]{2,1,0:T(1,128)}, u32[]{:S(2)}) copy-start(s32[1,1,64]{2,1,0:T(1,128)} %param.17) | copy-start | bytes 772
  10.2 0.7 %copy-start.14 = (f32[1,1,64]{2,1,0:T(1,128)S(1)}, f32[1,1,64]{2,1,0:T(1,128)}, u32[]{:S(2)}) copy-start(f32[1,1,64]{2,1,0:T(1,128)} %param.15) | copy-start | bytes 772
  10.2 0.7 %copy-start.15 = (f32[1,1,64]{2,1,0:T(1,128)S(1)}, f32[1,1,64]{2,1,0:T(1,128)}, u32[]{:S(2)}) copy-start(f32[1,1,64]{2,1,0:T(1,128)} %param.14) | copy-start | bytes 772
  11.2 8.3 %copy-start.16 = (s32[1,1,4]{2,1,0:T(1,128)S(1)}, s32[1,1,4]{2,1,0:T(1,128)}, u32[]{:S(2)}) copy-start(s32[1,1,4]{2,1,0:T(1,128)} %param.12) | copy-start | bytes 52
  14.0 11.4 %copy-start.3 = (bf16[80,1024]{1,0:T(8,128)(2,1)}, bf16[80,1024]{1,0:T(8,128)(2,1)S(1)}, u32[]{:S(2)}) copy-start(bf16[80,1024]{1,0:T(8,128)(2,1)S(1)} %collective-permute-done.1.refs_2_) | copy-start | bytes 491524
  14.0 6.1 %collective-permute-start.7 = (bf16[80,1024]{1,0:T(8,128)(2,1)S(1)}, bf16[80,1024]{1,0:T(8,128)(2,1)S(1)}, u32[]{:S(2)}, u32[]{:S(2)}) collective-permute-start(bf16[80,1024]{1,0:T(8,128)(2,1)S(1)} %collective-permute-done.1.refs_2_), channel_id=1, source_target_pairs={{0,112},{16,32},{32,16},{48,64},{64,48},{80,96},{96,80},{112,0},{1... | collective-permute-start | bytes 491528 | tf_op jit(solution)/shard_map/ppermute | solution.py:39
  14.0 6.1 %collective-permute-start.4 = (bf16[80,1024]{1,0:T(8,128)(2,1)S(1)}, bf16[80,1024]{1,0:T(8,128)(2,1)S(1)}, u32[]{:S(2)}, u32[]{:S(2)}) collective-permute-start(bf16[80,1024]{1,0:T(8,128)(2,1)S(1)} %collective-permute-done.1.refs_2_), channel_id=1, source_target_pairs={{0,16},{16,0},{32,48},{48,32},{64,80},{80,64},{96,112},{112,96},{1... | collective-permute-start | bytes 491528 | tf_op jit(solution)/shard_map/ppermute | solution.py:39
  19.4 6.0 %copy-start.4 = (bf16[80,1024]{1,0:T(8,128)(2,1)}, bf16[80,1024]{1,0:T(8,128)(2,1)S(1)}, u32[]{:S(2)}) copy-start(bf16[80,1024]{1,0:T(8,128)(2,1)S(1)} %collective-permute-done.refs_1_) | copy-start | bytes 491524
  19.4 6.0 %collective-permute-start.6 = (bf16[80,1024]{1,0:T(8,128)(2,1)S(1)}, bf16[80,1024]{1,0:T(8,128)(2,1)S(1)}, u32[]{:S(2)}, u32[]{:S(2)}) collective-permute-start(bf16[80,1024]{1,0:T(8,128)(2,1)S(1)} %collective-permute-done.refs_1_), channel_id=1, source_target_pairs={{0,112},{16,32},{32,16},{48,64},{64,48},{80,96},{96,80},{112,0},{1... | collective-permute-start | bytes 491528 | tf_op jit(solution)/shard_map/ppermute | solution.py:39
  19.4 6.0 %copy-start.1 = (bf16[80,1024]{1,0:T(8,128)(2,1)}, bf16[80,1024]{1,0:T(8,128)(2,1)S(1)}, u32[]{:S(2)}) copy-start(bf16[80,1024]{1,0:T(8,128)(2,1)S(1)} %collective-permute-done.5.refs_6_) | copy-start | bytes 491524
  19.4 5.9 %collective-permute-start.3 = (bf16[80,1024]{1,0:T(8,128)(2,1)S(1)}, bf16[80,1024]{1,0:T(8,128)(2,1)S(1)}, u32[]{:S(2)}, u32[]{:S(2)}) collective-permute-start(bf16[80,1024]{1,0:T(8,128)(2,1)S(1)} %collective-permute-done.refs_1_), channel_id=1, source_target_pairs={{0,16},{16,0},{32,48},{48,32},{64,80},{80,64},{96,112},{112,96},{1... | collective-permute-start | bytes 491528 | tf_op jit(solution)/shard_map/ppermute | solution.py:39
  20.0 5.3 %copy-start.2 = (bf16[80,1024]{1,0:T(8,128)(2,1)}, bf16[80,1024]{1,0:T(8,128)(2,1)S(1)}, u32[]{:S(2)}) copy-start(bf16[80,1024]{1,0:T(8,128)(2,1)S(1)} %collective-permute-done.2.refs_3_) | copy-start | bytes 491524
  20.0 5.3 %copy-start.5 = (bf16[80,1024]{1,0:T(8,128)(2,1)}, bf16[80,1024]{1,0:T(8,128)(2,1)S(1)}, u32[]{:S(2)}) copy-start(bf16[80,1024]{1,0:T(8,128)(2,1)S(1)} %collective-permute-done.7.refs_8_) | copy-start | bytes 491524
  20.1 5.3 %copy-start.6 = (bf16[80,1024]{1,0:T(8,128)(2,1)}, bf16[80,1024]{1,0:T(8,128)(2,1)S(1)}, u32[]{:S(2)}) copy-start(bf16[80,1024]{1,0:T(8,128)(2,1)S(1)} %collective-permute-done.4.refs_5_) | copy-start | bytes 491524
  25.3 0.7 %copy-start.7 = (bf16[80,1024]{1,0:T(8,128)(2,1)}, bf16[80,1024]{1,0:T(8,128)(2,1)S(1)}, u32[]{:S(2)}) copy-start(bf16[80,1024]{1,0:T(8,128)(2,1)S(1)} %collective-permute-done.6.refs_7_) | copy-start | bytes 491524
  25.3 0.7 %copy-start.8 = (bf16[80,1024]{1,0:T(8,128)(2,1)}, bf16[80,1024]{1,0:T(8,128)(2,1)S(1)}, u32[]{:S(2)}) copy-start(bf16[80,1024]{1,0:T(8,128)(2,1)S(1)} %collective-permute-done.3.refs_4_) | copy-start | bytes 491524
  26.1 18.8 %copy-start = (f32[1,1,80,12,128]{4,2,3,1,0:T(8,128)S(1)}, f32[1,1,80,12,128]{4,2,3,1,0:T(8,128)}, u32[]{:S(2)}) copy-start(f32[1,1,80,12,128]{4,2,3,1,0:T(8,128)} %param.9) | copy-start | bytes 1474564
  29.5 4.2 %collective-permute-start.9 = (f32[80,128]{1,0:T(8,128)}, f32[80,128]{1,0:T(8,128)S(1)}, u32[]{:S(2)}, u32[]{:S(2)}) collective-permute-start(f32[80,128]{1,0:T(8,128)} %get-tuple-element.11), channel_id=1, source_target_pairs={{0,15},{1,0},{2,1},{3,2},{4,3},{5,4},{6,5},{7,6},{8,7},{9,8},{10,9... | collective-permute-start | bytes 122888 | tf_op jit(solution)/shard_map/ppermute | solution.py:30
  31.5 7.5 %collective-permute-start.8 = (f32[80,128]{1,0:T(8,128)}, f32[80,128]{1,0:T(8,128)S(1)}, u32[]{:S(2)}, u32[]{:S(2)}) collective-permute-start(f32[80,128]{1,0:T(8,128)} %get-tuple-element.11), channel_id=1, source_target_pairs={{0,1},{1,2},{2,3},{3,4},{4,5},{5,6},{6,7},{7,8},{8,9},{9,10},{10,1... | collective-permute-start | bytes 122888 | tf_op jit(solution)/shard_map/ppermute | solution.py:30
  33.7 5.4 %copy-start.9 = (f32[80,128]{1,0:T(8,128)}, f32[80,128]{1,0:T(8,128)S(1)}, u32[]{:S(2)}) copy-start(f32[80,128]{1,0:T(8,128)S(1)} %collective-permute-done.9.after_ref) | copy-start | bytes 122884
  39.0 0.6 %copy-start.10 = (f32[80,128]{1,0:T(8,128)}, f32[80,128]{1,0:T(8,128)S(1)}, u32[]{:S(2)}) copy-start(f32[80,128]{1,0:T(8,128)S(1)} %collective-permute-done.8.before_ref) | copy-start | bytes 122884
  41.2 6.8 %collective-permute-start.10 = (f32[80,128]{1,0:T(8,128)}, f32[80,128]{1,0:T(8,128)S(1)}, u32[]{:S(2)}, u32[]{:S(2)}) collective-permute-start(f32[80,128]{1,0:T(8,128)} %get-tuple-element.12), channel_id=1, source_target_pairs={{0,16},{16,32},{32,48},{48,64},{64,80},{80,96},{96,112},{112,0},{1... | collective-permute-start | bytes 122888 | tf_op jit(solution)/shard_map/ppermute | solution.py:30
  41.2 6.8 %collective-permute-start.11 = (f32[80,128]{1,0:T(8,128)}, f32[80,128]{1,0:T(8,128)S(1)}, u32[]{:S(2)}, u32[]{:S(2)}) collective-permute-start(f32[80,128]{1,0:T(8,128)} %get-tuple-element.13), channel_id=1, source_target_pairs={{0,112},{16,0},{32,16},{48,32},{64,48},{80,64},{96,80},{112,96},{1... | collective-permute-start | bytes 122888 | tf_op jit(solution)/shard_map/ppermute | solution.py:30
  48.1 0.6 %copy-start.11 = (f32[80,128]{1,0:T(8,128)}, f32[80,128]{1,0:T(8,128)S(1)}, u32[]{:S(2)}) copy-start(f32[80,128]{1,0:T(8,128)S(1)} %collective-permute-done.10.west_ref) | copy-start | bytes 122884
  48.1 0.6 %copy-start.12 = (f32[80,128]{1,0:T(8,128)}, f32[80,128]{1,0:T(8,128)S(1)}, u32[]{:S(2)}) copy-start(f32[80,128]{1,0:T(8,128)S(1)} %collective-permute-done.11.east_ref) | copy-start | bytes 122884

commit v2 on v1

v2 whole, which is shorter than its diff:
```python
import functools

import jax
import jax.numpy as jnp
from jax import lax
from jax.experimental import pallas as pl
from jax.experimental.pallas import tpu as pltpu
from jax.sharding import PartitionSpec as P

MEM = 80
AX = 8
AY = 16
OCN_DEV = 1024
OB = 32
NB = 2
K = 4
FIELDS = 12
COMP = 13
CELLS = 128
OBS_DEV = 64

f32 = jnp.float32
META = 4
TAPER = {0: 1.0, 1: 0.5625, 2: 0.25}
OFFSETS = [(dx, dy) for dx in (-1, 0, 1) for dy in (-1, 0, 1)]


def ring(block, axis, step):
    count = lax.axis_size(axis)
    return lax.ppermute(block, axis, [(i, (i + step) % count) for i in range(count)])


def swap(block, axis, first):
    count = lax.axis_size(axis)
    pairs = []
    for at in range(first, count + first, 2):
        low, high = at % count, (at + 1) % count
        pairs += [(low, high), (high, low)]
    return lax.ppermute(block, axis, sorted(pairs))


def lanes(rows=1):
    return lax.broadcasted_iota(jnp.int32, (rows, CELLS), 1)


def prepare_kernel(
    atm_hbm, weight_hbm, order_ref, cell_ref, live_ref, value_ref, error_ref,
    weight_ref, anom_ref, mean_ref, meta_ref, sem_ref,
):
    weights = pltpu.make_async_copy(weight_hbm, weight_ref, sem_ref.at[0])
    fields = pltpu.make_async_copy(atm_hbm, anom_ref, sem_ref.at[1])
    fields.start()
    weights.start()
    order = jnp.transpose(jnp.broadcast_to(order_ref[...], (OBS_DEV, OBS_DEV)))
    taken = order == lax.broadcasted_iota(jnp.int32, (OBS_DEV, OBS_DEV), 1)
    lane = lanes(OBS_DEV)

    def ordered(row):
        picked = jnp.sum(jnp.where(taken, row, 0.0), axis=1, keepdims=True)
        return jnp.broadcast_to(picked, (OBS_DEV, CELLS))

    cell = jnp.where(live_ref[...] > 0, cell_ref[...], -1).astype(f32)
    meta_ref[...] = jnp.zeros_like(meta_ref)
    meta_ref[0:OBS_DEV, :] = jnp.where(
        lane == META,
        ordered(cell),
        jnp.where(lane == META + 1, ordered(value_ref[...]), ordered(error_ref[...])),
    )
    fields.wait()
    mean_ref[...] = jnp.zeros_like(mean_ref)
    for v in range(FIELDS):
        field = anom_ref[v]
        mean = jnp.sum(field, axis=0, keepdims=True) / MEM
        mean_ref[v : v + 1, :] = mean
        anom_ref[v] = field - mean
    weights.wait()


def remap_kernel(sel_ref, meta_ref, w_ref, *refs):
    tiles, (state_ref, message_ref) = refs[:9], refs[9:]
    state_ref[...] = jnp.zeros_like(state_ref)

    def one(k, carry):
        for index, tile in enumerate(tiles):

            @pl.when(sel_ref[k] == index)
            def _():
                state_ref[...] += jnp.dot(tile[...], w_ref[k], preferred_element_type=f32)

        return carry

    lax.fori_loop(0, K, one, 0)
    lane = lanes()
    message_ref[...] = jnp.where(
        (lane >= META) & (lane < META + 3), meta_ref[...], state_ref[...]
    )


def side_kernel(meta_ref, state_ref, before_ref, after_ref, right_ref, left_ref):
    lane = lanes()
    state = state_ref[...]
    before = before_ref[...]
    after = after_ref[...]
    columns = jnp.where(lane % AY >= 8, before, after)
    turned = pltpu.roll(columns, 64, 1)
    right = jnp.where(lane >= 64, state, turned)
    left = jnp.where(lane < 64, state, turned)
    meta = meta_ref[...]

    def put(block, start, record, shift):
        moved = pltpu.roll(record, shift, 1) if shift else record
        return jnp.where((lane >= start) & (lane < start + 3), moved, block)

    for n, record in enumerate((meta, before, after)):
        right = put(right, META + 3 * n, record, 3 * n)
        left = put(left, 32 + META + 3 * n, record, 32 + 3 * n)
    right_ref[...] = right
    left_ref[...] = left


def views(blocks):
    lane = lanes()
    y = lane % AY
    x = lane // AY
    m0, m1, h0, h1 = blocks

    def up(a, b):
        return jnp.where(y == 15, pltpu.roll(b, 15, 1), pltpu.roll(a, 127, 1))

    def down(a, b):
        return jnp.where(y == 0, pltpu.roll(b, 113, 1), pltpu.roll(a, 1, 1))

    rows = {
        0: blocks,
        1: (up(m0, h0), up(m1, h1), up(h0, m0), up(h1, m1)),
        -1: (down(m0, h0), down(m1, h1), down(h0, m0), down(h1, m1)),
    }
    out = {}
    for dy, (a0, a1, b0, b1) in rows.items():
        out[0, dy] = (a0, a1, b0, b1)
        for dx, edge, shift in ((1, 0, 112), (-1, 7, 16)):

            def pair(u, v):
                return (
                    pltpu.roll(jnp.where(x == edge, v, u), shift, 1),
                    pltpu.roll(jnp.where(x == edge, u, v), shift, 1),
                )

            out[dx, dy] = pair(a0, a1) + pair(b0, b1)
    return out


def own_views(blocks):
    lane = lanes()
    y = lane % AY
    x = lane // AY
    m0, m1, h0, h1 = blocks
    rows = {0: (m0, m1), 1: [], -1: []}
    for a, b in ((m0, h0), (m1, h1)):
        rows[1].append(jnp.where(y == 15, pltpu.roll(b, 15, 1), pltpu.roll(a, 127, 1)))
        rows[-1].append(jnp.where(y == 0, pltpu.roll(b, 113, 1), pltpu.roll(a, 1, 1)))
    out = {}
    for dy, (u, v) in rows.items():
        out[0, dy] = u
        out[1, dy] = pltpu.roll(jnp.where(x == 0, v, u), 112, 1)
        out[-1, dy] = pltpu.roll(jnp.where(x == 7, v, u), 16, 1)
    return out


ROWS = MEM // 8


def group(r):
    return pl.ds(pl.multiple_of(r * 8, 8), 8)


def total(block):
    return jnp.sum(block, axis=0, keepdims=True)


def analysis_kernel(
    meta_ref, state_ref, before_ref, after_ref, west_ref, east_ref, mean_ref, anom_ref,
    post_mean_hbm, post_anom_hbm,
    field_ref, moved_ref, first_ref, second_ref, out_ref, out_mean_ref, sem_ref,
):
    lane = lanes()
    y = lane % AY
    low_x = lane < 64
    high_y = y >= 8
    at_x, at_y = lax.axis_index("gx"), lax.axis_index("gy")
    has_west = (at_x > 0).astype(jnp.int32)
    has_east = (at_x < lax.axis_size("gx") - 1).astype(jnp.int32)
    has_before = (at_y > 0).astype(jnp.int32)
    has_after = (at_y < lax.axis_size("gy") - 1).astype(jnp.int32)
    west = west_ref[...]
    east = east_ref[...]
    fields = [
        state_ref[...],
        jnp.where(low_x, east, west),
        jnp.where(high_y, before_ref[...], after_ref[...]),
        pltpu.roll(jnp.where(low_x, west, east), 64, 1),
    ]
    means = [total(field) / MEM for field in fields]
    squares = []
    for block in range(4):
        anom = fields[block] - means[block]
        field_ref[block] = anom
        squares.append(total(anom * anom))
    side_x = jnp.where(low_x, has_east, has_west)
    side_y = jnp.where(high_y, has_before, has_after)
    open_lane = [jnp.ones_like(side_x), side_x, side_y, side_x * side_y]

    def weights(batch, squares, means):
        rows = pl.ds(batch * OB, OB)

        def column(ref, at):
            return jnp.broadcast_to(ref[rows, at : at + 1], (OB, CELLS))

        def record(block, n):
            if block == 0:
                return column(meta_ref, META + n)
            if block == 1:
                return jnp.where(
                    low_x, column(east_ref, 32 + META + n), column(west_ref, META + n)
                )
            if block == 2:
                return jnp.where(
                    high_y, column(before_ref, META + n), column(after_ref, META + n)
                )
            return jnp.where(
                low_x,
                jnp.where(
                    high_y,
                    column(east_ref, 32 + META + 3 + n),
                    column(east_ref, 32 + META + 6 + n),
                ),
                jnp.where(
                    high_y, column(west_ref, META + 3 + n), column(west_ref, META + 6 + n)
                ),
            )

        pulls, damped = [], []
        for block in range(4):
            variance = squares[block] / (MEM - 1)
            here = (record(block, 0) == lane.astype(f32)) & (open_lane[block] > 0)
            error = record(block, 2)
            denominator = variance + error
            pull = (record(block, 1) - means[block]) / denominator
            damp = 1.0 / (denominator + jnp.sqrt(error * denominator))
            pulls.append(total(jnp.where(here, pull, 0.0)))
            damped.append(total(jnp.where(here, damp, 0.0)))
        return pulls, damped

    def spread(rows):
        return [jnp.broadcast_to(row, (8, CELLS)) for row in rows]

    def scale(key):
        return TAPER[key[0] ** 2 + key[1] ** 2] / (MEM - 1)

    zero = jnp.zeros((8, CELLS), f32)

    pulls, damped = weights(0, squares, means)
    pull_views = views(spread(pulls))
    damp_views = views(spread(damped))

    def shift_first(r, sums):
        at = group(r)
        blocks = [field_ref[block, at, :] for block in range(4)]
        shifted = views(blocks)
        out = []
        for n, key in enumerate(OFFSETS):
            for block in range(4):
                first_ref[block, n, at, :] = shifted[key][block]
                out.append(sums[n * 4 + block] + shifted[key][block] * blocks[block])
        return tuple(out)

    sums = lax.fori_loop(0, ROWS, shift_first, (zero,) * 36)
    next_means, next_squares = [], []
    for block in range(4):
        step = jnp.zeros_like(means[block])
        gains = []
        for n, key in enumerate(OFFSETS):
            covariance = total(sums[n * 4 + block]) * scale(key)
            step = step + covariance * pull_views[key][block][0:1]
            gains.append(covariance * damp_views[key][block][0:1])
        square = zero
        for r in range(ROWS):
            at = slice(8 * r, 8 * r + 8)
            moved = field_ref[block, at, :]
            for n in range(9):
                moved = moved - gains[n] * first_ref[block, n, at, :]
            moved_ref[block, at, :] = moved
            square = square + moved * moved
        next_means.append(means[block] + step)
        next_squares.append(total(square))
    next_pulls, next_damped = weights(1, next_squares, next_means)
    next_pull_views = own_views(spread(next_pulls))
    next_damp_views = own_views(spread(next_damped))

    def shift_second(r, sums):
        at = group(r)
        blocks = [moved_ref[block, at, :] for block in range(4)]
        shifted = own_views(blocks)
        out = []
        for n, key in enumerate(OFFSETS):
            second_ref[n, at, :] = shifted[key]
            out.append(sums[n] + shifted[key] * blocks[0])
        return tuple(out)

    sums = lax.fori_loop(0, ROWS, shift_second, (zero,) * 9)

    def finish(sums, mean):
        gains = []
        for n, key in enumerate(OFFSETS):
            covariance = total(sums[n]) * scale(key)
            mean = mean + covariance * next_pull_views[key][0:1]
            gains.append(covariance * next_damp_views[key][0:1])
        return gains, mean

    gains, mean = finish(sums, next_means[0])
    out_mean_ref[FIELDS] = mean
    for r in range(ROWS):
        at = slice(8 * r, 8 * r + 8)
        block = moved_ref[0, at, :]
        for n in range(9):
            block = block - gains[n] * second_ref[n, at, :]
        out_ref[FIELDS, at, :] = block

    def send(v, count):
        return pltpu.make_async_copy(
            out_ref.at[pl.ds(v, count)], post_anom_hbm.at[pl.ds(v, count)], sem_ref.at[0]
        )

    def pair(g, carry):
        comps = [2 * g, 2 * g + 1]
        sums = [[zero] * 9, [zero] * 9]
        for r in range(ROWS):
            at = slice(8 * r, 8 * r + 8)
            shifted = [first_ref[0, n, at, :] for n in range(9)]
            for i, v in enumerate(comps):
                block = anom_ref[v, at, :]
                sums[i] = [s + block * w for s, w in zip(sums[i], shifted)]
        means, gains = [], []
        for i, v in enumerate(comps):
            mean = mean_ref[pl.ds(v, 1), :]
            own = []
            for n, key in enumerate(OFFSETS):
                covariance = total(sums[i][n]) * scale(key)
                mean = mean + covariance * pull_views[key][0][0:1]
                own.append(covariance * damp_views[key][0][0:1])
            means.append(mean)
            gains.append(own)
        sums = [[zero] * 9, [zero] * 9]
        for r in range(ROWS):
            at = slice(8 * r, 8 * r + 8)
            shifted = [first_ref[0, n, at, :] for n in range(9)]
            later = [second_ref[n, at, :] for n in range(9)]
            for i, v in enumerate(comps):
                block = anom_ref[v, at, :]
                for n in range(9):
                    block = block - gains[i][n] * shifted[n]
                out_ref[v, at, :] = block
                sums[i] = [s + block * w for s, w in zip(sums[i], later)]
        for i, v in enumerate(comps):
            gains[i], mean = finish(sums[i], means[i])
            out_mean_ref[v] = mean
        for r in range(ROWS):
            at = slice(8 * r, 8 * r + 8)
            later = [second_ref[n, at, :] for n in range(9)]
            for i, v in enumerate(comps):
                block = out_ref[v, at, :]
                for n in range(9):
                    block = block - gains[i][n] * later[n]
                out_ref[v, at, :] = block
        send(2 * g, 2).start()
        return carry

    send(FIELDS, 1).start()
    lax.fori_loop(0, FIELDS // 2, pair, 0)
    last = pltpu.make_async_copy(out_mean_ref, post_mean_hbm, sem_ref.at[1])
    last.start()
    pltpu.make_async_copy(out_ref, post_anom_hbm, sem_ref.at[0]).wait()
    last.wait()


VMEM = pl.BlockSpec(memory_space=pltpu.VMEM)
SMEM = pl.BlockSpec(memory_space=pltpu.SMEM)
ANY = pl.BlockSpec(memory_space=pl.ANY)
LIMIT = pltpu.CompilerParams(vmem_limit_bytes=8 << 20)


def flat(*shape):
    return jax.ShapeDtypeStruct(shape, f32)


def local(
    atm_members,
    ocean_members,
    remap_weights,
    pair_src,
    obs_cell,
    obs_value,
    obs_error,
    obs_live,
    obs_order,
):
    at_x = lax.axis_index("gx")
    at_y = lax.axis_index("gy")
    rows = lax.axis_size("gy")
    own = ocean_members[0, 0]
    before = ring(own, "gy", 1)
    after = ring(own, "gy", -1)
    tiles = [own, before, after]
    for first in (0, 1):
        tiles += [swap(tile, "gx", first) for tile in (own, before, after)]
    source = pair_src[0, 0]
    step_x = source // rows - at_x
    step_y = source % rows - at_y
    side = jnp.where(step_x == 0, 0, jnp.where((step_x == 1) == (at_x % 2 == 0), 1, 2))
    select = side * 3 + jnp.where(step_y == 0, 0, jnp.where(step_y < 0, 1, 2))

    weights, anomaly, mean, meta = pl.pallas_call(
        prepare_kernel,
        in_specs=[ANY, ANY] + [VMEM] * 5,
        out_specs=[VMEM] * 4,
        out_shape=[
            jax.ShapeDtypeStruct((K, OCN_DEV, CELLS), jnp.bfloat16),
            flat(FIELDS, MEM, CELLS),
            flat(16, CELLS),
            flat(MEM, CELLS),
        ],
        scratch_shapes=[pltpu.SemaphoreType.DMA((2,))],
        name="prepare",
        compiler_params=LIMIT,
    )(
        jnp.transpose(atm_members[0, 0], (1, 0, 2)),
        remap_weights[0, 0],
        obs_order[0],
        obs_cell[0],
        obs_live[0],
        obs_value[0],
        obs_error[0],
    )
    state, message = pl.pallas_call(
        remap_kernel,
        in_specs=[SMEM, VMEM, VMEM] + [VMEM] * 9,
        out_specs=[VMEM, VMEM],
        out_shape=[flat(MEM, CELLS), flat(MEM, CELLS)],
        name="remap",
        compiler_params=LIMIT,
    )(select, meta, weights, *tiles)
    from_before = ring(message, "gy", 1)
    from_after = ring(message, "gy", -1)
    to_right, to_left = pl.pallas_call(
        side_kernel,
        in_specs=[VMEM] * 4,
        out_specs=[VMEM, VMEM],
        out_shape=[flat(MEM, CELLS), flat(MEM, CELLS)],
        name="side",
        compiler_params=LIMIT,
    )(meta, state, from_before, from_after)
    from_west = ring(to_right, "gx", 1)
    from_east = ring(to_left, "gx", -1)
    post_mean, post_anom = pl.pallas_call(
        analysis_kernel,
        in_specs=[VMEM] * 8,
        out_specs=[ANY, ANY],
        out_shape=[flat(COMP, 1, CELLS), flat(COMP, MEM, CELLS)],
        scratch_shapes=[
            pltpu.VMEM((4, MEM, CELLS), f32),
            pltpu.VMEM((4, MEM, CELLS), f32),
            pltpu.VMEM((4, 9, MEM, CELLS), f32),
            pltpu.VMEM((9, MEM, CELLS), f32),
            pltpu.VMEM((COMP, MEM, CELLS), f32),
            pltpu.VMEM((COMP, 1, CELLS), f32),
            pltpu.SemaphoreType.DMA((2,)),
        ],
        name="analysis",
        compiler_params=LIMIT,
    )(meta, state, from_before, from_after, from_west, from_east, mean, anomaly)
    post_mean = jnp.transpose(post_mean, (1, 0, 2))
    post_anom = jnp.transpose(post_anom, (1, 0, 2))
    return post_mean[None], post_anom[None, None]


def solution(mesh):
    in_specs = (
        P("gx", "gy", None, None, None),
        P("gx", "gy", None, None),
        P("gx", "gy", None, None, None),
        P("gx", "gy", None),
        P("gx", "gy", None),
        P("gx", "gy", None),
        P("gx", "gy", None),
        P("gx", "gy", None),
        P("gx", "gy", None),
    )
    out_specs = (P("gx", "gy", None, None), P("gx", "gy", None, None, None))
    return jax.shard_map(local, mesh=mesh, in_specs=in_specs, out_specs=out_specs, check_vma=False)
```

time: 58.8 us -> 45.8 us (0.78)
  waiting for transfers between devices: 20.2 us -> 13.9 us
  starting transfers between devices: 14 us -> 19.6 us
  local copies, waits for them, and re-layouts: 8.27 us -> 2.96 us
  Pallas kernels: 13.5 us -> 8.46 us
  other arithmetic: 1.51 us -> 0.02 us
    unnamed x41 -> x18, local copies, waits for them, and re-layouts: 7.65 us -> 2.96 us
    ppermute x6, waiting for transfers between devices: 15 us -> 10.3 us  [ring(): lax.ppermute(block, axis, [(i, (i + step) % count) for i in range(count)])]
    ppermute x6, starting transfers between devices: 10.2 us -> 13 us  [ring(): lax.ppermute(block, axis, [(i, (i + step) % count) for i in range(count)])]
    ppermute x6, starting transfers between devices: 3.84 us -> 6.58 us  [swap(): return lax.ppermute(block, axis, sorted(pairs))]
    pallas_call x1, Pallas kernels: 3.4 us -> 1.59 us  [local(): pl.pallas_call(remap_kernel, in_specs=[SMEM, VMEM, VMEM] + [VMEM] * 9, ou...]
    pallas_call x2, Pallas kernels: 8.51 us -> 6.74 us  [the longest x1 6.1 us: local(): pl.pallas_call(analysis_kernel, in_specs=[VMEM] * 8, out_specs=[ANY, ANY]...]
    ppermute x6, waiting for transfers between devices: 5.28 us -> 3.57 us  [swap(): return lax.ppermute(block, axis, sorted(pairs))]
    pallas_call x1, Pallas kernels: 1.6 us -> 0.13 us  [local(): pl.pallas_call(side_kernel, in_specs=[VMEM] * 4, out_specs=[VMEM, VMEM],...]
  transfers between devices with their start and end apart: 12 -> 12, of which waited for: 5 -> 6; matrix products, arithmetic and copies ran while one was open for 5% -> 0% of each run, Pallas kernels for 4% -> 1%
where the time goes in v2:
time: 45.8 us; the launch traced here: 45.6 us
  starting transfers between devices  19.6 us (43%)
  waiting for transfers between devices  13.9 us (30%)
  Pallas kernels  8.46 us (18%)
  local copies, waits for them, and re-layouts  2.96 us (6%)
  between operations  0.72 us (2%)
    ppermute x6, starting transfers between devices, ring(): lax.ppermute(block, axis, [(i, (i + step) % count) for i in range(count)])  13 us
    ppermute x6, waiting for transfers between devices, ring(): lax.ppermute(block, axis, [(i, (i + step) % count) for i in range(count)])  10.3 us
    ppermute x6, starting transfers between devices, swap(): return lax.ppermute(block, axis, sorted(pairs))  6.58 us
    pallas_call x1, Pallas kernels, local(): pl.pallas_call(analysis_kernel, in_specs=[VMEM] * 8, out_specs=[ANY, ANY]...  6.1 us
    ppermute x6, waiting for transfers between devices, swap(): return lax.ppermute(block, axis, sorted(pairs))  3.57 us
    unnamed x18, local copies, waits for them, and re-layouts  2.96 us
    pallas_call x1, Pallas kernels, local(): pl.pallas_call(remap_kernel, in_specs=[SMEM, VMEM, VMEM] + [VMEM] * 9, ou...  1.59 us
  transfers between devices with their start and end apart: 12, of which 6 were waited for; matrix products, arithmetic and copies ran while one was open for 0% of the time, Pallas kernels for 1%

profile of v2, /device:TPU:0, one launch (start us, length us, event | category | flops | bytes accessed | tf_op | source)
XLA Modules:
  0.0 45.6 jit_solution(6388609788298110373)
XLA Ops:
  0.6 5.4 %collective-permute-start.1 = (bf16[80,1024]{1,0:T(8,128)(2,1)}, bf16[80,1024]{1,0:T(8,128)(2,1)S(1)}, u32[]{:S(2)}, u32[]{:S(2)}) collective-permute-start(bf16[80,1024]{1,0:T(8,128)(2,1)} %bitcast.31), channel_id=1, source_target_pairs={{0,15},{1,0},{2,1},{3,2},{4,3},{5,4},{6,5},{7,6},{8,7},{9,8},{10,9... | collective-permute-start | bytes 491528 | tf_op jit(solution)/shard_map/ppermute | solution.py:30
  6.0 0.0 collective-permute-start
  6.0 3.2 %collective-permute-start.5 = (bf16[80,1024]{1,0:T(8,128)(2,1)}, bf16[80,1024]{1,0:T(8,128)(2,1)S(1)}, u32[]{:S(2)}, u32[]{:S(2)}) collective-permute-start(bf16[80,1024]{1,0:T(8,128)(2,1)} %bitcast.33), channel_id=1, source_target_pairs={{0,112},{16,32},{32,16},{48,64},{64,48},{80,96},{96,80},{112,0},{1... | collective-permute-start | bytes 491528 | tf_op jit(solution)/shard_map/ppermute | solution.py:39
  9.2 0.0 collective-permute-start.2
  9.2 0.0 copy-start.6
  9.2 0.0 copy-start.7
  9.2 0.0 copy-start.3
  9.2 0.0 copy-start.4
  9.2 0.0 copy-start.5
  9.3 0.6 %copy-done.6 = f32[1,1,64]{2,1,0:T(1,128)S(1)} copy-done((f32[1,1,64]{2,1,0:T(1,128)S(1)}, f32[1,1,64]{2,1,0:T(1,128)}, u32[]{:S(2)}) %copy-start.6) | copy-done | bytes 280
  9.9 0.0 copy-done.7
  9.9 0.0 copy-done.3
  9.9 0.0 copy-done.4
  9.9 0.0 copy-done.5
  9.9 0.0 copy-start
  9.9 1.2 %copy-done = bf16[1,1,4,1024,128]{4,3,2,1,0:T(8,128)(2,1)S(1)} copy-done((bf16[1,1,4,1024,128]{4,3,2,1,0:T(8,128)(2,1)S(1)}, bf16[1,1,4,1024,128]{4,3,2,1,0:T(8,128)(2,1)}, u32[]{:S(2)}) %copy-start) | copy-done | bytes 1048600
  11.2 0.0 copy-start.1
  11.2 1.0 %copy-done.1 = f32[1,1,80,12,128]{4,2,3,1,0:T(8,128)S(1)} copy-done((f32[1,1,80,12,128]{4,2,3,1,0:T(8,128)S(1)}, f32[1,1,80,12,128]{4,2,3,1,0:T(8,128)}, u32[]{:S(2)}) %copy-start.1) | copy-done | bytes 491544
  12.2 0.0 copy-start.8
  12.2 0.0 copy-start.2
  12.2 0.6 %prepare.1 = (bf16[4,1024,128]{2,1,0:T(8,128)(2,1)S(1)}, f32[12,80,128]{2,1,0:T(8,128)S(1)}, f32[16,128]{1,0:T(8,128)S(1)}, f32[80,128]{1,0:T(8,128)S(1)}) custom-call(f32[12,80,128]{2,1,0:T(8,128)S(1)} %bitcast.30, bf16[4,1024,128]{2,1,0:T(8,128)(2,1)S(1)} %bitcast.29, s32[1,64]{1,0:T(1,128)S(1)} %bitcast.36, s32[1,64]{1,0:T(1,128)S(1)} %bitcast.37, ...), custom_call_target="tpu_custom_call" | custom-call | tf_op jit(solution)/shard_map/prepare/pallas_call | solution.py:422
  12.9 0.0 collective-permute-done.1.refs_2_
  12.9 1.0 %collective-permute-start.7 = (bf16[80,1024]{1,0:T(8,128)(2,1)S(1)}, bf16[80,1024]{1,0:T(8,128)(2,1)S(1)}, u32[]{:S(2)}, u32[]{:S(2)}) collective-permute-start(bf16[80,1024]{1,0:T(8,128)(2,1)S(1)} %collective-permute-done.1.refs_2_), channel_id=1, source_target_pairs={{0,112},{16,32},{32,16},{48,64},{64,48},{80,96},{96,80},{112,0},{1... | collective-permute-start | bytes 491528 | tf_op jit(solution)/shard_map/ppermute | solution.py:39
  13.9 0.0 collective-permute-start.4
  13.9 1.3 %collective-permute-done.refs_1_ = bf16[80,1024]{1,0:T(8,128)(2,1)S(1)} collective-permute-done((bf16[80,1024]{1,0:T(8,128)(2,1)}, bf16[80,1024]{1,0:T(8,128)(2,1)S(1)}, u32[]{:S(2)}, u32[]{:S(2)}) %collective-permute-start) | collective-permute-done | bytes 163872 | tf_op jit(solution)/shard_map/ppermute | solution.py:30
  15.2 2.3 %collective-permute-start.6 = (bf16[80,1024]{1,0:T(8,128)(2,1)S(1)}, bf16[80,1024]{1,0:T(8,128)(2,1)S(1)}, u32[]{:S(2)}, u32[]{:S(2)}) collective-permute-start(bf16[80,1024]{1,0:T(8,128)(2,1)S(1)} %collective-permute-done.refs_1_), channel_id=1, source_target_pairs={{0,112},{16,32},{32,16},{48,64},{64,48},{80,96},{96,80},{112,0},{1... | collective-permute-start | bytes 491528 | tf_op jit(solution)/shard_map/ppermute | solution.py:39
  17.6 0.0 collective-permute-done.5.refs_6_
  17.6 0.0 collective-permute-start.3
  17.6 0.0 copy-done.8
  17.6 0.0 collective-permute-done.2.refs_3_
  17.6 1.3 %collective-permute-done.7.refs_8_ = bf16[80,1024]{1,0:T(8,128)(2,1)S(1)} collective-permute-done((bf16[80,1024]{1,0:T(8,128)(2,1)S(1)}, bf16[80,1024]{1,0:T(8,128)(2,1)S(1)}, u32[]{:S(2)}, u32[]{:S(2)}) %collective-permute-start.7) | collective-permute-done | bytes 163872 | tf_op jit(solution)/shard_map/ppermute | solution.py:39
  18.9 0.0 collective-permute-done.4.refs_5_
  18.9 2.3 %collective-permute-done.6.refs_7_ = bf16[80,1024]{1,0:T(8,128)(2,1)S(1)} collective-permute-done((bf16[80,1024]{1,0:T(8,128)(2,1)S(1)}, bf16[80,1024]{1,0:T(8,128)(2,1)S(1)}, u32[]{:S(2)}, u32[]{:S(2)}) %collective-permute-start.6) | collective-permute-done | bytes 163872 | tf_op jit(solution)/shard_map/ppermute | solution.py:39
  21.2 0.0 collective-permute-done.3.refs_4_
  21.2 0.0 copy-done.2
  21.2 1.6 %remap.1 = (f32[80,128]{1,0:T(8,128)S(1)}, f32[80,128]{1,0:T(8,128)S(1)}) custom-call(s32[4]{0:T(128)S(1)} %fusion.1.sel_ref, f32[80,128]{1,0:T(8,128)S(1)} %get-tuple-element.12.meta_ref, bf16[4,1024,128]{2,1,0:T(8,128)(2,1)S(1)} %get-tuple-element.13.w_ref, bf16[80,1024]{1,0:T(8,128)(2,1)S(1)} %bitcast.35, ...), custom_call_target="tpu_custom_call" | custom-call | tf_op jit(solution)/shard_map/remap/pallas_call | solution.py:444
  22.8 4.6 %collective-permute-start.9 = (f32[80,128]{1,0:T(8,128)S(1)}, f32[80,128]{1,0:T(8,128)S(1)}, u32[]{:S(2)}, u32[]{:S(2)}) collective-permute-start(f32[80,128]{1,0:T(8,128)S(1)} %get-tuple-element.15), channel_id=1, source_target_pairs={{0,15},{1,0},{2,1},{3,2},{4,3},{5,4},{6,5},{7,6},{8,7},{9,8},{10,9... | collective-permute-start | bytes 122888 | tf_op jit(solution)/shard_map/ppermute | solution.py:30
  27.4 0.0 collective-permute-start.8
  27.4 1.7 %collective-permute-done.9.after_ref = f32[80,128]{1,0:T(8,128)S(1)} collective-permute-done((f32[80,128]{1,0:T(8,128)S(1)}, f32[80,128]{1,0:T(8,128)S(1)}, u32[]{:S(2)}, u32[]{:S(2)}) %collective-permute-start.9) | collective-permute-done | bytes 40992 | tf_op jit(solution)/shard_map/ppermute | solution.py:30
  29.1 5.6 %collective-permute-done.8.before_ref = f32[80,128]{1,0:T(8,128)S(1)} collective-permute-done((f32[80,128]{1,0:T(8,128)S(1)}, f32[80,128]{1,0:T(8,128)S(1)}, u32[]{:S(2)}, u32[]{:S(2)}) %collective-permute-start.8) | collective-permute-done | bytes 40992 | tf_op jit(solution)/shard_map/ppermute | solution.py:30
  34.7 0.1 side.1
  34.9 0.0 collective-permute-start.10
  34.9 2.9 %collective-permute-start.11 = (f32[80,128]{1,0:T(8,128)S(1)}, f32[80,128]{1,0:T(8,128)S(1)}, u32[]{:S(2)}, u32[]{:S(2)}) collective-permute-start(f32[80,128]{1,0:T(8,128)S(1)} %get-tuple-element.17), channel_id=1, source_target_pairs={{0,112},{16,0},{32,16},{48,32},{64,48},{80,64},{96,80},{112,96},{1... | collective-permute-start | bytes 122888 | tf_op jit(solution)/shard_map/ppermute | solution.py:30
  37.8 1.7 %collective-permute-done.10.west_ref = f32[80,128]{1,0:T(8,128)S(1)} collective-permute-done((f32[80,128]{1,0:T(8,128)S(1)}, f32[80,128]{1,0:T(8,128)S(1)}, u32[]{:S(2)}, u32[]{:S(2)}) %collective-permute-start.10) | collective-permute-done | bytes 40992 | tf_op jit(solution)/shard_map/ppermute | solution.py:30
  39.5 0.0 collective-permute-done.11.east_ref
  39.5 6.1 %analysis.1 = (f32[13,1,128]{2,1,0:T(1,128)}, f32[13,80,128]{2,1,0:T(8,128)}) custom-call(f32[80,128]{1,0:T(8,128)S(1)} %get-tuple-element.12.meta_ref, f32[80,128]{1,0:T(8,128)S(1)} %get-tuple-element.14.state_ref, f32[80,128]{1,0:T(8,128)S(1)} %collective-permute-done.8.before_ref, f32[80,128]{1,0:T(8,128)S(1)} %collective-permute-done.9.after_ref, ...), custom_call_target="tpu_custom_call" | custom-call | tf_op jit(solution)/shard_map/analysis/pallas_call | solution.py:464
  (1 shorter events, 0.0 us)
Async XLA Ops:
  0.6 12.2 %collective-permute-start.1 = (bf16[80,1024]{1,0:T(8,128)(2,1)}, bf16[80,1024]{1,0:T(8,128)(2,1)S(1)}, u32[]{:S(2)}, u32[]{:S(2)}) collective-permute-start(bf16[80,1024]{1,0:T(8,128)(2,1)} %bitcast.31), channel_id=1, source_target_pairs={{0,15},{1,0},{2,1},{3,2},{4,3},{5,4},{6,5},{7,6},{8,7},{9,8},{10,9... | collective-permute-start | bytes 491528 | tf_op jit(solution)/shard_map/ppermute | solution.py:30
  6.0 9.2 %collective-permute-start = (bf16[80,1024]{1,0:T(8,128)(2,1)}, bf16[80,1024]{1,0:T(8,128)(2,1)S(1)}, u32[]{:S(2)}, u32[]{:S(2)}) collective-permute-start(bf16[80,1024]{1,0:T(8,128)(2,1)} %bitcast.32), channel_id=1, source_target_pairs={{0,1},{1,2},{2,3},{3,4},{4,5},{5,6},{6,7},{7,8},{8,9},{9,10},{10,1... | collective-permute-start | bytes 491528 | tf_op jit(solution)/shard_map/ppermute | solution.py:30
  6.0 11.5 %collective-permute-start.5 = (bf16[80,1024]{1,0:T(8,128)(2,1)}, bf16[80,1024]{1,0:T(8,128)(2,1)S(1)}, u32[]{:S(2)}, u32[]{:S(2)}) collective-permute-start(bf16[80,1024]{1,0:T(8,128)(2,1)} %bitcast.33), channel_id=1, source_target_pairs={{0,112},{16,32},{32,16},{48,64},{64,48},{80,96},{96,80},{112,0},{1... | collective-permute-start | bytes 491528 | tf_op jit(solution)/shard_map/ppermute | solution.py:39
  9.2 8.4 %collective-permute-start.2 = (bf16[80,1024]{1,0:T(8,128)(2,1)}, bf16[80,1024]{1,0:T(8,128)(2,1)S(1)}, u32[]{:S(2)}, u32[]{:S(2)}) collective-permute-start(bf16[80,1024]{1,0:T(8,128)(2,1)} %bitcast.34), channel_id=1, source_target_pairs={{0,16},{16,0},{32,48},{48,32},{64,80},{80,64},{96,112},{112,96},{1... | collective-permute-start | bytes 491528 | tf_op jit(solution)/shard_map/ppermute | solution.py:39
  9.2 0.7 %copy-start.6 = (f32[1,1,64]{2,1,0:T(1,128)S(1)}, f32[1,1,64]{2,1,0:T(1,128)}, u32[]{:S(2)}) copy-start(f32[1,1,64]{2,1,0:T(1,128)} %param.14) | copy-start | bytes 772
  9.2 0.7 %copy-start.7 = (f32[1,1,64]{2,1,0:T(1,128)S(1)}, f32[1,1,64]{2,1,0:T(1,128)}, u32[]{:S(2)}) copy-start(f32[1,1,64]{2,1,0:T(1,128)} %param.15) | copy-start | bytes 772
  9.2 0.7 %copy-start.3 = (s32[1,1,64]{2,1,0:T(1,128)S(1)}, s32[1,1,64]{2,1,0:T(1,128)}, u32[]{:S(2)}) copy-start(s32[1,1,64]{2,1,0:T(1,128)} %param.17) | copy-start | bytes 772
  9.2 0.7 %copy-start.4 = (s32[1,1,64]{2,1,0:T(1,128)S(1)}, s32[1,1,64]{2,1,0:T(1,128)}, u32[]{:S(2)}) copy-start(s32[1,1,64]{2,1,0:T(1,128)} %param.13) | copy-start | bytes 772
  9.2 0.7 %copy-start.5 = (s32[1,1,64]{2,1,0:T(1,128)S(1)}, s32[1,1,64]{2,1,0:T(1,128)}, u32[]{:S(2)}) copy-start(s32[1,1,64]{2,1,0:T(1,128)} %param.16) | copy-start | bytes 772
  9.9 1.2 %copy-start = (bf16[1,1,4,1024,128]{4,3,2,1,0:T(8,128)(2,1)S(1)}, bf16[1,1,4,1024,128]{4,3,2,1,0:T(8,128)(2,1)}, u32[]{:S(2)}) copy-start(bf16[1,1,4,1024,128]{4,3,2,1,0:T(8,128)(2,1)} %param.11) | copy-start | bytes 3145732
  11.2 1.0 %copy-start.1 = (f32[1,1,80,12,128]{4,2,3,1,0:T(8,128)S(1)}, f32[1,1,80,12,128]{4,2,3,1,0:T(8,128)}, u32[]{:S(2)}) copy-start(f32[1,1,80,12,128]{4,2,3,1,0:T(8,128)} %param.9) | copy-start | bytes 1474564
  12.2 5.4 %copy-start.8 = (s32[1,1,4]{2,1,0:T(1,128)S(1)}, s32[1,1,4]{2,1,0:T(1,128)}, u32[]{:S(2)}) copy-start(s32[1,1,4]{2,1,0:T(1,128)} %param.12) | copy-start | bytes 52
  12.2 9.0 %copy-start.2 = (bf16[1,1,80,1024]{3,2,1,0:T(8,128)(2,1)S(1)}, bf16[1,1,80,1024]{3,2,1,0:T(8,128)(2,1)}, u32[]{:S(2)}) copy-start(bf16[1,1,80,1024]{3,2,1,0:T(8,128)(2,1)} %param.10) | copy-start | bytes 491524
  12.9 6.0 %collective-permute-start.7 = (bf16[80,1024]{1,0:T(8,128)(2,1)S(1)}, bf16[80,1024]{1,0:T(8,128)(2,1)S(1)}, u32[]{:S(2)}, u32[]{:S(2)}) collective-permute-start(bf16[80,1024]{1,0:T(8,128)(2,1)S(1)} %collective-permute-done.1.refs_2_), channel_id=1, source_target_pairs={{0,112},{16,32},{32,16},{48,64},{64,48},{80,96},{96,80},{112,0},{1... | collective-permute-start | bytes 491528 | tf_op jit(solution)/shard_map/ppermute | solution.py:39
  13.9 5.0 %collective-permute-start.4 = (bf16[80,1024]{1,0:T(8,128)(2,1)S(1)}, bf16[80,1024]{1,0:T(8,128)(2,1)S(1)}, u32[]{:S(2)}, u32[]{:S(2)}) collective-permute-start(bf16[80,1024]{1,0:T(8,128)(2,1)S(1)} %collective-permute-done.1.refs_2_), channel_id=1, source_target_pairs={{0,16},{16,0},{32,48},{48,32},{64,80},{80,64},{96,112},{112,96},{1... | collective-permute-start | bytes 491528 | tf_op jit(solution)/shard_map/ppermute | solution.py:39
  15.2 6.0 %collective-permute-start.6 = (bf16[80,1024]{1,0:T(8,128)(2,1)S(1)}, bf16[80,1024]{1,0:T(8,128)(2,1)S(1)}, u32[]{:S(2)}, u32[]{:S(2)}) collective-permute-start(bf16[80,1024]{1,0:T(8,128)(2,1)S(1)} %collective-permute-done.refs_1_), channel_id=1, source_target_pairs={{0,112},{16,32},{32,16},{48,64},{64,48},{80,96},{96,80},{112,0},{1... | collective-permute-start | bytes 491528 | tf_op jit(solution)/shard_map/ppermute | solution.py:39
  17.6 3.6 %collective-permute-start.3 = (bf16[80,1024]{1,0:T(8,128)(2,1)S(1)}, bf16[80,1024]{1,0:T(8,128)(2,1)S(1)}, u32[]{:S(2)}, u32[]{:S(2)}) collective-permute-start(bf16[80,1024]{1,0:T(8,128)(2,1)S(1)} %collective-permute-done.refs_1_), channel_id=1, source_target_pairs={{0,16},{16,0},{32,48},{48,32},{64,80},{80,64},{96,112},{112,96},{1... | collective-permute-start | bytes 491528 | tf_op jit(solution)/shard_map/ppermute | solution.py:39
  22.8 6.3 %collective-permute-start.9 = (f32[80,128]{1,0:T(8,128)S(1)}, f32[80,128]{1,0:T(8,128)S(1)}, u32[]{:S(2)}, u32[]{:S(2)}) collective-permute-start(f32[80,128]{1,0:T(8,128)S(1)} %get-tuple-element.15), channel_id=1, source_target_pairs={{0,15},{1,0},{2,1},{3,2},{4,3},{5,4},{6,5},{7,6},{8,7},{9,8},{10,9... | collective-permute-start | bytes 122888 | tf_op jit(solution)/shard_map/ppermute | solution.py:30
  27.4 7.3 %collective-permute-start.8 = (f32[80,128]{1,0:T(8,128)S(1)}, f32[80,128]{1,0:T(8,128)S(1)}, u32[]{:S(2)}, u32[]{:S(2)}) collective-permute-start(f32[80,128]{1,0:T(8,128)S(1)} %get-tuple-element.15), channel_id=1, source_target_pairs={{0,1},{1,2},{2,3},{3,4},{4,5},{5,6},{6,7},{7,8},{8,9},{9,10},{10,1... | collective-permute-start | bytes 122888 | tf_op jit(solution)/shard_map/ppermute | solution.py:30
  34.9 4.7 %collective-permute-start.10 = (f32[80,128]{1,0:T(8,128)S(1)}, f32[80,128]{1,0:T(8,128)S(1)}, u32[]{:S(2)}, u32[]{:S(2)}) collective-permute-start(f32[80,128]{1,0:T(8,128)S(1)} %get-tuple-element.16), channel_id=1, source_target_pairs={{0,16},{16,32},{32,48},{48,64},{64,80},{80,96},{96,112},{112,0},{1... | collective-permute-start | bytes 122888 | tf_op jit(solution)/shard_map/ppermute | solution.py:30
  34.9 4.6 %collective-permute-start.11 = (f32[80,128]{1,0:T(8,128)S(1)}, f32[80,128]{1,0:T(8,128)S(1)}, u32[]{:S(2)}, u32[]{:S(2)}) collective-permute-start(f32[80,128]{1,0:T(8,128)S(1)} %get-tuple-element.17), channel_id=1, source_target_pairs={{0,112},{16,0},{32,16},{48,32},{64,48},{80,64},{96,80},{112,96},{1... | collective-permute-start | bytes 122888 | tf_op jit(solution)/shard_map/ppermute | solution.py:30

commit v3 on v2

--- a/solution.py
+++ b/solution.py
@@ -25,18 +25,19 @@
 OFFSETS = [(dx, dy) for dx in (-1, 0, 1) for dy in (-1, 0, 1)]
 
 
-def ring(block, axis, step):
-    count = lax.axis_size(axis)
-    return lax.ppermute(block, axis, [(i, (i + step) % count) for i in range(count)])
-
-
-def swap(block, axis, first):
-    count = lax.axis_size(axis)
+def exchange(block, axis, first):
+    count_x, count_y = lax.axis_size("gx"), lax.axis_size("gy")
     pairs = []
-    for at in range(first, count + first, 2):
-        low, high = at % count, (at + 1) % count
-        pairs += [(low, high), (high, low)]
-    return lax.ppermute(block, axis, sorted(pairs))
+    for x in range(count_x):
+        for y in range(count_y):
+            at, count = (x, count_x) if axis == "gx" else (y, count_y)
+            other = at ^ 1 if first == 0 else at - 1 + 2 * (at % 2)
+            if not 0 <= other < count:
+                to = (x, y ^ 1) if axis == "gx" else (x ^ 1, y)
+            else:
+                to = (other, y) if axis == "gx" else (x, other)
+            pairs.append((x * count_y + y, to[0] * count_y + to[1]))
+    return lax.ppermute(block, ("gx", "gy"), pairs)
 
 
 def lanes(rows=1):
@@ -96,11 +97,19 @@
     )
 
 
-def side_kernel(meta_ref, state_ref, before_ref, after_ref, right_ref, left_ref):
+def even(axis):
+    return lax.axis_index(axis) % 2 == 0
+
+
+def sides(low_ref, high_ref, axis):
+    low, high = low_ref[...], high_ref[...]
+    return jnp.where(even(axis), high, low), jnp.where(even(axis), low, high)
+
+
+def side_kernel(meta_ref, state_ref, close_ref, far_ref, near_out_ref, far_out_ref):
     lane = lanes()
     state = state_ref[...]
-    before = before_ref[...]
-    after = after_ref[...]
+    before, after = sides(close_ref, far_ref, "gy")
     columns = jnp.where(lane % AY >= 8, before, after)
     turned = pltpu.roll(columns, 64, 1)
     right = jnp.where(lane >= 64, state, turned)
@@ -114,8 +123,8 @@
     for n, record in enumerate((meta, before, after)):
         right = put(right, META + 3 * n, record, 3 * n)
         left = put(left, 32 + META + 3 * n, record, 32 + 3 * n)
-    right_ref[...] = right
-    left_ref[...] = left
+    near_out_ref[...] = jnp.where(even("gx"), right, left)
+    far_out_ref[...] = jnp.where(even("gx"), left, right)
 
 
 def views(blocks):
@@ -179,7 +188,7 @@
 
 
 def analysis_kernel(
-    meta_ref, state_ref, before_ref, after_ref, west_ref, east_ref, mean_ref, anom_ref,
+    meta_ref, state_ref, near_y_ref, far_y_ref, near_x_ref, far_x_ref, mean_ref, anom_ref,
     post_mean_hbm, post_anom_hbm,
     field_ref, moved_ref, first_ref, second_ref, out_ref, out_mean_ref, sem_ref,
 ):
@@ -192,12 +201,13 @@
     has_east = (at_x < lax.axis_size("gx") - 1).astype(jnp.int32)
     has_before = (at_y > 0).astype(jnp.int32)
     has_after = (at_y < lax.axis_size("gy") - 1).astype(jnp.int32)
-    west = west_ref[...]
-    east = east_ref[...]
+    meta = meta_ref[...]
+    before, after = sides(near_y_ref, far_y_ref, "gy")
+    west, east = sides(near_x_ref, far_x_ref, "gx")
     fields = [
         state_ref[...],
         jnp.where(low_x, east, west),
-        jnp.where(high_y, before_ref[...], after_ref[...]),
+        jnp.where(high_y, before, after),
         pltpu.roll(jnp.where(low_x, west, east), 64, 1),
     ]
     means = [total(field) / MEM for field in fields]
@@ -211,31 +221,31 @@
     open_lane = [jnp.ones_like(side_x), side_x, side_y, side_x * side_y]
 
     def weights(batch, squares, means):
-        rows = pl.ds(batch * OB, OB)
-
-        def column(ref, at):
-            return jnp.broadcast_to(ref[rows, at : at + 1], (OB, CELLS))
+        rows = slice(batch * OB, batch * OB + OB)
+
+        def column(block, at):
+            return jnp.broadcast_to(block[rows, at : at + 1], (OB, CELLS))
 
         def record(block, n):
             if block == 0:
-                return column(meta_ref, META + n)
+                return column(meta, META + n)
             if block == 1:
                 return jnp.where(
-                    low_x, column(east_ref, 32 + META + n), column(west_ref, META + n)
+                    low_x, column(east, 32 + META + n), column(west, META + n)
                 )
             if block == 2:
                 return jnp.where(
-                    high_y, column(before_ref, META + n), column(after_ref, META + n)
+                    high_y, column(before, META + n), column(after, META + n)
                 )
             return jnp.where(
                 low_x,
                 jnp.where(
                     high_y,
-                    column(east_ref, 32 + META + 3 + n),
-                    column(east_ref, 32 + META + 6 + n),
+                    column(east, 32 + META + 3 + n),
+                    column(east, 32 + META + 6 + n),
                 ),
                 jnp.where(
-                    high_y, column(west_ref, META + 3 + n), column(west_ref, META + 6 + n)
+                    high_y, column(west, META + 3 + n), column(west, META + 6 + n)
                 ),
             )
 
@@ -408,17 +418,16 @@
     at_y = lax.axis_index("gy")
     rows = lax.axis_size("gy")
     own = ocean_members[0, 0]
-    before = ring(own, "gy", 1)
-    after = ring(own, "gy", -1)
-    tiles = [own, before, after]
+    column = [own] + [exchange(own, "gy", first) for first in (0, 1)]
+    tiles = list(column)
     for first in (0, 1):
-        tiles += [swap(tile, "gx", first) for tile in (own, before, after)]
+        tiles += [exchange(tile, "gx", first) for tile in column]
     source = pair_src[0, 0]
-    step_x = source // rows - at_x
-    step_y = source % rows - at_y
-    side = jnp.where(step_x == 0, 0, jnp.where((step_x == 1) == (at_x % 2 == 0), 1, 2))
-    select = side * 3 + jnp.where(step_y == 0, 0, jnp.where(step_y < 0, 1, 2))
-
+
+    def slot(step, at):
+        return jnp.where(step == 0, 0, jnp.where((step == 1) == (at % 2 == 0), 1, 2))
+
+    select = slot(source // rows - at_x, at_x) * 3 + slot(source % rows - at_y, at_y)
     weights, anomaly, mean, meta = pl.pallas_call(
         prepare_kernel,
         in_specs=[ANY, ANY] + [VMEM] * 5,
@@ -449,18 +458,18 @@
         name="remap",
         compiler_params=LIMIT,
     )(select, meta, weights, *tiles)
-    from_before = ring(message, "gy", 1)
-    from_after = ring(message, "gy", -1)
-    to_right, to_left = pl.pallas_call(
+    near_y = exchange(message, "gy", 0)
+    far_y = exchange(message, "gy", 1)
+    near_out, far_out = pl.pallas_call(
         side_kernel,
         in_specs=[VMEM] * 4,
         out_specs=[VMEM, VMEM],
         out_shape=[flat(MEM, CELLS), flat(MEM, CELLS)],
         name="side",
         compiler_params=LIMIT,
-    )(meta, state, from_before, from_after)
-    from_west = ring(to_right, "gx", 1)
-    from_east = ring(to_left, "gx", -1)
+    )(meta, state, near_y, far_y)
+    near_x = exchange(near_out, "gx", 0)
+    far_x = exchange(far_out, "gx", 1)
     post_mean, post_anom = pl.pallas_call(
         analysis_kernel,
         in_specs=[VMEM] * 8,
@@ -477,7 +486,7 @@
         ],
         name="analysis",
         compiler_params=LIMIT,
-    )(meta, state, from_before, from_after, from_west, from_east, mean, anomaly)
+    )(meta, state, near_y, far_y, near_x, far_x, mean, anomaly)
     post_mean = jnp.transpose(post_mean, (1, 0, 2))
     post_anom = jnp.transpose(post_anom, (1, 0, 2))
     return post_mean[None], post_anom[None, None]

time: 45.8 us -> 36.2 us (0.79)
  the two profiles are of different devices: /device:TPU:0 before, /device:TPU:7 now
where the time goes in v3:
time: 36.2 us; the launch traced here: 36 us
  starting transfers between devices  15.2 us (42%)
  waiting for transfers between devices  8.68 us (24%)
  Pallas kernels  8.47 us (23%)
  local copies, waits for them, and re-layouts  2.96 us (8%)
  between operations  0.7 us (2%)
    ppermute x12, starting transfers between devices, exchange(): return lax.ppermute(block, ('gx', 'gy'), pairs)  15.2 us
    ppermute x12, waiting for transfers between devices, exchange(): return lax.ppermute(block, ('gx', 'gy'), pairs)  8.68 us
    pallas_call x1, Pallas kernels, local(): pl.pallas_call(analysis_kernel, in_specs=[VMEM] * 8, out_specs=[ANY, ANY]...  6.1 us
    unnamed x18, local copies, waits for them, and re-layouts  2.96 us
    pallas_call x1, Pallas kernels, local(): pl.pallas_call(remap_kernel, in_specs=[SMEM, VMEM, VMEM] + [VMEM] * 9, ou...  1.59 us
  transfers between devices with their start and end apart: 12, of which 5 were waited for; matrix products, arithmetic and copies ran while one was open for 0% of the time, Pallas kernels for 2%

profile of v3, /device:TPU:7, one launch (start us, length us, event | category | flops | bytes accessed | tf_op | source)
XLA Modules:
  0.0 36.0 jit_solution(15094947002390032802)
XLA Ops:
  0.6 3.1 %collective-permute-start.1 = (bf16[80,1024]{1,0:T(8,128)(2,1)}, bf16[80,1024]{1,0:T(8,128)(2,1)S(1)}, u32[]{:S(2)}, u32[]{:S(2)}) collective-permute-start(bf16[80,1024]{1,0:T(8,128)(2,1)} %bitcast.31), channel_id=1, source_target_pairs={{0,16},{1,2},{2,1},{3,4},{4,3},{5,6},{6,5},{7,8},{8,7},{9,10},{10,... | collective-permute-start | bytes 491528 | tf_op jit(solution)/shard_map/ppermute | solution.py:40
  3.7 0.0 collective-permute-start
  3.7 2.5 %collective-permute-start.5 = (bf16[80,1024]{1,0:T(8,128)(2,1)}, bf16[80,1024]{1,0:T(8,128)(2,1)S(1)}, u32[]{:S(2)}, u32[]{:S(2)}) collective-permute-start(bf16[80,1024]{1,0:T(8,128)(2,1)} %bitcast.33), channel_id=1, source_target_pairs={{0,1},{1,0},{2,3},{3,2},{4,5},{5,4},{6,7},{7,6},{8,9},{9,8},{10,11... | collective-permute-start | bytes 491528 | tf_op jit(solution)/shard_map/ppermute | solution.py:40
  6.2 0.5 %collective-permute-start.2 = (bf16[80,1024]{1,0:T(8,128)(2,1)}, bf16[80,1024]{1,0:T(8,128)(2,1)S(1)}, u32[]{:S(2)}, u32[]{:S(2)}) collective-permute-start(bf16[80,1024]{1,0:T(8,128)(2,1)} %bitcast.34), channel_id=1, source_target_pairs={{0,16},{1,17},{2,18},{3,19},{4,20},{5,21},{6,22},{7,23},{8,24},{9,... | collective-permute-start | bytes 491528 | tf_op jit(solution)/shard_map/ppermute | solution.py:40
  6.7 0.0 copy-start.6
  6.7 0.0 copy-start.7
  6.7 0.0 copy-start.3
  6.7 0.0 copy-start.4
  6.7 0.0 copy-start.5
  6.7 0.6 %copy-done.6 = f32[1,1,64]{2,1,0:T(1,128)S(1)} copy-done((f32[1,1,64]{2,1,0:T(1,128)S(1)}, f32[1,1,64]{2,1,0:T(1,128)}, u32[]{:S(2)}) %copy-start.6) | copy-done | bytes 280
  7.4 0.0 copy-done.7
  7.4 0.0 copy-done.3
  7.4 0.0 copy-done.4
  7.4 0.0 copy-done.5
  7.4 0.0 copy-start
  7.4 1.2 %copy-done = bf16[1,1,4,1024,128]{4,3,2,1,0:T(8,128)(2,1)S(1)} copy-done((bf16[1,1,4,1024,128]{4,3,2,1,0:T(8,128)(2,1)S(1)}, bf16[1,1,4,1024,128]{4,3,2,1,0:T(8,128)(2,1)}, u32[]{:S(2)}) %copy-start) | copy-done | bytes 1048600
  8.6 0.0 copy-start.1
  8.6 1.0 %copy-done.1 = f32[1,1,80,12,128]{4,2,3,1,0:T(8,128)S(1)} copy-done((f32[1,1,80,12,128]{4,2,3,1,0:T(8,128)S(1)}, f32[1,1,80,12,128]{4,2,3,1,0:T(8,128)}, u32[]{:S(2)}) %copy-start.1) | copy-done | bytes 491544
  9.7 0.0 copy-start.8
  9.7 0.0 copy-start.2
  9.7 0.6 %prepare.1 = (bf16[4,1024,128]{2,1,0:T(8,128)(2,1)S(1)}, f32[12,80,128]{2,1,0:T(8,128)S(1)}, f32[16,128]{1,0:T(8,128)S(1)}, f32[80,128]{1,0:T(8,128)S(1)}) custom-call(f32[12,80,128]{2,1,0:T(8,128)S(1)} %bitcast.30, bf16[4,1024,128]{2,1,0:T(8,128)(2,1)S(1)} %bitcast.29, s32[1,64]{1,0:T(1,128)S(1)} %bitcast.36, s32[1,64]{1,0:T(1,128)S(1)} %bitcast.37, ...), custom_call_target="tpu_custom_call" | custom-call | tf_op jit(solution)/shard_map/prepare/pallas_call | solution.py:431
  10.3 0.0 collective-permute-done.1.refs_2_
  10.3 1.6 %collective-permute-start.7 = (bf16[80,1024]{1,0:T(8,128)(2,1)S(1)}, bf16[80,1024]{1,0:T(8,128)(2,1)S(1)}, u32[]{:S(2)}, u32[]{:S(2)}) collective-permute-start(bf16[80,1024]{1,0:T(8,128)(2,1)S(1)} %collective-permute-done.1.refs_2_), channel_id=1, source_target_pairs={{0,1},{1,0},{2,3},{3,2},{4,5},{5,4},{6,7},{7,6},{8,9},{9,8},{10,11... | collective-permute-start | bytes 491528 | tf_op jit(solution)/shard_map/ppermute | solution.py:40
  12.0 0.5 %collective-permute-start.4 = (bf16[80,1024]{1,0:T(8,128)(2,1)S(1)}, bf16[80,1024]{1,0:T(8,128)(2,1)S(1)}, u32[]{:S(2)}, u32[]{:S(2)}) collective-permute-start(bf16[80,1024]{1,0:T(8,128)(2,1)S(1)} %collective-permute-done.1.refs_2_), channel_id=1, source_target_pairs={{0,16},{1,17},{2,18},{3,19},{4,20},{5,21},{6,22},{7,23},{8,24},{9,... | collective-permute-start | bytes 491528 | tf_op jit(solution)/shard_map/ppermute | solution.py:40
  12.5 0.0 collective-permute-done.refs_1_
  12.5 1.2 %collective-permute-start.6 = (bf16[80,1024]{1,0:T(8,128)(2,1)S(1)}, bf16[80,1024]{1,0:T(8,128)(2,1)S(1)}, u32[]{:S(2)}, u32[]{:S(2)}) collective-permute-start(bf16[80,1024]{1,0:T(8,128)(2,1)S(1)} %collective-permute-done.refs_1_), channel_id=1, source_target_pairs={{0,1},{1,0},{2,3},{3,2},{4,5},{5,4},{6,7},{7,6},{8,9},{9,8},{10,11... | collective-permute-start | bytes 491528 | tf_op jit(solution)/shard_map/ppermute | solution.py:40
  13.7 0.0 collective-permute-done.5.refs_6_
  13.7 0.8 %collective-permute-start.3 = (bf16[80,1024]{1,0:T(8,128)(2,1)S(1)}, bf16[80,1024]{1,0:T(8,128)(2,1)S(1)}, u32[]{:S(2)}, u32[]{:S(2)}) collective-permute-start(bf16[80,1024]{1,0:T(8,128)(2,1)S(1)} %collective-permute-done.refs_1_), channel_id=1, source_target_pairs={{0,16},{1,17},{2,18},{3,19},{4,20},{5,21},{6,22},{7,23},{8,24},{9,... | collective-permute-start | bytes 491528 | tf_op jit(solution)/shard_map/ppermute | solution.py:40
  14.5 0.0 copy-done.8
  14.5 0.0 collective-permute-done.2.refs_3_
  14.5 0.8 %collective-permute-done.7.refs_8_ = bf16[80,1024]{1,0:T(8,128)(2,1)S(1)} collective-permute-done((bf16[80,1024]{1,0:T(8,128)(2,1)S(1)}, bf16[80,1024]{1,0:T(8,128)(2,1)S(1)}, u32[]{:S(2)}, u32[]{:S(2)}) %collective-permute-start.7) | collective-permute-done | bytes 163872 | tf_op jit(solution)/shard_map/ppermute | solution.py:40
  15.4 0.0 collective-permute-done.4.refs_5_
  15.4 2.0 %collective-permute-done.6.refs_7_ = bf16[80,1024]{1,0:T(8,128)(2,1)S(1)} collective-permute-done((bf16[80,1024]{1,0:T(8,128)(2,1)S(1)}, bf16[80,1024]{1,0:T(8,128)(2,1)S(1)}, u32[]{:S(2)}, u32[]{:S(2)}) %collective-permute-start.6) | collective-permute-done | bytes 163872 | tf_op jit(solution)/shard_map/ppermute | solution.py:40
  17.4 0.0 collective-permute-done.3.refs_4_
  17.4 0.0 copy-done.2
  17.4 1.6 %remap.1 = (f32[80,128]{1,0:T(8,128)S(1)}, f32[80,128]{1,0:T(8,128)S(1)}) custom-call(s32[4]{0:T(128)S(1)} %fusion.1.sel_ref, f32[80,128]{1,0:T(8,128)S(1)} %get-tuple-element.12.meta_ref, bf16[4,1024,128]{2,1,0:T(8,128)(2,1)S(1)} %get-tuple-element.13.w_ref, bf16[80,1024]{1,0:T(8,128)(2,1)S(1)} %bitcast.35, ...), custom_call_target="tpu_custom_call" | custom-call | tf_op jit(solution)/shard_map/remap/pallas_call | solution.py:453
  19.0 2.2 %collective-permute-start.9 = (f32[80,128]{1,0:T(8,128)S(1)}, f32[80,128]{1,0:T(8,128)S(1)}, u32[]{:S(2)}, u32[]{:S(2)}) collective-permute-start(f32[80,128]{1,0:T(8,128)S(1)} %get-tuple-element.15), channel_id=1, source_target_pairs={{0,16},{1,2},{2,1},{3,4},{4,3},{5,6},{6,5},{7,8},{8,7},{9,10},{10,... | collective-permute-start | bytes 122888 | tf_op jit(solution)/shard_map/ppermute | solution.py:40
  21.2 0.0 collective-permute-start.8
  21.2 2.8 %collective-permute-done.9.far_ref.far_y_ref = f32[80,128]{1,0:T(8,128)S(1)} collective-permute-done((f32[80,128]{1,0:T(8,128)S(1)}, f32[80,128]{1,0:T(8,128)S(1)}, u32[]{:S(2)}, u32[]{:S(2)}) %collective-permute-start.9) | collective-permute-done | bytes 40992 | tf_op jit(solution)/shard_map/ppermute | solution.py:40
  24.0 0.3 collective-permute-done.8.close_ref.near_y_ref
  24.3 0.1 side.1
  24.5 1.7 %collective-permute-start.10 = (f32[80,128]{1,0:T(8,128)S(1)}, f32[80,128]{1,0:T(8,128)S(1)}, u32[]{:S(2)}, u32[]{:S(2)}) collective-permute-start(f32[80,128]{1,0:T(8,128)S(1)} %get-tuple-element.16), channel_id=1, source_target_pairs={{0,16},{1,17},{2,18},{3,19},{4,20},{5,21},{6,22},{7,23},{8,24},{9,... | collective-permute-start | bytes 122888 | tf_op jit(solution)/shard_map/ppermute | solution.py:40
  26.2 1.0 %collective-permute-start.11 = (f32[80,128]{1,0:T(8,128)S(1)}, f32[80,128]{1,0:T(8,128)S(1)}, u32[]{:S(2)}, u32[]{:S(2)}) collective-permute-start(f32[80,128]{1,0:T(8,128)S(1)} %get-tuple-element.17), channel_id=1, source_target_pairs={{0,1},{1,0},{2,3},{3,2},{4,5},{5,4},{6,7},{7,6},{8,9},{9,8},{10,11... | collective-permute-start | bytes 122888 | tf_op jit(solution)/shard_map/ppermute | solution.py:40
  27.2 0.0 collective-permute-done.10.near_x_ref
  27.2 2.7 %collective-permute-done.11.far_x_ref = f32[80,128]{1,0:T(8,128)S(1)} collective-permute-done((f32[80,128]{1,0:T(8,128)S(1)}, f32[80,128]{1,0:T(8,128)S(1)}, u32[]{:S(2)}, u32[]{:S(2)}) %collective-permute-start.11) | collective-permute-done | bytes 40992 | tf_op jit(solution)/shard_map/ppermute | solution.py:40
  29.9 6.1 %analysis.1 = (f32[13,1,128]{2,1,0:T(1,128)}, f32[13,80,128]{2,1,0:T(8,128)}) custom-call(f32[80,128]{1,0:T(8,128)S(1)} %get-tuple-element.12.meta_ref, f32[80,128]{1,0:T(8,128)S(1)} %get-tuple-element.14.state_ref, f32[80,128]{1,0:T(8,128)S(1)} %collective-permute-done.8.close_ref.near_y_ref, f32[80,128]{1,0:T(8,128)S(1)} %collective-permute-done.9.far_ref.far_y_ref, ...), custom_call_target="tpu_custom_call" | custom-call | tf_op jit(solution)/shard_map/analysis/pallas_call | solution.py:473
  (1 shorter events, 0.0 us)
Async XLA Ops:
  0.6 9.7 %collective-permute-start.1 = (bf16[80,1024]{1,0:T(8,128)(2,1)}, bf16[80,1024]{1,0:T(8,128)(2,1)S(1)}, u32[]{:S(2)}, u32[]{:S(2)}) collective-permute-start(bf16[80,1024]{1,0:T(8,128)(2,1)} %bitcast.31), channel_id=1, source_target_pairs={{0,16},{1,2},{2,1},{3,4},{4,3},{5,6},{6,5},{7,8},{8,7},{9,10},{10,... | collective-permute-start | bytes 491528 | tf_op jit(solution)/shard_map/ppermute | solution.py:40
  3.7 8.7 %collective-permute-start = (bf16[80,1024]{1,0:T(8,128)(2,1)}, bf16[80,1024]{1,0:T(8,128)(2,1)S(1)}, u32[]{:S(2)}, u32[]{:S(2)}) collective-permute-start(bf16[80,1024]{1,0:T(8,128)(2,1)} %bitcast.32), channel_id=1, source_target_pairs={{0,1},{1,0},{2,3},{3,2},{4,5},{5,4},{6,7},{7,6},{8,9},{9,8},{10,11... | collective-permute-start | bytes 491528 | tf_op jit(solution)/shard_map/ppermute | solution.py:40
  3.7 10.0 %collective-permute-start.5 = (bf16[80,1024]{1,0:T(8,128)(2,1)}, bf16[80,1024]{1,0:T(8,128)(2,1)S(1)}, u32[]{:S(2)}, u32[]{:S(2)}) collective-permute-start(bf16[80,1024]{1,0:T(8,128)(2,1)} %bitcast.33), channel_id=1, source_target_pairs={{0,1},{1,0},{2,3},{3,2},{4,5},{5,4},{6,7},{7,6},{8,9},{9,8},{10,11... | collective-permute-start | bytes 491528 | tf_op jit(solution)/shard_map/ppermute | solution.py:40
  6.2 8.3 %collective-permute-start.2 = (bf16[80,1024]{1,0:T(8,128)(2,1)}, bf16[80,1024]{1,0:T(8,128)(2,1)S(1)}, u32[]{:S(2)}, u32[]{:S(2)}) collective-permute-start(bf16[80,1024]{1,0:T(8,128)(2,1)} %bitcast.34), channel_id=1, source_target_pairs={{0,16},{1,17},{2,18},{3,19},{4,20},{5,21},{6,22},{7,23},{8,24},{9,... | collective-permute-start | bytes 491528 | tf_op jit(solution)/shard_map/ppermute | solution.py:40
  6.7 0.7 %copy-start.6 = (f32[1,1,64]{2,1,0:T(1,128)S(1)}, f32[1,1,64]{2,1,0:T(1,128)}, u32[]{:S(2)}) copy-start(f32[1,1,64]{2,1,0:T(1,128)} %param.14) | copy-start | bytes 772
  6.7 0.7 %copy-start.7 = (f32[1,1,64]{2,1,0:T(1,128)S(1)}, f32[1,1,64]{2,1,0:T(1,128)}, u32[]{:S(2)}) copy-start(f32[1,1,64]{2,1,0:T(1,128)} %param.15) | copy-start | bytes 772
  6.7 0.7 %copy-start.3 = (s32[1,1,64]{2,1,0:T(1,128)S(1)}, s32[1,1,64]{2,1,0:T(1,128)}, u32[]{:S(2)}) copy-start(s32[1,1,64]{2,1,0:T(1,128)} %param.17) | copy-start | bytes 772
  6.7 0.7 %copy-start.4 = (s32[1,1,64]{2,1,0:T(1,128)S(1)}, s32[1,1,64]{2,1,0:T(1,128)}, u32[]{:S(2)}) copy-start(s32[1,1,64]{2,1,0:T(1,128)} %param.13) | copy-start | bytes 772
  6.7 0.7 %copy-start.5 = (s32[1,1,64]{2,1,0:T(1,128)S(1)}, s32[1,1,64]{2,1,0:T(1,128)}, u32[]{:S(2)}) copy-start(s32[1,1,64]{2,1,0:T(1,128)} %param.16) | copy-start | bytes 772
  7.4 1.2 %copy-start = (bf16[1,1,4,1024,128]{4,3,2,1,0:T(8,128)(2,1)S(1)}, bf16[1,1,4,1024,128]{4,3,2,1,0:T(8,128)(2,1)}, u32[]{:S(2)}) copy-start(bf16[1,1,4,1024,128]{4,3,2,1,0:T(8,128)(2,1)} %param.11) | copy-start | bytes 3145732
  8.6 1.0 %copy-start.1 = (f32[1,1,80,12,128]{4,2,3,1,0:T(8,128)S(1)}, f32[1,1,80,12,128]{4,2,3,1,0:T(8,128)}, u32[]{:S(2)}) copy-start(f32[1,1,80,12,128]{4,2,3,1,0:T(8,128)} %param.9) | copy-start | bytes 1474564
  9.7 4.8 %copy-start.8 = (s32[1,1,4]{2,1,0:T(1,128)S(1)}, s32[1,1,4]{2,1,0:T(1,128)}, u32[]{:S(2)}) copy-start(s32[1,1,4]{2,1,0:T(1,128)} %param.12) | copy-start | bytes 52
  9.7 7.7 %copy-start.2 = (bf16[1,1,80,1024]{3,2,1,0:T(8,128)(2,1)S(1)}, bf16[1,1,80,1024]{3,2,1,0:T(8,128)(2,1)}, u32[]{:S(2)}) copy-start(bf16[1,1,80,1024]{3,2,1,0:T(8,128)(2,1)} %param.10) | copy-start | bytes 491524
  10.3 5.0 %collective-permute-start.7 = (bf16[80,1024]{1,0:T(8,128)(2,1)S(1)}, bf16[80,1024]{1,0:T(8,128)(2,1)S(1)}, u32[]{:S(2)}, u32[]{:S(2)}) collective-permute-start(bf16[80,1024]{1,0:T(8,128)(2,1)S(1)} %collective-permute-done.1.refs_2_), channel_id=1, source_target_pairs={{0,1},{1,0},{2,3},{3,2},{4,5},{5,4},{6,7},{7,6},{8,9},{9,8},{10,11... | collective-permute-start | bytes 491528 | tf_op jit(solution)/shard_map/ppermute | solution.py:40
  12.0 3.4 %collective-permute-start.4 = (bf16[80,1024]{1,0:T(8,128)(2,1)S(1)}, bf16[80,1024]{1,0:T(8,128)(2,1)S(1)}, u32[]{:S(2)}, u32[]{:S(2)}) collective-permute-start(bf16[80,1024]{1,0:T(8,128)(2,1)S(1)} %collective-permute-done.1.refs_2_), channel_id=1, source_target_pairs={{0,16},{1,17},{2,18},{3,19},{4,20},{5,21},{6,22},{7,23},{8,24},{9,... | collective-permute-start | bytes 491528 | tf_op jit(solution)/shard_map/ppermute | solution.py:40
  12.5 4.9 %collective-permute-start.6 = (bf16[80,1024]{1,0:T(8,128)(2,1)S(1)}, bf16[80,1024]{1,0:T(8,128)(2,1)S(1)}, u32[]{:S(2)}, u32[]{:S(2)}) collective-permute-start(bf16[80,1024]{1,0:T(8,128)(2,1)S(1)} %collective-permute-done.refs_1_), channel_id=1, source_target_pairs={{0,1},{1,0},{2,3},{3,2},{4,5},{5,4},{6,7},{7,6},{8,9},{9,8},{10,11... | collective-permute-start | bytes 491528 | tf_op jit(solution)/shard_map/ppermute | solution.py:40
  13.7 3.7 %collective-permute-start.3 = (bf16[80,1024]{1,0:T(8,128)(2,1)S(1)}, bf16[80,1024]{1,0:T(8,128)(2,1)S(1)}, u32[]{:S(2)}, u32[]{:S(2)}) collective-permute-start(bf16[80,1024]{1,0:T(8,128)(2,1)S(1)} %collective-permute-done.refs_1_), channel_id=1, source_target_pairs={{0,16},{1,17},{2,18},{3,19},{4,20},{5,21},{6,22},{7,23},{8,24},{9,... | collective-permute-start | bytes 491528 | tf_op jit(solution)/shard_map/ppermute | solution.py:40
  19.0 5.0 %collective-permute-start.9 = (f32[80,128]{1,0:T(8,128)S(1)}, f32[80,128]{1,0:T(8,128)S(1)}, u32[]{:S(2)}, u32[]{:S(2)}) collective-permute-start(f32[80,128]{1,0:T(8,128)S(1)} %get-tuple-element.15), channel_id=1, source_target_pairs={{0,16},{1,2},{2,1},{3,4},{4,3},{5,6},{6,5},{7,8},{8,7},{9,10},{10,... | collective-permute-start | bytes 122888 | tf_op jit(solution)/shard_map/ppermute | solution.py:40
  21.2 3.1 %collective-permute-start.8 = (f32[80,128]{1,0:T(8,128)S(1)}, f32[80,128]{1,0:T(8,128)S(1)}, u32[]{:S(2)}, u32[]{:S(2)}) collective-permute-start(f32[80,128]{1,0:T(8,128)S(1)} %get-tuple-element.15), channel_id=1, source_target_pairs={{0,1},{1,0},{2,3},{3,2},{4,5},{5,4},{6,7},{7,6},{8,9},{9,8},{10,11... | collective-permute-start | bytes 122888 | tf_op jit(solution)/shard_map/ppermute | solution.py:40
  24.5 2.8 %collective-permute-start.10 = (f32[80,128]{1,0:T(8,128)S(1)}, f32[80,128]{1,0:T(8,128)S(1)}, u32[]{:S(2)}, u32[]{:S(2)}) collective-permute-start(f32[80,128]{1,0:T(8,128)S(1)} %get-tuple-element.16), channel_id=1, source_target_pairs={{0,16},{1,17},{2,18},{3,19},{4,20},{5,21},{6,22},{7,23},{8,24},{9,... | collective-permute-start | bytes 122888 | tf_op jit(solution)/shard_map/ppermute | solution.py:40
  26.2 3.7 %collective-permute-start.11 = (f32[80,128]{1,0:T(8,128)S(1)}, f32[80,128]{1,0:T(8,128)S(1)}, u32[]{:S(2)}, u32[]{:S(2)}) collective-permute-start(f32[80,128]{1,0:T(8,128)S(1)} %get-tuple-element.17), channel_id=1, source_target_pairs={{0,1},{1,0},{2,3},{3,2},{4,5},{5,4},{6,7},{7,6},{8,9},{9,8},{10,11... | collective-permute-start | bytes 122888 | tf_op jit(solution)/shard_map/ppermute | solution.py:40

commit v4 on v3

v4 whole, which is shorter than its diff:
```python
import jax
import jax.numpy as jnp
from jax import lax
from jax.experimental import pallas as pl
from jax.experimental.pallas import tpu as pltpu
from jax.sharding import PartitionSpec as P

MEM = 80
AX = 8
AY = 16
OCN_DEV = 1024
OB = 32
NB = 2
K = 4
FIELDS = 12
COMP = 13
CELLS = 128
OBS_DEV = 64

f32 = jnp.float32
RECORD = 3
TAPER = {0: 1.0, 1: 0.5625, 2: 0.25}
OFFSETS = [(dx, dy) for dx in (-1, 0, 1) for dy in (-1, 0, 1)]


def exchange(block, axis, first):
    count_x, count_y = lax.axis_size("gx"), lax.axis_size("gy")
    pairs = []
    for x in range(count_x):
        for y in range(count_y):
            at, count = (x, count_x) if axis == "gx" else (y, count_y)
            other = at ^ 1 if first == 0 else at - 1 + 2 * (at % 2)
            if not 0 <= other < count:
                to = (x, y ^ 1) if axis == "gx" else (x ^ 1, y)
            else:
                to = (other, y) if axis == "gx" else (x, other)
            pairs.append((x * count_y + y, to[0] * count_y + to[1]))
    return lax.ppermute(block, ("gx", "gy"), pairs)


def lanes(rows=1):
    return lax.broadcasted_iota(jnp.int32, (rows, CELLS), 1)


def records_kernel(first_hbm, w_ref, order_ref, cell_ref, live_ref, value_ref, error_ref, meta_ref):
    order = jnp.transpose(jnp.broadcast_to(order_ref[...], (OBS_DEV, OBS_DEV)))
    taken = order == lax.broadcasted_iota(jnp.int32, (OBS_DEV, OBS_DEV), 1)
    lane = lanes(8)
    records = jnp.zeros((8, CELLS), f32)
    cell = jnp.where(live_ref[...] > 0, cell_ref[...], -1).astype(f32)
    for n, row in enumerate((cell, value_ref[...], error_ref[...])):
        picked = jnp.sum(jnp.where(taken, row, 0.0), axis=1, keepdims=True)
        for g in range(OBS_DEV // 8):
            column = jnp.broadcast_to(picked[8 * g : 8 * g + 8], (8, CELLS))
            records = jnp.where(lane == RECORD * g + n, column, records)
    meta_ref[...] = records


def fields_kernel(state_hbm, atm_ref, anom_ref, mean_ref):
    mean_ref[...] = jnp.zeros_like(mean_ref)
    for v in range(FIELDS):
        field = atm_ref[v]
        mean = jnp.sum(field, axis=0, keepdims=True) / MEM
        mean_ref[v : v + 1, :] = mean
        anom_ref[v] = field - mean


def even(axis):
    return lax.axis_index(axis) % 2 == 0


def remap_kernel(slot_ref, meta_ref, w_ref, *refs):
    tiles, (state_ref, near_ref, far_ref) = refs[:9], refs[9:]
    state_ref[...] = jnp.zeros_like(state_ref)
    for index, tile in enumerate(tiles):
        k = slot_ref[index]

        @pl.when(k >= 0)
        def _(tile=tile, k=k):
            state_ref[...] += jnp.dot(tile[...], w_ref[k], preferred_element_type=f32)

    y = lanes() % AY
    high = low = jnp.zeros((16, CELLS), f32)
    for g in range(MEM // 16):
        part = state_ref[16 * g : 16 * g + 16, :]
        up = pltpu.roll(part, (CELLS - 2 * g) % CELLS, 1) if g else part
        down = pltpu.roll(part, 2 * g, 1) if g else part
        high = jnp.where(y // 2 == 7 - g, up, high)
        low = jnp.where(y // 2 == g, down, low)
    near_ref[0:16, :] = jnp.where(even("gy"), high, low)
    far_ref[0:16, :] = jnp.where(even("gy"), low, high)
    near_ref[16:24, :] = meta_ref[...]
    far_ref[16:24, :] = meta_ref[...]


def sides(near_ref, far_ref, axis):
    near, far = near_ref[...], far_ref[...]
    return jnp.where(even(axis), far, near), jnp.where(even(axis), near, far)


HALF = MEM // 2


def side_kernel(meta_ref, state_ref, near_ref, far_ref, column_ref, near_out_ref, far_out_ref):
    lane = lanes()
    before, after = sides(near_ref, far_ref, "gy")
    high_y = lane % AY >= 8
    for g in range(MEM // 16):
        lower, upper = before[0:16], after[0:16]
        if g:
            lower = pltpu.roll(lower, 2 * g, 1)
            upper = pltpu.roll(upper, CELLS - 2 * g, 1)
        column_ref[16 * g : 16 * g + 16, :] = jnp.where(high_y, lower, upper)
    quarter = lane // 32
    state_a, state_b = state_ref[0:HALF, :], state_ref[HALF:MEM, :]
    column_a, column_b = column_ref[0:HALF, :], column_ref[HALF:MEM, :]
    turned = pltpu.roll(column_a, 64, 1)

    def pack(order, blocks):
        out = blocks[3]
        for n in range(3):
            out = jnp.where(quarter == order[n], blocks[n], out)
        return out

    right = pack(
        (3, 2, 1), (state_a, pltpu.roll(state_b, 96, 1), turned, pltpu.roll(column_b, 32, 1))
    )
    left = pack(
        (0, 1, 2), (state_a, pltpu.roll(state_b, 32, 1), turned, pltpu.roll(column_b, 96, 1))
    )
    near_out_ref[0:HALF, :] = jnp.where(even("gx"), right, left)
    far_out_ref[0:HALF, :] = jnp.where(even("gx"), left, right)
    records = pack(
        (0, 1, 2),
        (
            meta_ref[...],
            pltpu.roll(before[16:24], 32, 1),
            pltpu.roll(after[16:24], 64, 1),
            jnp.zeros((8, CELLS), f32),
        ),
    )
    near_out_ref[HALF : HALF + 8, :] = records
    far_out_ref[HALF : HALF + 8, :] = records


def turned_up(a, b):
    return jnp.where(lanes() % AY == 15, pltpu.roll(b, 15, 1), pltpu.roll(a, 127, 1))


def turned_down(a, b):
    return jnp.where(lanes() % AY == 0, pltpu.roll(b, 113, 1), pltpu.roll(a, 1, 1))


def turned_right(a, b):
    return pltpu.roll(jnp.where(lanes() < AY, b, a), 112, 1)


def turned_left(a, b):
    return pltpu.roll(jnp.where(lanes() >= CELLS - AY, b, a), 16, 1)


def shifted_rows(blocks):
    m0, m1, h0, h1 = blocks
    return {
        0: blocks,
        1: [turned_up(m0, h0), turned_up(m1, h1), turned_up(h0, m0), turned_up(h1, m1)],
        -1: [turned_down(m0, h0), turned_down(m1, h1), turned_down(h0, m0), turned_down(h1, m1)],
    }


def views_of(rows, count=4):
    out = {}
    for dy, blocks in rows.items():
        out[0, dy] = list(blocks[:count])
        for dx, turn in ((1, turned_right), (-1, turned_left)):
            out[dx, dy] = [turn(blocks[n], blocks[n ^ 1]) for n in range(count)]
    return out


def own_rows(blocks):
    m0, m1, h0, h1 = blocks
    return {
        0: [m0, m1],
        1: [turned_up(m0, h0), turned_up(m1, h1)],
        -1: [turned_down(m0, h0), turned_down(m1, h1)],
    }


def own_views(blocks):
    return {key: value[0] for key, value in views_of(own_rows(blocks), 1).items()}


ROWS = MEM // 8


def group(r):
    return pl.ds(pl.multiple_of(r * 8, 8), 8)


def total(block):
    return jnp.sum(block, axis=0, keepdims=True)


def spread(rows):
    return [jnp.broadcast_to(row, (8, CELLS)) for row in rows]


def scale(key):
    return TAPER[key[0] ** 2 + key[1] ** 2] / (MEM - 1)


def present():
    at_x, at_y = lax.axis_index("gx"), lax.axis_index("gy")
    return [
        flag.astype(jnp.int32)
        for flag in (
            at_x > 0,
            at_x < lax.axis_size("gx") - 1,
            at_y > 0,
            at_y < lax.axis_size("gy") - 1,
        )
    ]


def cell_weights(record, there, batch, square, mean):
    variance = square / (MEM - 1)
    pulls = damped = jnp.zeros((8, CELLS), f32)
    for g in range(batch * OB // 8, (batch + 1) * OB // 8):
        here = (record(RECORD * g) == lanes().astype(f32)) & there
        error = record(RECORD * g + 2)
        denominator = variance + error
        pull = (record(RECORD * g + 1) - mean) / denominator
        damp = 1.0 / (denominator + jnp.sqrt(error * denominator))
        pulls = pulls + jnp.where(here, pull, 0.0)
        damped = damped + jnp.where(here, damp, 0.0)
    return total(pulls), total(damped)


def column_of(records):
    return lambda at: jnp.broadcast_to(records[:, at : at + 1], (8, CELLS))


def window_kernel(
    meta_ref, state_ref, column_ref, near_ref, far_ref, anom_ref,
    field_ref, turned_ref, rows_ref, partial_ref, view_ref,
):
    lane = lanes()
    high_y = lane % AY >= 8
    before, after = sides(near_ref, far_ref, "gy")
    lower, upper = column_of(before[16:24]), column_of(after[16:24])
    _, _, has_before, has_after = present()
    records = (
        column_of(meta_ref[...]),
        lambda at: jnp.where(high_y, lower(at), upper(at)),
    )
    there = (lane >= 0, jnp.where(high_y, has_before, has_after) > 0)
    for block, ref in enumerate((state_ref, column_ref)):
        state = ref[...]
        mean = total(state) / MEM
        anom = state - mean
        field_ref[block] = anom
        square = total(anom * anom)
        pulls, damped = cell_weights(records[block], there[block], 0, square, mean)
        rows_ref[block : block + 1, :] = mean
        rows_ref[2 + block : 3 + block, :] = pulls
        rows_ref[4 + block : 5 + block, :] = damped

    for r in range(ROWS):
        at = slice(8 * r, 8 * r + 8)
        own, beside = field_ref[0, at, :], field_ref[1, at, :]
        up, down = turned_up(own, beside), turned_down(own, beside)
        turned_ref[0, 0, at, :] = up
        turned_ref[0, 1, at, :] = turned_up(beside, own)
        turned_ref[1, 0, at, :] = down
        turned_ref[1, 1, at, :] = turned_down(beside, own)
        rows = {0: own, 1: up, -1: down}
        for n, (dx, dy) in enumerate(OFFSETS):
            view = rows[dy]
            if dx == 1:
                view = turned_right(view, 0.0)
            if dx == -1:
                view = turned_left(view, 0.0)
            view_ref[n, at, :] = view

    zero = jnp.zeros((8, CELLS), f32)
    partial_ref[...] = jnp.zeros_like(partial_ref)

    def sums_of(blocks):
        sums = [[zero] * 9 for _ in blocks]
        for r in range(ROWS):
            at = slice(8 * r, 8 * r + 8)
            shifted = [view_ref[n, at, :] for n in range(9)]
            for i, block in enumerate(blocks):
                rows = block(at)
                sums[i] = [s + rows * w for s, w in zip(sums[i], shifted)]
        return sums

    (sums,) = sums_of([lambda at: field_ref[0, at, :]])
    for n in range(9):
        partial_ref[FIELDS, n : n + 1, :] = total(sums[n])

    def pair(g, carry):
        sums = sums_of([lambda at, v=2 * g + i: anom_ref[v, at, :] for i in range(2)])
        for i in range(2):
            for n in range(9):
                partial_ref[2 * g + i, n : n + 1, :] = total(sums[i][n])
        return carry

    lax.fori_loop(0, FIELDS // 2, pair, 0)


def analysis_kernel(
    meta_ref, near_y_ref, far_y_ref, near_x_ref, far_x_ref, field_ref, turned_ref, rows_ref,
    partial_ref, mean_ref, anom_ref, post_mean_hbm, post_anom_hbm,
    other_ref, moved_ref, first_ref, edge_ref, second_ref, out_ref, out_mean_ref, sem_ref,
):
    lane = lanes()
    low_x = lane < 64
    high_y = lane % AY >= 8
    has_west, has_east, has_before, has_after = present()
    before, after = sides(near_y_ref, far_y_ref, "gy")
    west, east = sides(near_x_ref, far_x_ref, "gx")
    west_column, east_column = column_of(west[HALF:]), column_of(east[HALF:])
    lower, upper = column_of(before[16:24]), column_of(after[16:24])
    records = (
        column_of(meta_ref[...]),
        lambda at: jnp.where(low_x, east_column(at), west_column(at)),
        lambda at: jnp.where(high_y, lower(at), upper(at)),
        lambda at: jnp.where(
            low_x,
            jnp.where(high_y, east_column(32 + at), east_column(64 + at)),
            jnp.where(high_y, west_column(32 + at), west_column(64 + at)),
        ),
    )
    side_x = jnp.where(low_x, has_east, has_west)
    side_y = jnp.where(high_y, has_before, has_after)
    there = (lane >= 0, side_x > 0, side_y > 0, side_x * side_y > 0)

    means = [rows_ref[0:1, :], None, rows_ref[1:2, :], None]
    pulls = [rows_ref[2:3, :], None, rows_ref[3:4, :], None]
    damped = [rows_ref[4:5, :], None, rows_ref[5:6, :], None]
    west_half, east_half = west[0:HALF], east[0:HALF]
    halves = {
        1: (
            jnp.where(low_x, east_half, west_half),
            jnp.where(low_x, pltpu.roll(east_half, 96, 1), pltpu.roll(west_half, 32, 1)),
        ),
        3: (
            pltpu.roll(jnp.where(low_x, west_half, east_half), 64, 1),
            jnp.where(low_x, pltpu.roll(east_half, 32, 1), pltpu.roll(west_half, 96, 1)),
        ),
    }
    for block, (first, second) in halves.items():
        mean = (total(first) + total(second)) / MEM
        first, second = first - mean, second - mean
        other_ref[block // 2, 0:HALF, :] = first
        other_ref[block // 2, HALF:MEM, :] = second
        square = total(first * first) + total(second * second)
        means[block] = mean
        pulls[block], damped[block] = cell_weights(records[block], there[block], 0, square, mean)

    zero = jnp.zeros((8, CELLS), f32)
    pull_views = views_of(shifted_rows(spread(pulls)))
    damp_views = views_of(shifted_rows(spread(damped)))
    edges = [(1, dy) for dy in (-1, 0, 1)]

    def at_edge(right, left):
        return jnp.where(lane >= CELLS - AY, right, jnp.where(lane < AY, left, 0.0))

    def shift_first(r, sums):
        at = group(r)
        m0, h0 = field_ref[0, at, :], field_ref[1, at, :]
        m1, h1 = other_ref[0, at, :], other_ref[1, at, :]
        rows = {
            0: [m0, m1, h0, h1],
            1: [turned_ref[0, 0, at, :], turned_up(m1, h1), turned_ref[0, 1, at, :], turned_up(h1, m1)],
            -1: [
                turned_ref[1, 0, at, :], turned_down(m1, h1), turned_ref[1, 1, at, :], turned_down(h1, m1),
            ],
        }
        shifted = views_of(rows)
        out = []
        for n, key in enumerate(OFFSETS):
            for block in range(4):
                first_ref[block, n, at, :] = shifted[key][block]
        for n, key in enumerate(OFFSETS):
            for block in range(1, 4):
                out.append(sums[n * 3 + block - 1] + shifted[key][block] * rows[0][block])
        for n, (_, dy) in enumerate(edges):
            edge = at_edge(shifted[1, dy][0], shifted[-1, dy][0])
            edge_ref[n, at, :] = edge
            out.append(sums[27 + n] + edge * m0)
        return tuple(out)

    sums = lax.fori_loop(0, ROWS, shift_first, (zero,) * 30, unroll=2)

    def completed(v, extra):
        out = {}
        for n, key in enumerate(OFFSETS):
            covariance = partial_ref[v, n : n + 1, :]
            if key[0]:
                more = total(extra[key[1] + 1])
                covariance = covariance + jnp.where(
                    lane >= CELLS - AY if key[0] == 1 else lane < AY, more, 0.0
                )
            out[key] = covariance * scale(key)
        return out

    next_means, next_squares = [], []
    for block in range(4):
        if block == 0:
            covariances = completed(FIELDS, sums[27:30])
        else:
            covariances = {
                key: total(sums[n * 3 + block - 1]) * scale(key) for n, key in enumerate(OFFSETS)
            }
        step = jnp.zeros_like(means[block])
        gains = []
        for key in OFFSETS:
            step = step + covariances[key] * pull_views[key][block][0:1]
            gains.append(covariances[key] * damp_views[key][block][0:1])
        square = zero
        for r in range(ROWS):
            at = slice(8 * r, 8 * r + 8)
            source = other_ref if block % 2 else field_ref
            moved = source[block // 2, at, :]
            for n in range(9):
                moved = moved - gains[n] * first_ref[block, n, at, :]
            moved_ref[block, at, :] = moved
            square = square + moved * moved
        next_means.append(means[block] + step)
        next_squares.append(total(square))
    next_pulls, next_damped = [], []
    for block in range(4):
        pull, damp = cell_weights(
            records[block], there[block], 1, next_squares[block], next_means[block]
        )
        next_pulls.append(pull)
        next_damped.append(damp)
    next_pull_views = own_views(spread(next_pulls))
    next_damp_views = own_views(spread(next_damped))

    def shift_second(r, sums):
        at = group(r)
        blocks = [moved_ref[block, at, :] for block in range(4)]
        shifted = own_views(blocks)
        out = []
        for n, key in enumerate(OFFSETS):
            second_ref[n, at, :] = shifted[key]
            out.append(sums[n] + shifted[key] * blocks[0])
        return tuple(out)

    sums = lax.fori_loop(0, ROWS, shift_second, (zero,) * 9, unroll=2)

    def finish(sums, mean):
        gains = []
        for n, key in enumerate(OFFSETS):
            covariance = total(sums[n]) * scale(key)
            mean = mean + covariance * next_pull_views[key][0:1]
            gains.append(covariance * next_damp_views[key][0:1])
        return gains, mean

    gains, mean = finish(sums, next_means[0])
    out_mean_ref[FIELDS] = mean
    for r in range(ROWS):
        at = slice(8 * r, 8 * r + 8)
        block = moved_ref[0, at, :]
        for n in range(9):
            block = block - gains[n] * second_ref[n, at, :]
        out_ref[FIELDS, at, :] = block

    def send(v, count):
        return pltpu.make_async_copy(
            out_ref.at[pl.ds(v, count)], post_anom_hbm.at[pl.ds(v, count)], sem_ref.at[0]
        )

    def pair(g, carry):
        comps = [2 * g, 2 * g + 1]
        sums = [[zero] * 3, [zero] * 3]
        for r in range(ROWS):
            at = slice(8 * r, 8 * r + 8)
            shifted = [edge_ref[n, at, :] for n in range(3)]
            for i, v in enumerate(comps):
                block = anom_ref[v, at, :]
                sums[i] = [s + block * w for s, w in zip(sums[i], shifted)]
        means, gains = [], []
        for i, v in enumerate(comps):
            mean = mean_ref[pl.ds(v, 1), :]
            own = []
            for key, covariance in completed(v, sums[i]).items():
                mean = mean + covariance * pull_views[key][0][0:1]
                own.append(covariance * damp_views[key][0][0:1])
            means.append(mean)
            gains.append(own)
        sums = [[zero] * 9, [zero] * 9]
        for r in range(ROWS):
            at = slice(8 * r, 8 * r + 8)
            shifted = [first_ref[0, n, at, :] for n in range(9)]
            later = [second_ref[n, at, :] for n in range(9)]
            for i, v in enumerate(comps):
                block = anom_ref[v, at, :]
                for n in range(9):
                    block = block - gains[i][n] * shifted[n]
                out_ref[v, at, :] = block
                sums[i] = [s + block * w for s, w in zip(sums[i], later)]
        for i, v in enumerate(comps):
            gains[i], mean = finish(sums[i], means[i])
            out_mean_ref[v] = mean
        for r in range(ROWS):
            at = slice(8 * r, 8 * r + 8)
            later = [second_ref[n, at, :] for n in range(9)]
            for i, v in enumerate(comps):
                block = out_ref[v, at, :]
                for n in range(9):
                    block = block - gains[i][n] * later[n]
                out_ref[v, at, :] = block
        send(2 * g, 2).start()
        return carry

    send(FIELDS, 1).start()
    lax.fori_loop(0, FIELDS // 2, pair, 0)
    last = pltpu.make_async_copy(out_mean_ref, post_mean_hbm, sem_ref.at[1])
    last.start()
    pltpu.make_async_copy(out_ref, post_anom_hbm, sem_ref.at[0]).wait()
    last.wait()


VMEM = pl.BlockSpec(memory_space=pltpu.VMEM)
SMEM = pl.BlockSpec(memory_space=pltpu.SMEM)
ANY = pl.BlockSpec(memory_space=pl.ANY)
LIMIT = pltpu.CompilerParams(vmem_limit_bytes=8 << 20)


def flat(*shape):
    return jax.ShapeDtypeStruct(shape, f32)


def local(
    atm_members,
    ocean_members,
    remap_weights,
    pair_src,
    obs_cell,
    obs_value,
    obs_error,
    obs_live,
    obs_order,
):
    at_x = lax.axis_index("gx")
    at_y = lax.axis_index("gy")
    rows = lax.axis_size("gy")
    own = ocean_members[0, 0]
    column = [own] + [exchange(own, "gy", first) for first in (0, 1)]
    tiles = list(column)
    for first in (0, 1):
        tiles += [exchange(tile, "gx", first) for tile in column]
    source = pair_src[0, 0]

    def slot(step, at):
        return jnp.where(step == 0, 0, jnp.where((step == 1) == (at % 2 == 0), 1, 2))

    select = slot(source // rows - at_x, at_x) * 3 + slot(source % rows - at_y, at_y)
    listed = select[None, :] == jnp.arange(9, dtype=jnp.int32)[:, None]
    slots = jnp.max(jnp.where(listed, jnp.arange(K, dtype=jnp.int32)[None, :], -1), axis=1)
    weights = remap_weights[0, 0]
    meta = pl.pallas_call(
        records_kernel,
        in_specs=[ANY] + [VMEM] * 6,
        out_specs=VMEM,
        out_shape=flat(8, CELLS),
        name="records",
        compiler_params=LIMIT,
    )(column[2], weights, obs_order[0], obs_cell[0], obs_live[0], obs_value[0], obs_error[0])
    state, near_message, far_message = pl.pallas_call(
        remap_kernel,
        in_specs=[SMEM, VMEM, VMEM] + [VMEM] * 9,
        out_specs=[VMEM] * 3,
        out_shape=[flat(MEM, CELLS), flat(24, CELLS), flat(24, CELLS)],
        name="remap",
        compiler_params=LIMIT,
    )(slots, meta, weights, *tiles)
    near_y = exchange(near_message, "gy", 0)
    far_y = exchange(far_message, "gy", 1)
    anomaly, mean = pl.pallas_call(
        fields_kernel,
        in_specs=[ANY, VMEM],
        out_specs=[VMEM, VMEM],
        out_shape=[flat(FIELDS, MEM, CELLS), flat(16, CELLS)],
        name="fields",
        compiler_params=LIMIT,
    )(state, jnp.transpose(atm_members[0, 0], (1, 0, 2)))
    beside, near_out, far_out = pl.pallas_call(
        side_kernel,
        in_specs=[VMEM] * 4,
        out_specs=[VMEM] * 3,
        out_shape=[flat(MEM, CELLS), flat(HALF + 8, CELLS), flat(HALF + 8, CELLS)],
        name="side",
        compiler_params=LIMIT,
    )(meta, state, near_y, far_y)
    near_x = exchange(near_out, "gx", 0)
    far_x = exchange(far_out, "gx", 1)
    field, turned, rows, partial = pl.pallas_call(
        window_kernel,
        in_specs=[VMEM] * 6,
        out_specs=[VMEM] * 4,
        out_shape=[
            flat(2, MEM, CELLS),
            flat(2, 2, MEM, CELLS),
            flat(8, CELLS),
            flat(COMP, 16, CELLS),
        ],
        scratch_shapes=[pltpu.VMEM((9, MEM, CELLS), f32)],
        name="window",
        compiler_params=LIMIT,
    )(meta, state, beside, near_y, far_y, anomaly)
    post_mean, post_anom = pl.pallas_call(
        analysis_kernel,
        in_specs=[VMEM] * 11,
        out_specs=[ANY, ANY],
        out_shape=[flat(COMP, 1, CELLS), flat(COMP, MEM, CELLS)],
        scratch_shapes=[
            pltpu.VMEM((2, MEM, CELLS), f32),
            pltpu.VMEM((4, MEM, CELLS), f32),
            pltpu.VMEM((4, 9, MEM, CELLS), f32),
            pltpu.VMEM((3, MEM, CELLS), f32),
            pltpu.VMEM((9, MEM, CELLS), f32),
            pltpu.VMEM((COMP, MEM, CELLS), f32),
            pltpu.VMEM((COMP, 1, CELLS), f32),
            pltpu.SemaphoreType.DMA((2,)),
        ],
        name="analysis",
        compiler_params=LIMIT,
    )(meta, near_y, far_y, near_x, far_x, field, turned, rows, partial, mean, anomaly)
    post_mean = jnp.transpose(post_mean, (1, 0, 2))
    post_anom = jnp.transpose(post_anom, (1, 0, 2))
    return post_mean[None], post_anom[None, None]


def solution(mesh):
    in_specs = (
        P("gx", "gy", None, None, None),
        P("gx", "gy", None, None),
        P("gx", "gy", None, None, None),
        P("gx", "gy", None),
        P("gx", "gy", None),
        P("gx", "gy", None),
        P("gx", "gy", None),
        P("gx", "gy", None),
        P("gx", "gy", None),
    )
    out_specs = (P("gx", "gy", None, None), P("gx", "gy", None, None, None))
    return jax.shard_map(local, mesh=mesh, in_specs=in_specs, out_specs=out_specs, check_vma=False)
```

time: 36.2 us -> 32.4 us (0.90)
  waiting for transfers between devices: 8.68 us -> 4.08 us
  starting transfers between devices: 15.2 us -> 18.1 us
  Pallas kernels: 8.47 us -> 7.14 us
  local copies, waits for them, and re-layouts: 2.96 us -> 1.92 us
    ppermute x12, waiting for transfers between devices: 8.68 us -> 4.08 us  [exchange(): return lax.ppermute(block, ('gx', 'gy'), pairs)]
    ppermute x12, starting transfers between devices: 15.2 us -> 18.1 us  [exchange(): return lax.ppermute(block, ('gx', 'gy'), pairs)]
    pallas_call x3 -> x5, Pallas kernels: 6.88 us -> 5.69 us  [the longest x1 4.41 us: local(): pl.pallas_call(analysis_kernel, in_specs=[VMEM] * 11, out_specs=[ANY, ANY...]
    unnamed x18, local copies, waits for them, and re-layouts: 2.96 us -> 1.92 us
  transfers between devices with their start and end apart: 12 -> 12, of which waited for: 5 -> 4; matrix products, arithmetic and copies ran while one was open for 0% -> 0% of each run, Pallas kernels for 2% -> 3%
where the time goes in v4:
time: 32.4 us; the launch traced here: 32.1 us
  starting transfers between devices  18.1 us (56%)
  Pallas kernels  7.14 us (22%)
  waiting for transfers between devices  4.08 us (13%)
  local copies, waits for them, and re-layouts  1.92 us (6%)
  between operations  0.77 us (2%)
    ppermute x12, starting transfers between devices, exchange(): return lax.ppermute(block, ('gx', 'gy'), pairs)  18.1 us
    pallas_call x1, Pallas kernels, local(): pl.pallas_call(analysis_kernel, in_specs=[VMEM] * 11, out_specs=[ANY, ANY...  4.41 us
    ppermute x12, waiting for transfers between devices, exchange(): return lax.ppermute(block, ('gx', 'gy'), pairs)  4.08 us
    unnamed x18, local copies, waits for them, and re-layouts  1.92 us
    pallas_call x1, Pallas kernels, local(): pl.pallas_call(remap_kernel, in_specs=[SMEM, VMEM, VMEM] + [VMEM] * 9, ou...  1.44 us
    pallas_call x1, Pallas kernels, local(): pl.pallas_call(window_kernel, in_specs=[VMEM] * 6, out_specs=[VMEM] * 4,...  0.88 us
  transfers between devices with their start and end apart: 12, of which 4 were waited for; matrix products, arithmetic and copies ran while one was open for 0% of the time, Pallas kernels for 3%

profile of v4, /device:TPU:7, one launch (start us, length us, event | category | flops | bytes accessed | tf_op | source)
XLA Modules:
  0.0 32.1 jit_solution(17870735215846645840)
XLA Ops:
  0.6 1.4 %collective-permute-start.1 = (bf16[80,1024]{1,0:T(8,128)(2,1)}, bf16[80,1024]{1,0:T(8,128)(2,1)S(1)}, u32[]{:S(2)}, u32[]{:S(2)}) collective-permute-start(bf16[80,1024]{1,0:T(8,128)(2,1)} %bitcast.32), channel_id=1, source_target_pairs={{0,1},{1,0},{2,3},{3,2},{4,5},{5,4},{6,7},{7,6},{8,9},{9,8},{10,11... | collective-permute-start | bytes 491528 | tf_op jit(solution)/shard_map/ppermute | solution.py:38
  2.0 2.2 %collective-permute-start = (bf16[80,1024]{1,0:T(8,128)(2,1)}, bf16[80,1024]{1,0:T(8,128)(2,1)S(1)}, u32[]{:S(2)}, u32[]{:S(2)}) collective-permute-start(bf16[80,1024]{1,0:T(8,128)(2,1)} %bitcast.33), channel_id=1, source_target_pairs={{0,16},{1,2},{2,1},{3,4},{4,3},{5,6},{6,5},{7,8},{8,7},{9,10},{10,... | collective-permute-start | bytes 491528 | tf_op jit(solution)/shard_map/ppermute | solution.py:38
  4.2 2.8 %collective-permute-start.5 = (bf16[80,1024]{1,0:T(8,128)(2,1)}, bf16[80,1024]{1,0:T(8,128)(2,1)S(1)}, u32[]{:S(2)}, u32[]{:S(2)}) collective-permute-start(bf16[80,1024]{1,0:T(8,128)(2,1)} %bitcast.34), channel_id=1, source_target_pairs={{0,1},{1,0},{2,3},{3,2},{4,5},{5,4},{6,7},{7,6},{8,9},{9,8},{10,11... | collective-permute-start | bytes 491528 | tf_op jit(solution)/shard_map/ppermute | solution.py:38
  6.9 0.0 collective-permute-start.2
  6.9 0.0 copy-start.8
  6.9 0.0 collective-permute-done.1.refs_1_
  6.9 2.1 %collective-permute-start.6 = (bf16[80,1024]{1,0:T(8,128)(2,1)S(1)}, bf16[80,1024]{1,0:T(8,128)(2,1)S(1)}, u32[]{:S(2)}, u32[]{:S(2)}) collective-permute-start(bf16[80,1024]{1,0:T(8,128)(2,1)S(1)} %collective-permute-done.1.refs_1_), channel_id=1, source_target_pairs={{0,1},{1,0},{2,3},{3,2},{4,5},{5,4},{6,7},{7,6},{8,9},{9,8},{10,11... | collective-permute-start | bytes 491528 | tf_op jit(solution)/shard_map/ppermute | solution.py:38
  9.1 0.1 collective-permute-start.3
  9.1 0.0 collective-permute-done.first_hbm.refs_2_
  9.1 3.3 %collective-permute-start.7 = (bf16[80,1024]{1,0:T(8,128)(2,1)S(1)}, bf16[80,1024]{1,0:T(8,128)(2,1)S(1)}, u32[]{:S(2)}, u32[]{:S(2)}) collective-permute-start(bf16[80,1024]{1,0:T(8,128)(2,1)S(1)} %collective-permute-done.first_hbm.refs_2_), channel_id=1, source_target_pairs={{0,1},{1,0},{2,3},{3,2},{4,5},{5,4},{6,7},{7,6},{8,9},{9,8},{10,11... | collective-permute-start | bytes 491528 | tf_op jit(solution)/shard_map/ppermute | solution.py:38
  12.5 0.0 collective-permute-done.5.refs_6_
  12.5 0.0 collective-permute-start.4
  12.5 0.0 copy-done.8
  12.5 0.1 select_reduce_fusion.slot_ref
  12.6 0.0 copy-start.6
  12.6 0.0 copy-start.7
  12.6 0.0 copy-start.3
  12.6 0.0 copy-start.4
  12.6 0.0 copy-start.5
  12.6 0.6 %copy-done.6 = f32[1,1,64]{2,1,0:T(1,128)S(1)} copy-done((f32[1,1,64]{2,1,0:T(1,128)S(1)}, f32[1,1,64]{2,1,0:T(1,128)}, u32[]{:S(2)}) %copy-start.6) | copy-done | bytes 280
  13.2 0.0 copy-done.7
  13.3 0.0 copy-done.3
  13.3 0.0 copy-done.4
  13.3 0.0 copy-done.5
  13.3 0.0 copy-start
  13.3 1.2 %copy-done = bf16[1,1,4,1024,128]{4,3,2,1,0:T(8,128)(2,1)S(1)} copy-done((bf16[1,1,4,1024,128]{4,3,2,1,0:T(8,128)(2,1)S(1)}, bf16[1,1,4,1024,128]{4,3,2,1,0:T(8,128)(2,1)}, u32[]{:S(2)}) %copy-start) | copy-done | bytes 1048600
  14.5 0.0 copy-start.2
  14.5 0.2 records.1.meta_ref
  14.7 0.0 copy-start.1
  14.7 0.0 collective-permute-done.2.refs_3_
  14.7 0.0 collective-permute-done.6.refs_7_
  14.8 0.0 collective-permute-done.3.refs_4_
  14.8 1.0 %collective-permute-done.7.refs_8_ = bf16[80,1024]{1,0:T(8,128)(2,1)S(1)} collective-permute-done((bf16[80,1024]{1,0:T(8,128)(2,1)S(1)}, bf16[80,1024]{1,0:T(8,128)(2,1)S(1)}, u32[]{:S(2)}, u32[]{:S(2)}) %collective-permute-start.7) | collective-permute-done | bytes 163872 | tf_op jit(solution)/shard_map/ppermute | solution.py:38
  15.8 0.0 collective-permute-done.4.refs_5_
  15.8 0.0 copy-done.2
  15.8 1.4 %remap.1 = (f32[80,128]{1,0:T(8,128)S(1)}, f32[24,128]{1,0:T(8,128)S(1)}, f32[24,128]{1,0:T(8,128)S(1)}) custom-call(s32[9]{0:T(128)S(1)} %select_reduce_fusion.slot_ref, f32[8,128]{1,0:T(8,128)S(1)} %records.1.meta_ref, bf16[4,1024,128]{2,1,0:T(8,128)(2,1)S(1)} %bitcast.30, bf16[80,1024]{1,0:T(8,128)(2,1)S(1)} %bitcast.36, ...), custom_call_target="tpu_custom_call" | custom-call | tf_op jit(solution)/shard_map/remap/pallas_call | solution.py:574
  17.2 0.1 collective-permute-start.8
  17.3 2.2 %collective-permute-start.9 = (f32[24,128]{1,0:T(8,128)S(1)}, f32[24,128]{1,0:T(8,128)S(1)}, u32[]{:S(2)}, u32[]{:S(2)}) collective-permute-start(f32[24,128]{1,0:T(8,128)S(1)} %get-tuple-element.17), channel_id=1, source_target_pairs={{0,16},{1,2},{2,1},{3,4},{4,3},{5,6},{6,5},{7,8},{8,7},{9,10},{10,... | collective-permute-start | bytes 36872 | tf_op jit(solution)/shard_map/ppermute | solution.py:38
  19.5 0.3 collective-permute-done.8.near_ref.near_y_ref
  19.8 2.2 %collective-permute-done.9.far_ref.far_y_ref = f32[24,128]{1,0:T(8,128)S(1)} collective-permute-done((f32[24,128]{1,0:T(8,128)S(1)}, f32[24,128]{1,0:T(8,128)S(1)}, u32[]{:S(2)}, u32[]{:S(2)}) %collective-permute-start.9) | collective-permute-done | bytes 12320 | tf_op jit(solution)/shard_map/ppermute | solution.py:38
  22.0 0.2 side.1
  22.2 1.8 %collective-permute-start.10 = (f32[48,128]{1,0:T(8,128)S(1)}, f32[48,128]{1,0:T(8,128)S(1)}, u32[]{:S(2)}, u32[]{:S(2)}) collective-permute-start(f32[48,128]{1,0:T(8,128)S(1)} %get-tuple-element.19), channel_id=1, source_target_pairs={{0,16},{1,17},{2,18},{3,19},{4,20},{5,21},{6,22},{7,23},{8,24},{9,... | collective-permute-start | bytes 73736 | tf_op jit(solution)/shard_map/ppermute | solution.py:38
  24.1 2.1 %collective-permute-start.11 = (f32[48,128]{1,0:T(8,128)S(1)}, f32[48,128]{1,0:T(8,128)S(1)}, u32[]{:S(2)}, u32[]{:S(2)}) collective-permute-start(f32[48,128]{1,0:T(8,128)S(1)} %get-tuple-element.20), channel_id=1, source_target_pairs={{0,1},{1,0},{2,3},{3,2},{4,5},{5,4},{6,7},{7,6},{8,9},{9,8},{10,11... | collective-permute-start | bytes 73736 | tf_op jit(solution)/shard_map/ppermute | solution.py:38
  26.2 0.0 copy-done.1
  26.2 0.1 fields.1
  26.2 0.9 %window.1 = (f32[2,80,128]{2,1,0:T(8,128)S(1)}, f32[2,2,80,128]{3,2,1,0:T(8,128)S(1)}, f32[8,128]{1,0:T(8,128)S(1)}, f32[13,16,128]{2,1,0:T(8,128)S(1)}) custom-call(f32[8,128]{1,0:T(8,128)S(1)} %records.1.meta_ref, f32[80,128]{1,0:T(8,128)S(1)} %get-tuple-element.18.state_ref.state_hbm, f32[80,128]{1,0:T(8,128)S(1)} %get-tuple-element.21.column_ref, ...), custom_call_target="tpu_custom_call" | custom-call | tf_op jit(solution)/shard_map/window/pallas_call | solution.py:602
  27.1 0.0 collective-permute-done.10.near_x_ref
  27.1 0.5 %collective-permute-done.11.far_x_ref = f32[48,128]{1,0:T(8,128)S(1)} collective-permute-done((f32[48,128]{1,0:T(8,128)S(1)}, f32[48,128]{1,0:T(8,128)S(1)}, u32[]{:S(2)}, u32[]{:S(2)}) %collective-permute-start.11) | collective-permute-done | bytes 24608 | tf_op jit(solution)/shard_map/ppermute | solution.py:38
  27.7 4.4 %analysis.1 = (f32[13,1,128]{2,1,0:T(1,128)}, f32[13,80,128]{2,1,0:T(8,128)}) custom-call(f32[8,128]{1,0:T(8,128)S(1)} %records.1.meta_ref, f32[24,128]{1,0:T(8,128)S(1)} %collective-permute-done.8.near_ref.near_y_ref, f32[24,128]{1,0:T(8,128)S(1)} %collective-permute-done.9.far_ref.far_y_ref, f32[48,128]{1,0:T(8,128)S(1)} %collective-permute-done.10.near_x_ref, ...), custom_call_target="tpu_custom_call" | custom-call | tf_op jit(solution)/shard_map/analysis/pallas_call | solution.py:616
  (1 shorter events, 0.0 us)
Async XLA Ops:
  0.6 6.3 %collective-permute-start.1 = (bf16[80,1024]{1,0:T(8,128)(2,1)}, bf16[80,1024]{1,0:T(8,128)(2,1)S(1)}, u32[]{:S(2)}, u32[]{:S(2)}) collective-permute-start(bf16[80,1024]{1,0:T(8,128)(2,1)} %bitcast.32), channel_id=1, source_target_pairs={{0,1},{1,0},{2,3},{3,2},{4,5},{5,4},{6,7},{7,6},{8,9},{9,8},{10,11... | collective-permute-start | bytes 491528 | tf_op jit(solution)/shard_map/ppermute | solution.py:38
  2.0 7.1 %collective-permute-start = (bf16[80,1024]{1,0:T(8,128)(2,1)}, bf16[80,1024]{1,0:T(8,128)(2,1)S(1)}, u32[]{:S(2)}, u32[]{:S(2)}) collective-permute-start(bf16[80,1024]{1,0:T(8,128)(2,1)} %bitcast.33), channel_id=1, source_target_pairs={{0,16},{1,2},{2,1},{3,4},{4,3},{5,6},{6,5},{7,8},{8,7},{9,10},{10,... | collective-permute-start | bytes 491528 | tf_op jit(solution)/shard_map/ppermute | solution.py:38
  4.2 8.3 %collective-permute-start.5 = (bf16[80,1024]{1,0:T(8,128)(2,1)}, bf16[80,1024]{1,0:T(8,128)(2,1)S(1)}, u32[]{:S(2)}, u32[]{:S(2)}) collective-permute-start(bf16[80,1024]{1,0:T(8,128)(2,1)} %bitcast.34), channel_id=1, source_target_pairs={{0,1},{1,0},{2,3},{3,2},{4,5},{5,4},{6,7},{7,6},{8,9},{9,8},{10,11... | collective-permute-start | bytes 491528 | tf_op jit(solution)/shard_map/ppermute | solution.py:38
  6.9 7.8 %collective-permute-start.2 = (bf16[80,1024]{1,0:T(8,128)(2,1)}, bf16[80,1024]{1,0:T(8,128)(2,1)S(1)}, u32[]{:S(2)}, u32[]{:S(2)}) collective-permute-start(bf16[80,1024]{1,0:T(8,128)(2,1)} %bitcast.35), channel_id=1, source_target_pairs={{0,16},{1,17},{2,18},{3,19},{4,20},{5,21},{6,22},{7,23},{8,24},{9,... | collective-permute-start | bytes 491528 | tf_op jit(solution)/shard_map/ppermute | solution.py:38
  6.9 5.5 %copy-start.8 = (s32[1,1,4]{2,1,0:T(1,128)S(1)}, s32[1,1,4]{2,1,0:T(1,128)}, u32[]{:S(2)}) copy-start(s32[1,1,4]{2,1,0:T(1,128)} %param.12) | copy-start | bytes 52
  6.9 7.8 %collective-permute-start.6 = (bf16[80,1024]{1,0:T(8,128)(2,1)S(1)}, bf16[80,1024]{1,0:T(8,128)(2,1)S(1)}, u32[]{:S(2)}, u32[]{:S(2)}) collective-permute-start(bf16[80,1024]{1,0:T(8,128)(2,1)S(1)} %collective-permute-done.1.refs_1_), channel_id=1, source_target_pairs={{0,1},{1,0},{2,3},{3,2},{4,5},{5,4},{6,7},{7,6},{8,9},{9,8},{10,11... | collective-permute-start | bytes 491528 | tf_op jit(solution)/shard_map/ppermute | solution.py:38
  9.1 5.7 %collective-permute-start.3 = (bf16[80,1024]{1,0:T(8,128)(2,1)S(1)}, bf16[80,1024]{1,0:T(8,128)(2,1)S(1)}, u32[]{:S(2)}, u32[]{:S(2)}) collective-permute-start(bf16[80,1024]{1,0:T(8,128)(2,1)S(1)} %collective-permute-done.1.refs_1_), channel_id=1, source_target_pairs={{0,16},{1,17},{2,18},{3,19},{4,20},{5,21},{6,22},{7,23},{8,24},{9,... | collective-permute-start | bytes 491528 | tf_op jit(solution)/shard_map/ppermute | solution.py:38
  9.1 6.6 %collective-permute-start.7 = (bf16[80,1024]{1,0:T(8,128)(2,1)S(1)}, bf16[80,1024]{1,0:T(8,128)(2,1)S(1)}, u32[]{:S(2)}, u32[]{:S(2)}) collective-permute-start(bf16[80,1024]{1,0:T(8,128)(2,1)S(1)} %collective-permute-done.first_hbm.refs_2_), channel_id=1, source_target_pairs={{0,1},{1,0},{2,3},{3,2},{4,5},{5,4},{6,7},{7,6},{8,9},{9,8},{10,11... | collective-permute-start | bytes 491528 | tf_op jit(solution)/shard_map/ppermute | solution.py:38
  12.5 3.3 %collective-permute-start.4 = (bf16[80,1024]{1,0:T(8,128)(2,1)S(1)}, bf16[80,1024]{1,0:T(8,128)(2,1)S(1)}, u32[]{:S(2)}, u32[]{:S(2)}) collective-permute-start(bf16[80,1024]{1,0:T(8,128)(2,1)S(1)} %collective-permute-done.first_hbm.refs_2_), channel_id=1, source_target_pairs={{0,16},{1,17},{2,18},{3,19},{4,20},{5,21},{6,22},{7,23},{8,24},{9,... | collective-permute-start | bytes 491528 | tf_op jit(solution)/shard_map/ppermute | solution.py:38
  12.6 0.7 %copy-start.6 = (f32[1,1,64]{2,1,0:T(1,128)S(1)}, f32[1,1,64]{2,1,0:T(1,128)}, u32[]{:S(2)}) copy-start(f32[1,1,64]{2,1,0:T(1,128)} %param.14) | copy-start | bytes 772
  12.6 0.7 %copy-start.7 = (f32[1,1,64]{2,1,0:T(1,128)S(1)}, f32[1,1,64]{2,1,0:T(1,128)}, u32[]{:S(2)}) copy-start(f32[1,1,64]{2,1,0:T(1,128)} %param.15) | copy-start | bytes 772
  12.6 0.7 %copy-start.3 = (s32[1,1,64]{2,1,0:T(1,128)S(1)}, s32[1,1,64]{2,1,0:T(1,128)}, u32[]{:S(2)}) copy-start(s32[1,1,64]{2,1,0:T(1,128)} %param.17) | copy-start | bytes 772
  12.6 0.7 %copy-start.4 = (s32[1,1,64]{2,1,0:T(1,128)S(1)}, s32[1,1,64]{2,1,0:T(1,128)}, u32[]{:S(2)}) copy-start(s32[1,1,64]{2,1,0:T(1,128)} %param.13) | copy-start | bytes 772
  12.6 0.7 %copy-start.5 = (s32[1,1,64]{2,1,0:T(1,128)S(1)}, s32[1,1,64]{2,1,0:T(1,128)}, u32[]{:S(2)}) copy-start(s32[1,1,64]{2,1,0:T(1,128)} %param.16) | copy-start | bytes 772
  13.3 1.2 %copy-start = (bf16[1,1,4,1024,128]{4,3,2,1,0:T(8,128)(2,1)S(1)}, bf16[1,1,4,1024,128]{4,3,2,1,0:T(8,128)(2,1)}, u32[]{:S(2)}) copy-start(bf16[1,1,4,1024,128]{4,3,2,1,0:T(8,128)(2,1)} %param.11) | copy-start | bytes 3145732
  14.5 1.2 %copy-start.2 = (bf16[1,1,80,1024]{3,2,1,0:T(8,128)(2,1)S(1)}, bf16[1,1,80,1024]{3,2,1,0:T(8,128)(2,1)}, u32[]{:S(2)}) copy-start(bf16[1,1,80,1024]{3,2,1,0:T(8,128)(2,1)} %param.10) | copy-start | bytes 491524
  14.7 11.5 %copy-start.1 = (f32[1,1,80,12,128]{4,2,3,1,0:T(8,128)S(1)}, f32[1,1,80,12,128]{4,2,3,1,0:T(8,128)}, u32[]{:S(2)}) copy-start(f32[1,1,80,12,128]{4,2,3,1,0:T(8,128)} %param.9) | copy-start | bytes 1474564
  17.2 2.6 %collective-permute-start.8 = (f32[24,128]{1,0:T(8,128)S(1)}, f32[24,128]{1,0:T(8,128)S(1)}, u32[]{:S(2)}, u32[]{:S(2)}) collective-permute-start(f32[24,128]{1,0:T(8,128)S(1)} %get-tuple-element.16), channel_id=1, source_target_pairs={{0,1},{1,0},{2,3},{3,2},{4,5},{5,4},{6,7},{7,6},{8,9},{9,8},{10,11... | collective-permute-start | bytes 36872 | tf_op jit(solution)/shard_map/ppermute | solution.py:38
  17.3 4.7 %collective-permute-start.9 = (f32[24,128]{1,0:T(8,128)S(1)}, f32[24,128]{1,0:T(8,128)S(1)}, u32[]{:S(2)}, u32[]{:S(2)}) collective-permute-start(f32[24,128]{1,0:T(8,128)S(1)} %get-tuple-element.17), channel_id=1, source_target_pairs={{0,16},{1,2},{2,1},{3,4},{4,3},{5,6},{6,5},{7,8},{8,7},{9,10},{10,... | collective-permute-start | bytes 36872 | tf_op jit(solution)/shard_map/ppermute | solution.py:38
  22.2 4.9 %collective-permute-start.10 = (f32[48,128]{1,0:T(8,128)S(1)}, f32[48,128]{1,0:T(8,128)S(1)}, u32[]{:S(2)}, u32[]{:S(2)}) collective-permute-start(f32[48,128]{1,0:T(8,128)S(1)} %get-tuple-element.19), channel_id=1, source_target_pairs={{0,16},{1,17},{2,18},{3,19},{4,20},{5,21},{6,22},{7,23},{8,24},{9,... | collective-permute-start | bytes 73736 | tf_op jit(solution)/shard_map/ppermute | solution.py:38
  24.1 3.6 %collective-permute-start.11 = (f32[48,128]{1,0:T(8,128)S(1)}, f32[48,128]{1,0:T(8,128)S(1)}, u32[]{:S(2)}, u32[]{:S(2)}) collective-permute-start(f32[48,128]{1,0:T(8,128)S(1)} %get-tuple-element.20), channel_id=1, source_target_pairs={{0,1},{1,0},{2,3},{3,2},{4,5},{5,4},{6,7},{7,6},{8,9},{9,8},{10,11... | collective-permute-start | bytes 73736 | tf_op jit(solution)/shard_map/ppermute | solution.py:38
